TPU v7x, 256 devices: a whole 4x4x8 slice. The times are simulated.
256 devices in a mesh: ba: 4 (over z_hi, core), gx: 16 (over x, y), gy: 4 (over z_lo).
Axes of the slice: x: 4, y: 4, z: 8 (z_hi: 2, z_lo: 4; z = z_hi * 4 + z_lo), core: 2. Of those that a mesh axis runs over, the one named last changes fastest.
Arguments:
- pixels: bfloat16 [896, 224, 6], P(('ba', 'gx'), 'gy'), parts along dimension 0, may hold values from -6 to 6
- conv_weight: bfloat16 [54, 704], replicated, may hold values from -0.875 to 0.875
- input_gain: float32 [704], replicated, may hold values from 0.5 to 1.5
- key_weight: bfloat16 [704, 1024], replicated, may hold values from -0.21875 to 0.21875
- value_weight: bfloat16 [704, 1024], replicated, may hold values from -0.21875 to 0.21875
- latents: bfloat16 [512, 1024], replicated, may hold values from -6 to 6
- latent_gain: float32 [1024], replicated, may hold values from 0.5 to 1.5
- query_weight: bfloat16 [1024, 1024], replicated, as said below
- out_weight: bfloat16 [1024, 1024], replicated, may hold values from -0.1875 to 0.1875
Outputs:
- new_latents: bfloat16 [2048, 1024], P(('ba', 'gx', 'gy')), parts along dimension 0
There are 4 independent parts, one for each index of `ba`. A program takes and returns all parts, laid end to end along the dimension named above; an argument that names none is the same for every part. Nothing has to cross between parts.
Inputs may be any that keep to these rules, and one draw needn't show every extreme that they name: `query_weight`: independent entries, mean zero, of order 3 * 1024 ** -0.5, and up to 20 times that in the columns of some heads.
All inputs are finite; a program needn't handle non-finite values.
Results may differ from a plain program's by a relative error of at most 0.025.
Values may be sent and summed in bfloat16 or wider, within the bound.
No kernel may reach another device: no remote copies, remote signals or barrier semaphores. Data moves between devices by JAX's collectives and lax.ppermute only.
A program may use at most 64 MiB of HBM per device.

v0:
```python
import jax
import jax.numpy as jnp
from jax import lax
from jax.sharding import PartitionSpec as P

HEADS = 8
DH = 128


def extended(cells, sides, width):
    for axis, dim in sides:
        count = lax.axis_size(axis)
        ends = count - 1
        head = lax.slice_in_dim(cells, 0, width, axis=dim)
        tail = lax.slice_in_dim(cells, cells.shape[dim] - width, cells.shape[dim], axis=dim)
        cells = jnp.concatenate(
            [
                lax.ppermute(tail, axis, [(i, (i + 1) % count) for i in range(ends)]),
                cells,
                lax.ppermute(head, axis, [((i + 1) % count, i) for i in range(ends)]),
            ],
            axis=dim,
        )
    return cells


def sent_to_all(shard, axis):
    copies = jnp.broadcast_to(shard, (lax.axis_size(axis), *shard.shape))
    return lax.all_to_all(copies, axis, split_axis=0, concat_axis=0, tiled=True)


def of_everyone(shard, axis):
    return sent_to_all(shard, axis).max(axis=0)


def split_up(shard, dim, devices):
    shape = shard.shape
    tiles = shard.reshape(*shape[:dim], devices, shape[dim] // devices, *shape[dim + 1 :])
    return jnp.moveaxis(tiles, dim, 0)


def summed_on_arrival(shard, axis, dim):
    devices = lax.axis_size(axis)
    tiles = lax.all_to_all(split_up(shard, dim, devices), axis, 0, 0, tiled=True)
    return jnp.sum(tiles.astype(jnp.float32), axis=0)


def sent_together(arrays, axis, dim, along):
    columns = [a.reshape(*a.shape[:along], -1) for a in arrays]
    both = jnp.concatenate(columns, axis=along)
    result, at, outs = (summed_on_arrival(both, axis, dim), 0, [])
    for a, column in zip(arrays, columns):
        section = result[..., at : at + column.shape[along]]
        outs.append(section.reshape(*section.shape[:along], *a.shape[along:]))
        at += column.shape[along]
    return tuple(outs)


def layer_norm(values, gain):
    mean = jnp.mean(values, axis=-1, keepdims=True)
    centred = values - mean
    variance = jnp.mean(centred * centred, axis=-1, keepdims=True)
    return centred * lax.rsqrt(variance + 1e-05) * gain


def project_latents(rows, latent_gain, query_weight):
    lat_normed = layer_norm(rows.astype(jnp.float32), latent_gain).astype(jnp.bfloat16)
    return jnp.dot(lat_normed, query_weight, preferred_element_type=jnp.float32).astype(
        jnp.bfloat16
    )


def on_device(
    pixels,
    conv_weight,
    input_gain,
    key_weight,
    value_weight,
    latents,
    latent_gain,
    query_weight,
    out_weight,
):
    tile_rows, tile_cols = (pixels.shape[0], pixels.shape[1])
    padded = extended(pixels, (("gx", 0), ("gy", 1)), 1)
    patches = jnp.concatenate(
        [
            padded[row_off : row_off + tile_rows, col_off : col_off + tile_cols, :]
            for row_off in range(3)
            for col_off in range(3)
        ],
        axis=-1,
    )
    patches = patches.reshape(tile_rows * tile_cols, -1)
    features = jnp.dot(patches, conv_weight, preferred_element_type=jnp.float32).astype(
        jnp.bfloat16
    )
    normed = layer_norm(features.astype(jnp.float32), input_gain).astype(jnp.bfloat16)
    key_rows = jnp.dot(normed, key_weight, preferred_element_type=jnp.float32).astype(jnp.bfloat16)
    value_rows = jnp.dot(normed, value_weight, preferred_element_type=jnp.float32).astype(
        jnp.bfloat16
    )
    devices = lax.axis_size(("gx", "gy"))
    share = latents.shape[0] // devices
    first_row = lax.axis_index(("gx", "gy")) * share
    queries = project_latents(latents, latent_gain, query_weight)
    scale = 1.0 / DH**0.5

    def one_head(head):
        start = head * DH
        query_head = lax.dynamic_slice_in_dim(queries, start, DH, 1)
        key_head = lax.dynamic_slice_in_dim(key_rows, start, DH, 1)
        value_head = lax.dynamic_slice_in_dim(value_rows, start, DH, 1)
        scores = jnp.dot(query_head, key_head.T, preferred_element_type=jnp.float32) * scale
        top = jnp.max(scores, axis=-1)
        expo = jnp.exp(scores - top[:, None])
        total = jnp.sum(expo, axis=-1)
        summed = jnp.dot(expo.astype(jnp.bfloat16), value_head, preferred_element_type=jnp.float32)
        return (top, total, summed)

    local_top, local_total, local_summed = lax.map(one_head, jnp.arange(HEADS, dtype=jnp.int32))
    global_top = of_everyone(local_top, ("gx", "gy"))
    factor = jnp.exp(local_top - global_top)
    summed, total = sent_together(
        (
            (local_summed * factor[..., None]).astype(jnp.bfloat16),
            (local_total * factor).astype(jnp.bfloat16),
        ),
        ("gx", "gy"),
        1,
        2,
    )
    attended = summed / total[..., None]
    attended = jnp.transpose(attended, (1, 0, 2)).reshape(share, -1).astype(jnp.bfloat16)
    own_rows = lax.dynamic_slice_in_dim(latents, first_row, share, 0)
    result = own_rows.astype(jnp.float32) + jnp.dot(
        attended, out_weight, preferred_element_type=jnp.float32
    )
    return result.astype(jnp.bfloat16)


def solution(mesh):
    return jax.shard_map(
        on_device,
        mesh=mesh,
        in_specs=(P(("ba", "gx"), "gy", None), P(), P(), P(), P(), P(), P(), P(), P()),
        out_specs=P(("ba", "gx", "gy"), None),
        check_vma=False,
    )
```

profile of v0, /device:TPU:32, one launch (start us, length us, event | category | flops | bytes accessed | tf_op | source)
XLA Modules:
  0.0 175.5 jit_solution(16656130357426580926)
XLA Ops:
  0.9 3.6 %collective-permute-start = (bf16[1,56,6]{1,0,2:T(2,128)(2,1)S(1)}, bf16[1,56,6]{1,0,2:T(2,128)(2,1)S(1)}, u32[]{:S(2)}, u32[]{:S(2)}) collective-permute-start(bf16[1,56,6]{1,0,2:T(2,128)(2,1)S(1)} %get-tuple-element.76), channel_id=1, source_target_pairs={{0,4},{4,8},{8,12},{12,16},{16,20},{20,24},{24,28},{28,32},{32,36}... | collective-permute-start | bytes 2024 | tf_op jit(solution)/shard_map/ppermute | solution.py:18
  7.3 1.6 fusion.20
  9.0 2.3 %convolution_convert_fusion.3 = bf16[512,1024]{1,0:T(8,128)(2,1)} fusion(bf16[1024,1024]{1,0:T(8,128)(2,1)S(1)} %copy-done, bf16[512,1024]{1,0:T(8,128)(2,1)S(1)} %copy-done.1, f32[1024]{0:T(1024)S(1)} %copy-done.10, f32[512]{0:T(512)S(1)} %add_rsqrt_fusion.1, f32[512]{0:T(512)S(1)} %broadcast_multiply_fusion.1), kind=kOutput, calls=%fused_computation.35 | convolution fusion | flops 1076887552 | bytes 4202496 | tf_op jit(solution)/shard_map/dot_general | solution.py:68
  11.4 3.8 %collective-permute-start.2 = (bf16[16,1,6]{1,0,2:T(8,128)(2,1)S(1)}, bf16[16,1,6]{1,0,2:T(8,128)(2,1)S(1)}, u32[]{:S(2)}, u32[]{:S(2)}) collective-permute-start(bf16[16,1,6]{1,0,2:T(8,128)(2,1)S(1)} %get-tuple-element.75), channel_id=1, source_target_pairs={{0,1},{1,2},{2,3},{4,5},{5,6},{6,7},{8,9},{9,10},{10,11},{12,13},{... | collective-permute-start | bytes 584 | tf_op jit(solution)/shard_map/ppermute | solution.py:18
  15.2 2.0 %collective-permute-start.3 = (bf16[16,1,6]{1,0,2:T(8,128)(2,1)S(1)}, bf16[16,1,6]{1,0,2:T(8,128)(2,1)S(1)}, u32[]{:S(2)}, u32[]{:S(2)}) collective-permute-start(bf16[16,1,6]{1,0,2:T(8,128)(2,1)S(1)} %get-tuple-element.74), channel_id=1, source_target_pairs={{1,0},{2,1},{3,2},{5,4},{6,5},{7,6},{9,8},{10,9},{11,10},{13,12},{... | collective-permute-start | bytes 584 | tf_op jit(solution)/shard_map/ppermute | solution.py:20
  17.2 3.7 %collective-permute-done.3 = bf16[16,1,6]{1,0,2:T(8,128)(2,1)S(1)} collective-permute-done((bf16[16,1,6]{1,0,2:T(8,128)(2,1)S(1)}, bf16[16,1,6]{1,0,2:T(8,128)(2,1)S(1)}, u32[]{:S(2)}, u32[]{:S(2)}) %collective-permute-start.3) | collective-permute-done | bytes 224 | tf_op jit(solution)/shard_map/ppermute | solution.py:20
  23.1 2.7 %convolution_convert_fusion = bf16[784,1024]{1,0:T(8,128)(2,1)} fusion(bf16[704,1024]{1,0:T(8,128)(2,1)S(1)} %copy-done.8, bf16[784,704]{1,0:T(8,128)(2,1)S(1)} %get-tuple-element.79, f32[704]{0:T(1024)S(1)} %copy-done.11, f32[784]{0:T(1024)S(1)} %add_rsqrt_fusion, f32[784]{0:T(1024)S(1)} %broadcast_multiply_fusion), kind=kOutput, calls=%fused_computation.32 | convolution fusion | flops 1133927424 | bytes 4160384 | tf_op jit(solution)/shard_map/dot_general | solution.py:100
  25.8 2.7 %convolution_convert_fusion.1 = bf16[784,1024]{1,0:T(8,128)(2,1)} fusion(bf16[704,1024]{1,0:T(8,128)(2,1)S(1)} %copy-done.9, bf16[784,704]{1,0:T(8,128)(2,1)S(1)} %get-tuple-element.79, f32[704]{0:T(1024)S(1)} %copy-done.11, f32[784]{0:T(1024)S(1)} %add_rsqrt_fusion, f32[784]{0:T(1024)S(1)} %broadcast_multiply_fusion), kind=kOutput, calls=%fused_computation.33 | convolution fusion | flops 1133927424 | bytes 4160384 | tf_op jit(solution)/shard_map/dot_general | solution.py:99
  28.4 41.5 %while.14 = (s32[]{:T(128)}, f32[8,512]{1,0:T(8,128)S(1)}, f32[8,512]{1,0:T(8,128)S(1)}, f32[8,512,128]{2,1,0:T(8,128)}, s32[8]{0:T(128)S(1)}, /*index=5*/bf16[5...) while((s32[]{:T(128)}, f32[8,512]{1,0:T(8,128)S(1)}, ...), condition=%wide.region_7.8_spmd, body=%wide.region_4.7_spmd.sunk | while | flops 208731136 | bytes 5629627 | solution.py:121
  31.1 2.1 %fusion.51 = f32[8,512,128]{2,1,0:T(8,128)} fusion(f32[8,512,128]{2,1,0:T(8,128)} %get-tuple-element.148, s32[]{:T(128)} %get-tuple-element.145, f32[512,784]{0,1:T(8,128)S(1)} %get-tuple-element.132, f32[512]{0:T(512)S(1)} %get-tuple-element.131, bf16[784,1024]{1,0:T(8,128)(2,1)} %get-tuple-element.164, s32[]{:T(128)S(6)} %select_n.10), kind=kOutput, calls=%fused_computation.5.clone.1 | convolution fusion | flops 103964672 | bytes 2071044 | tf_op jit(solution)/shard_map/while/body/eval_jaxpr/dot_general | solution.py:118
  36.2 2.1 %fusion.51 = f32[8,512,128]{2,1,0:T(8,128)} fusion(f32[8,512,128]{2,1,0:T(8,128)} %get-tuple-element.148, s32[]{:T(128)} %get-tuple-element.145, f32[512,784]{0,1:T(8,128)S(1)} %get-tuple-element.132, f32[512]{0:T(512)S(1)} %get-tuple-element.131, bf16[784,1024]{1,0:T(8,128)(2,1)} %get-tuple-element.164, s32[]{:T(128)S(6)} %select_n.10), kind=kOutput, calls=%fused_computation.5.clone.1 | convolution fusion | flops 103964672 | bytes 2071044 | tf_op jit(solution)/shard_map/while/body/eval_jaxpr/dot_general | solution.py:118
  41.4 2.1 %fusion.51 = f32[8,512,128]{2,1,0:T(8,128)} fusion(f32[8,512,128]{2,1,0:T(8,128)} %get-tuple-element.148, s32[]{:T(128)} %get-tuple-element.145, f32[512,784]{0,1:T(8,128)S(1)} %get-tuple-element.132, f32[512]{0:T(512)S(1)} %get-tuple-element.131, bf16[784,1024]{1,0:T(8,128)(2,1)} %get-tuple-element.164, s32[]{:T(128)S(6)} %select_n.10), kind=kOutput, calls=%fused_computation.5.clone.1 | convolution fusion | flops 103964672 | bytes 2071044 | tf_op jit(solution)/shard_map/while/body/eval_jaxpr/dot_general | solution.py:118
  46.6 2.1 %fusion.51 = f32[8,512,128]{2,1,0:T(8,128)} fusion(f32[8,512,128]{2,1,0:T(8,128)} %get-tuple-element.148, s32[]{:T(128)} %get-tuple-element.145, f32[512,784]{0,1:T(8,128)S(1)} %get-tuple-element.132, f32[512]{0:T(512)S(1)} %get-tuple-element.131, bf16[784,1024]{1,0:T(8,128)(2,1)} %get-tuple-element.164, s32[]{:T(128)S(6)} %select_n.10), kind=kOutput, calls=%fused_computation.5.clone.1 | convolution fusion | flops 103964672 | bytes 2071044 | tf_op jit(solution)/shard_map/while/body/eval_jaxpr/dot_general | solution.py:118
  51.8 2.1 %fusion.51 = f32[8,512,128]{2,1,0:T(8,128)} fusion(f32[8,512,128]{2,1,0:T(8,128)} %get-tuple-element.148, s32[]{:T(128)} %get-tuple-element.145, f32[512,784]{0,1:T(8,128)S(1)} %get-tuple-element.132, f32[512]{0:T(512)S(1)} %get-tuple-element.131, bf16[784,1024]{1,0:T(8,128)(2,1)} %get-tuple-element.164, s32[]{:T(128)S(6)} %select_n.10), kind=kOutput, calls=%fused_computation.5.clone.1 | convolution fusion | flops 103964672 | bytes 2071044 | tf_op jit(solution)/shard_map/while/body/eval_jaxpr/dot_general | solution.py:118
  57.0 2.1 %fusion.51 = f32[8,512,128]{2,1,0:T(8,128)} fusion(f32[8,512,128]{2,1,0:T(8,128)} %get-tuple-element.148, s32[]{:T(128)} %get-tuple-element.145, f32[512,784]{0,1:T(8,128)S(1)} %get-tuple-element.132, f32[512]{0:T(512)S(1)} %get-tuple-element.131, bf16[784,1024]{1,0:T(8,128)(2,1)} %get-tuple-element.164, s32[]{:T(128)S(6)} %select_n.10), kind=kOutput, calls=%fused_computation.5.clone.1 | convolution fusion | flops 103964672 | bytes 2071044 | tf_op jit(solution)/shard_map/while/body/eval_jaxpr/dot_general | solution.py:118
  62.2 2.1 %fusion.51 = f32[8,512,128]{2,1,0:T(8,128)} fusion(f32[8,512,128]{2,1,0:T(8,128)} %get-tuple-element.148, s32[]{:T(128)} %get-tuple-element.145, f32[512,784]{0,1:T(8,128)S(1)} %get-tuple-element.132, f32[512]{0:T(512)S(1)} %get-tuple-element.131, bf16[784,1024]{1,0:T(8,128)(2,1)} %get-tuple-element.164, s32[]{:T(128)S(6)} %select_n.10), kind=kOutput, calls=%fused_computation.5.clone.1 | convolution fusion | flops 103964672 | bytes 2071044 | tf_op jit(solution)/shard_map/while/body/eval_jaxpr/dot_general | solution.py:118
  67.4 2.1 %fusion.51 = f32[8,512,128]{2,1,0:T(8,128)} fusion(f32[8,512,128]{2,1,0:T(8,128)} %get-tuple-element.148, s32[]{:T(128)} %get-tuple-element.145, f32[512,784]{0,1:T(8,128)S(1)} %get-tuple-element.132, f32[512]{0:T(512)S(1)} %get-tuple-element.131, bf16[784,1024]{1,0:T(8,128)(2,1)} %get-tuple-element.164, s32[]{:T(128)S(6)} %select_n.10), kind=kOutput, calls=%fused_computation.5.clone.1 | convolution fusion | flops 103964672 | bytes 2071044 | tf_op jit(solution)/shard_map/while/body/eval_jaxpr/dot_general | solution.py:118
  70.1 37.9 %all_to_all.10 = f32[64,8,512]{2,1,0:T(8,128)} all-to-all(f32[64,8,512]{2,1,0:T(8,128)S(1)} %broadcast_in_dim.26), channel_id=1, replica_groups=mesh['ba'=4,'gx'=16,'gy'=4] {'gx','gy'}, dimensions={0} | all-to-all | bytes 2097152 | tf_op jit(solution)/shard_map/all_to_all | solution.py:29
  109.3 3.2 %concatenate.40 = bf16[8,64,8,1]{3,2,1,0:T(8,128)(2,1)} reshape(bf16[8,512]{1,0:T(8,128)(2,1)S(1)} %get-tuple-element.68) | data formatting | bytes 16384 | tf_op jit(solution)/shard_map/concatenate | solution.py:50
  112.5 2.0 %fusion.24 = bf16[8,64,8,128]{3,2,1,0:T(8,128)(2,1)S(1)} fusion(f32[8,512,128]{2,1,0:T(8,128)} %get-tuple-element.49, f32[8,512]{1,0:T(8,128)S(1)} %get-tuple-element.69), kind=kLoop, calls=%fused_computation.38 | loop fusion | flops 1048576 | bytes 3162112 | tf_op jit(solution)/shard_map/concatenate | solution.py:50
  115.0 1.6 copy.19
  116.5 6.3 %all-to-all-start.1 = ((bf16[64,8,8,129]{3,2,1,0:T(8,128)(2,1)}), bf16[64,8,8,129]{3,2,1,0:T(8,128)(2,1)}, u32[]{:S(2)}, u32[]{:S(2)}) async-start(bf16[64,8,8,129]{3,2,1,0:T(8,128)(2,1)} %copy.19), calls=%async_computation.1 | async-start | bytes 4194304 | tf_op jit(solution)/shard_map/all_to_all | solution.py:44
  122.8 49.4 %all-to-all-done.1 = bf16[64,8,8,129]{3,2,1,0:T(8,128)(2,1)} async-done(((bf16[64,8,8,129]{3,2,1,0:T(8,128)(2,1)}), bf16[64,8,8,129]{3,2,1,0:T(8,128)(2,1)}, u32[]{:S(2)}, u32[]{:S(2)}) %all-to-all-start.1) | async-done | bytes 1056800 | tf_op jit(solution)/shard_map/all_to_all | solution.py:44
  172.2 2.1 %convert_reduce_fusion = f32[8,8,129]{2,1,0:T(8,128)S(1)} fusion(bf16[64,8,8,129]{3,2,1,0:T(8,128)(2,1)} %all-to-all-done.1), kind=kLoop, calls=%fused_computation.15 | loop fusion | flops 1048512 | bytes 1089792 | tf_op jit(solution)/shard_map/reduce_sum | solution.py:45
  (99 shorter events, 28.0 us)
Async XLA Ops:
  0.0 8.9 %copy-start = (bf16[1024,1024]{1,0:T(8,128)(2,1)S(1)}, bf16[1024,1024]{1,0:T(8,128)(2,1)}, u32[]{:S(2)}) copy-start(bf16[1024,1024]{1,0:T(8,128)(2,1)} %param.18) | copy-start | bytes 6291460
  0.0 8.9 %copy-start.1 = (bf16[512,1024]{1,0:T(8,128)(2,1)S(1)}, bf16[512,1024]{1,0:T(8,128)(2,1)}, u32[]{:S(2)}) copy-start(bf16[512,1024]{1,0:T(8,128)(2,1)} %param.16) | copy-start | bytes 3145732
  0.0 8.9 %copy-start.10 = (f32[1024]{0:T(1024)S(1)}, f32[1024]{0:T(1024)}, u32[]{:S(2)}) copy-start(f32[1024]{0:T(1024)} %param.17) | copy-start | bytes 12292
  0.9 10.4 %collective-permute-start = (bf16[1,56,6]{1,0,2:T(2,128)(2,1)S(1)}, bf16[1,56,6]{1,0,2:T(2,128)(2,1)S(1)}, u32[]{:S(2)}, u32[]{:S(2)}) collective-permute-start(bf16[1,56,6]{1,0,2:T(2,128)(2,1)S(1)} %get-tuple-element.76), channel_id=1, source_target_pairs={{0,4},{4,8},{8,12},{12,16},{16,20},{20,24},{24,28},{28,32},{32,36}... | collective-permute-start | bytes 2024 | tf_op jit(solution)/shard_map/ppermute | solution.py:18
  4.5 6.8 %collective-permute-start.1 = (bf16[1,56,6]{1,0,2:T(2,128)(2,1)S(1)}, bf16[1,56,6]{1,0,2:T(2,128)(2,1)S(1)}, u32[]{:S(2)}, u32[]{:S(2)}) collective-permute-start(bf16[1,56,6]{1,0,2:T(2,128)(2,1)S(1)} %get-tuple-element.77), channel_id=1, source_target_pairs={{4,0},{8,4},{12,8},{16,12},{20,16},{24,20},{28,24},{32,28},{36,32}... | collective-permute-start | bytes 2024 | tf_op jit(solution)/shard_map/ppermute | solution.py:20
  8.9 2.3 %copy-start.4 = (bf16[14,56,6]{1,0,2:T(8,128)(2,1)S(1)}, bf16[14,56,6]{1,0,2:T(8,128)(2,1)}, u32[]{:S(2)}) copy-start(bf16[14,56,6]{1,0,2:T(8,128)(2,1)} %param.11) | copy-start | bytes 28228
  8.9 12.7 %copy-start.5 = (bf16[54,704]{1,0:T(8,128)(2,1)S(1)}, bf16[54,704]{1,0:T(8,128)(2,1)}, u32[]{:S(2)}) copy-start(bf16[54,704]{1,0:T(8,128)(2,1)} %param.12) | copy-start | bytes 228100
  11.4 5.8 %collective-permute-start.2 = (bf16[16,1,6]{1,0,2:T(8,128)(2,1)S(1)}, bf16[16,1,6]{1,0,2:T(8,128)(2,1)S(1)}, u32[]{:S(2)}, u32[]{:S(2)}) collective-permute-start(bf16[16,1,6]{1,0,2:T(8,128)(2,1)S(1)} %get-tuple-element.75), channel_id=1, source_target_pairs={{0,1},{1,2},{2,3},{4,5},{5,6},{6,7},{8,9},{9,10},{10,11},{12,13},{... | collective-permute-start | bytes 584 | tf_op jit(solution)/shard_map/ppermute | solution.py:18
  15.2 5.7 %collective-permute-start.3 = (bf16[16,1,6]{1,0,2:T(8,128)(2,1)S(1)}, bf16[16,1,6]{1,0,2:T(8,128)(2,1)S(1)}, u32[]{:S(2)}, u32[]{:S(2)}) collective-permute-start(bf16[16,1,6]{1,0,2:T(8,128)(2,1)S(1)} %get-tuple-element.74), channel_id=1, source_target_pairs={{1,0},{2,1},{3,2},{5,4},{6,5},{7,6},{9,8},{10,9},{11,10},{13,12},{... | collective-permute-start | bytes 584 | tf_op jit(solution)/shard_map/ppermute | solution.py:20
  21.7 1.4 copy-start.8
  21.7 1.4 copy-start.11
  23.1 2.7 %copy-start.9 = (bf16[704,1024]{1,0:T(8,128)(2,1)S(1)}, bf16[704,1024]{1,0:T(8,128)(2,1)}, u32[]{:S(2)}) copy-start(bf16[704,1024]{1,0:T(8,128)(2,1)} %param.14) | copy-start | bytes 4325380
  25.8 2.7 %copy-start.6 = (f32[8,512]{1,0:T(8,128)S(1)}, f32[8,512]{1,0:T(8,128)}, u32[]{:S(2)}) copy-start(f32[8,512]{1,0:T(8,128)} %custom-call.1) | copy-start | bytes 49156
  25.8 2.7 %copy-start.7 = (f32[8,512]{1,0:T(8,128)S(1)}, f32[8,512]{1,0:T(8,128)}, u32[]{:S(2)}) copy-start(f32[8,512]{1,0:T(8,128)} %custom-call.2) | copy-start | bytes 49156
  112.5 2.0 %copy-start.2 = (bf16[8,64,8,1]{3,2,1,0:T(8,128)(2,1)S(1)}, bf16[8,64,8,1]{3,2,1,0:T(8,128)(2,1)}, u32[]{:S(2)}) copy-start(bf16[8,64,8,1]{3,2,1,0:T(8,128)(2,1)} %concatenate.40) | copy-start | bytes 24580
  116.5 55.7 %all-to-all-start.1 = ((bf16[64,8,8,129]{3,2,1,0:T(8,128)(2,1)}), bf16[64,8,8,129]{3,2,1,0:T(8,128)(2,1)}, u32[]{:S(2)}, u32[]{:S(2)}) async-start(bf16[64,8,8,129]{3,2,1,0:T(8,128)(2,1)} %copy.19), calls=%async_computation.1 | async-start | bytes 4194304 | tf_op jit(solution)/shard_map/all_to_all | solution.py:44
  172.2 2.2 %copy-start.3 = (bf16[1024,1024]{1,0:T(8,128)(2,1)S(1)}, bf16[1024,1024]{1,0:T(8,128)(2,1)}, u32[]{:S(2)}) copy-start(bf16[1024,1024]{1,0:T(8,128)(2,1)} %param.19) | copy-start | bytes 6291460
where the time goes:
time: 177 us; the launch traced here: 175 us
  waiting for transfers between devices  53.1 us (30%)
  blocking collectives  37.9 us (21%)
  matrix products  37.3 us (21%)
  starting transfers between devices  17 us (10%)
  local copies, waits for them, and re-layouts  12.3 us (7%)
  other arithmetic  12.2 us (7%)
  loops' own time  5.5 us (3%)
    all_to_all x1, waiting for transfers between devices, summed_on_arrival(): lax.all_to_all(split_up(shard, dim, devices), axis, 0, 0, tiled=True)  49.4 us
    all_to_all x1, blocking collectives, sent_to_all(): return lax.all_to_all(copies, axis, split_axis=0, concat_axis=0, tiled=True)  37.9 us
    dot_general x8, matrix products, one_head(): jnp.dot(expo.astype(jnp.bfloat16), value_head, preferred_element_type=jnp...  16.9 us
    dot_general x8, matrix products, one_head(): jnp.dot(query_head, key_head.T, preferred_element_type=jnp.float32) * scale  11.1 us
    ppermute x2, starting transfers between devices, extended(): lax.ppermute(tail, axis, [(i, (i + 1) % count) for i in range(ends)])  7.43 us
    all_to_all x1, starting transfers between devices, summed_on_arrival(): lax.all_to_all(split_up(shard, dim, devices), axis, 0, 0, tiled=True)  6.29 us
    another operation x1, loops' own time, on_device(): lax.map(one_head, jnp.arange(HEADS, dtype=jnp.int32))  5.5 us
    dynamic_slice x8, local copies, waits for them, and re-layouts, on_device(): lax.map(one_head, jnp.arange(HEADS, dtype=jnp.int32))  4.69 us
  transfers between devices with their start and end apart: 5, of which 2 were waited for; matrix products, arithmetic and copies ran while one was open for 3% of the time, Pallas kernels for 0%

commit v1 on v0

v1 whole, which is shorter than its diff:
```python
import jax
import jax.numpy as jnp
from jax import lax
from jax.experimental import pallas as pl
from jax.experimental.pallas import tpu as pltpu
from jax.sharding import PartitionSpec as P

HEADS = 8
DH = 128
LANES = 128
SLOT = 64
ONE = 54
MASK = 56
TOP = 57
BIG = 1e30
QUAD = 4
LOG2E = 1.4426950408889634
GROUP = ("gx", "gy")
F32 = jnp.float32
BF16 = jnp.bfloat16


def extended(cells, sides, width):
    for axis, dim in sides:
        count = lax.axis_size(axis)
        ends = count - 1
        head = lax.slice_in_dim(cells, 0, width, axis=dim)
        tail = lax.slice_in_dim(cells, cells.shape[dim] - width, cells.shape[dim], axis=dim)
        cells = jnp.concatenate(
            [
                lax.ppermute(tail, axis, [(i, (i + 1) % count) for i in range(ends)]),
                cells,
                lax.ppermute(head, axis, [((i + 1) % count, i) for i in range(ends)]),
            ],
            axis=dim,
        )
    return cells


def nn(a, b):
    return lax.dot_general(a, b, (((1,), (0,)), ((), ())), preferred_element_type=F32)


def nt(a, b):
    return lax.dot_general(a, b, (((1,), (1,)), ((), ())), preferred_element_type=F32)


def lanes_of(shape):
    return lax.broadcasted_iota(jnp.int32, shape, len(shape) - 1)


def centred_weight(conv_ref):
    weight = conv_ref[...].astype(F32)
    return weight - jnp.mean(weight, axis=-1, keepdims=True)


def split_up(values):
    high = values.astype(BF16)
    return high, (values - high.astype(F32)).astype(BF16)


def through(conv_ref, gain_ref, weight_ref):
    high, low = split_up(centred_weight(conv_ref) * gain_ref[...])
    both = nn(jnp.concatenate([high, low], axis=0), weight_ref[...])
    return both[:SLOT] + both[SLOT:]


def query_kernel(lat_ref, lat_gain_ref, query_ref, conv_ref, gain_ref, key_ref, rows_ref, wide_ref):
    high, low = split_up(centred_weight(conv_ref))
    wide_ref[...] = jnp.concatenate([high, low], axis=0)
    keys = through(conv_ref, gain_ref, key_ref) * (LOG2E / DH**0.5)
    key_high, key_low = split_up(keys)
    values = lat_ref[...].astype(F32)
    centred = values - jnp.mean(values, axis=-1, keepdims=True)
    variance = jnp.mean(centred * centred, axis=-1, keepdims=True)
    normed = (centred * lax.rsqrt(variance + 1e-05) * lat_gain_ref[...]).astype(BF16)
    queries = nn(normed, query_ref[...]).astype(BF16)
    count = values.shape[0]
    lane = lanes_of((count, LANES))
    for head in range(HEADS):
        cut = slice(head * DH, (head + 1) * DH)
        query = jnp.concatenate([queries[:, cut], queries[:, cut]], axis=1)
        key = jnp.concatenate([key_high[:, cut], key_low[:, cut]], axis=1)
        rows = nt(query, jnp.concatenate([key, key], axis=0))
        rows = jnp.where(lane == MASK, -1.0, rows)
        top, rest = split_up(rows)
        rows_ref[head, :, :LANES] = jnp.where(lane < SLOT, top, rest)
        rows_ref[head, :, LANES:] = jnp.where(lane < SLOT, top, jnp.zeros_like(top))


def output_kernel(conv_ref, gain_ref, value_ref, out_ref, both_ref):
    values = through(conv_ref, gain_ref, value_ref)
    for head in range(HEADS):
        cut = slice(head * DH, (head + 1) * DH)
        high, low = split_up(values[:, cut])
        both = nn(jnp.concatenate([high, low], axis=1), jnp.concatenate([out_ref[cut], out_ref[cut]], axis=0))
        both_ref[head * SLOT : (head + 1) * SLOT, :] = both.astype(BF16)


def attend_kernel(block, patch_ref, wide_ref, rows_ref, sums_ref, left_ref, right_ref, expo_ref):
    pixels = patch_ref.shape[0]
    padded = left_ref.shape[0]
    taps = patch_ref.shape[1]
    row = lax.broadcasted_iota(jnp.int32, (taps, LANES), 0)
    lane = lanes_of((taps, LANES))
    copies = jnp.where((lane == row) | (lane == row + SLOT), 1.0, 0.0).astype(BF16)
    patches = nn(patch_ref[...], copies)
    features = nn(patches.astype(BF16), wide_ref[...])
    variance = jnp.mean(features * features, axis=-1, keepdims=True)
    scaled = patches * lax.rsqrt(variance + 1e-05)
    lane = lanes_of((pixels, LANES))
    column = lane % SLOT
    scaled = jnp.where((column == ONE) | (column == ONE + 1), 1.0, scaled)
    high, low = split_up(scaled)
    left_ref[:pixels, :LANES] = high
    left_ref[:pixels, LANES:] = low
    nothing = jnp.zeros((padded - pixels, LANES), F32)
    edge = jnp.where(lanes_of(nothing.shape) == MASK, BIG, nothing).astype(BF16)
    nothing = nothing.astype(BF16)
    left_ref[pixels:, :LANES] = edge
    left_ref[pixels:, LANES:] = nothing
    for part in range(QUAD):
        at = part * padded
        side = part // 2 * LANES
        keep = (lane < SLOT) if part % 2 == 0 else (lane >= SLOT)
        right_ref[at : at + pixels, side : side + LANES] = jnp.where(keep, high, jnp.zeros_like(high))
        right_ref[at : at + pixels, LANES - side : 2 * LANES - side] = jnp.zeros_like(high)
        right_ref[at + pixels : at + padded, :LANES] = nothing
        right_ref[at + pixels : at + padded, LANES:] = nothing

    width = QUAD * SLOT
    wide_lane = lanes_of((block, width))
    wide_column = wide_lane % SLOT

    def step(index, carry):
        at = pl.multiple_of(index * block, block)
        for quad in range(HEADS // QUAD):
            tops = []
            for part in range(QUAD):
                scores = nt(rows_ref[quad * QUAD + part, pl.ds(at, block), :], left_ref[...])
                top = jnp.max(scores, axis=-1, keepdims=True)
                expo = jnp.exp2(scores - top).astype(BF16)
                expo_ref[:, part * padded : (part + 1) * padded] = expo
                tops.append(top)
            sums = nn(expo_ref[...], right_ref[...])
            top = tops[QUAD - 1]
            for part in range(QUAD - 1):
                top = jnp.where(wide_lane < (part + 1) * SLOT, tops[part], top) if part == 0 else jnp.where(
                    (wide_lane >= part * SLOT) & (wide_lane < (part + 1) * SLOT), tops[part], top
                )
            one = top.astype(BF16).astype(F32)
            two = (top - one).astype(BF16).astype(F32)
            three = top - one - two
            sums = jnp.where(wide_column == ONE + 1, sums - sums.astype(BF16).astype(F32), sums)
            sums = jnp.where(wide_column == TOP, one, sums)
            sums = jnp.where(wide_column == TOP + 1, two, sums)
            sums = jnp.where(wide_column == TOP + 2, three, sums)
            sums_ref[pl.ds(at, block), quad * width : (quad + 1) * width] = sums.astype(BF16)
        return carry

    lax.fori_loop(0, sums_ref.shape[0] // block, step, 0)


def combine_kernel(share, parts_ref, both_ref, own_ref, result_ref):
    count = parts_ref.shape[0] // share
    row = lax.broadcasted_iota(jnp.int32, (LANES, LANES), 0)
    lane = lanes_of((LANES, LANES))
    same = row // SLOT == lane // SLOT
    column = row % SLOT
    pick_top = jnp.where(same & (column >= TOP) & (column < TOP + 3), 1.0, 0.0).astype(BF16)
    pick_one = jnp.where(same & (column >= ONE) & (column < ONE + 2), 1.0, 0.0).astype(BF16)
    highs, lows = [], []
    for at in range(0, parts_ref.shape[1], LANES):
        parts = parts_ref[:, at : at + LANES]
        tops = nn(parts, pick_top).reshape(count, share, LANES)
        ones = nn(parts, pick_one).reshape(count, share, LANES)
        factor = jnp.exp2(tops - jnp.max(tops, axis=0, keepdims=True))
        sums = jnp.sum(factor * parts.astype(F32).reshape(count, share, LANES), axis=0)
        total = jnp.sum(factor * ones, axis=0)
        high, low = split_up(sums / total)
        highs.append(high)
        lows.append(low)
    mean = jnp.concatenate([jnp.concatenate(highs, axis=1), jnp.concatenate(lows, axis=1)], axis=0)
    result = nn(mean, both_ref[...])
    result = own_ref[...].astype(F32) + (result[:share] + result[share:])
    result_ref[...] = result.astype(BF16)


def vmem(count):
    return [pl.BlockSpec(memory_space=pltpu.VMEM)] * count


def on_device(
    pixels,
    conv_weight,
    input_gain,
    key_weight,
    value_weight,
    latents,
    latent_gain,
    query_weight,
    out_weight,
):
    tile_rows, tile_cols = (pixels.shape[0], pixels.shape[1])
    count = tile_rows * tile_cols
    padded_count = -(-count // LANES) * LANES
    feat = conv_weight.shape[1]
    lat, width = latents.shape
    conv = jnp.pad(conv_weight, ((0, SLOT - conv_weight.shape[0]), (0, 0)))
    gain = input_gain.reshape(1, feat)

    rows, wide = pl.pallas_call(
        query_kernel,
        out_shape=(
            jax.ShapeDtypeStruct((HEADS, lat, 2 * LANES), BF16),
            jax.ShapeDtypeStruct((2 * SLOT, feat), BF16),
        ),
        in_specs=vmem(6),
        out_specs=tuple(vmem(2)),
        cost_estimate=pl.CostEstimate(flops=2 * lat * width * width * 2, bytes_accessed=4 * width * width, transcendentals=0),
        name="query_rows",
    )(latents, latent_gain.reshape(1, width), query_weight, conv, gain, key_weight)

    padded = extended(pixels, (("gx", 0), ("gy", 1)), 1)
    patches = jnp.concatenate(
        [
            padded[row_off : row_off + tile_rows, col_off : col_off + tile_cols, :]
            for row_off in range(3)
            for col_off in range(3)
        ],
        axis=-1,
    ).reshape(count, -1)

    block = 128
    sums = pl.pallas_call(
        lambda *refs: attend_kernel(block, *refs),
        out_shape=jax.ShapeDtypeStruct((lat, HEADS * SLOT), BF16),
        in_specs=vmem(3),
        out_specs=vmem(1)[0],
        scratch_shapes=[
            pltpu.VMEM((padded_count, 2 * LANES), BF16),
            pltpu.VMEM((QUAD * padded_count, QUAD * SLOT), BF16),
            pltpu.VMEM((block, QUAD * padded_count), BF16),
        ],
        cost_estimate=pl.CostEstimate(flops=4 * lat * HEADS * padded_count * 256, bytes_accessed=4 * width * width, transcendentals=0),
        name="attend",
    )(patches, wide, rows)

    devices = lax.axis_size(GROUP)
    share = lat // devices
    parts = lax.all_to_all(sums.reshape(devices, share, -1), GROUP, 0, 0, tiled=True)
    both = pl.pallas_call(
        output_kernel,
        out_shape=jax.ShapeDtypeStruct((HEADS * SLOT, width), BF16),
        in_specs=vmem(4),
        out_specs=vmem(1)[0],
        cost_estimate=pl.CostEstimate(flops=2 * HEADS * SLOT * width * width, bytes_accessed=4 * width * width, transcendentals=0),
        name="value_output",
    )(conv, gain, value_weight, out_weight)
    own = lax.dynamic_slice_in_dim(latents, lax.axis_index(GROUP) * share, share, 0)
    return pl.pallas_call(
        lambda *refs: combine_kernel(share, *refs),
        out_shape=jax.ShapeDtypeStruct((share, width), BF16),
        in_specs=vmem(3),
        out_specs=vmem(1)[0],
        cost_estimate=pl.CostEstimate(flops=2 * share * width * width, bytes_accessed=2 * width * width, transcendentals=0),
        name="combine",
    )(parts.reshape(lat, -1), both, own)


def solution(mesh):
    return jax.shard_map(
        on_device,
        mesh=mesh,
        in_specs=(P(("ba", "gx"), "gy", None), P(), P(), P(), P(), P(), P(), P(), P()),
        out_specs=P(("ba", "gx", "gy"), None),
        check_vma=False,
    )
```

time: 177 us -> 69 us (0.39)
  waiting for transfers between devices: 53.1 us -> 11.2 us
  blocking collectives: 37.9 us -> 0 us
  matrix products: 37.3 us -> 0 us
  Pallas kernels: 0 us -> 25.2 us
  other arithmetic: 12.2 us -> 0.92 us
  starting transfers between devices: 17 us -> 23.4 us
  loops' own time: 5.5 us -> 0 us
  local copies, waits for them, and re-layouts: 12.3 us -> 7.01 us
    all_to_all x1, waiting for transfers between devices: 49.4 us -> 9.85 us  [on_device(): lax.all_to_all(sums.reshape(devices, share, -1), GROUP, 0, 0, tiled=True)]
    all_to_all x1 -> x0, blocking collectives: 37.9 us -> none  [sent_to_all(): return lax.all_to_all(copies, axis, split_axis=0, concat_axis=0, tiled=True)]
    dot_general x21 -> x0, matrix products: 37.3 us -> none  [the longest x8 16.9 us: one_head(): jnp.dot(expo.astype(jnp.bfloat16), value_head, preferred_element_type=jnp...]
    pallas_call x0 -> x4, Pallas kernels: none -> 25.2 us  [the longest x1 12 us: on_device(): pl.pallas_call(lambda *refs: attend_kernel(block, *refs), out_shape=jax.S...]
    reduce_sum x12 -> x0, other arithmetic: 8.21 us -> none  [the longest x8 2.47 us: one_head(): total = jnp.sum(expo, axis=-1)]
    all_to_all x1, starting transfers between devices: 6.29 us -> 12.9 us  [on_device(): lax.all_to_all(sums.reshape(devices, share, -1), GROUP, 0, 0, tiled=True)]
    another operation x1 -> x0, loops' own time: 5.5 us -> none  [on_device(): lax.map(one_head, jnp.arange(HEADS, dtype=jnp.int32))]
    dynamic_slice x8 -> x1, local copies, waits for them, and re-layouts: 4.69 us -> 1.31 us  [on_device(): lax.dynamic_slice_in_dim(latents, lax.axis_index(GROUP) * share, share, 0)]
  transfers between devices with their start and end apart: 5 -> 5, of which waited for: 2 -> 2; matrix products, arithmetic and copies ran while one was open for 3% -> 6% of each run, Pallas kernels for 0% -> 15%
where the time goes in v1:
time: 69 us; the launch traced here: 68 us
  Pallas kernels  25.2 us (37%)
  starting transfers between devices  23.4 us (34%)
  waiting for transfers between devices  11.2 us (16%)
  local copies, waits for them, and re-layouts  7.01 us (10%)
  other arithmetic  0.92 us (1%)
    all_to_all x1, starting transfers between devices, on_device(): lax.all_to_all(sums.reshape(devices, share, -1), GROUP, 0, 0, tiled=True)  12.9 us
    pallas_call x1, Pallas kernels, on_device(): pl.pallas_call(lambda *refs: attend_kernel(block, *refs), out_shape=jax.S...  12 us
    all_to_all x1, waiting for transfers between devices, on_device(): lax.all_to_all(sums.reshape(devices, share, -1), GROUP, 0, 0, tiled=True)  9.85 us
    ppermute x2, starting transfers between devices, extended(): lax.ppermute(tail, axis, [(i, (i + 1) % count) for i in range(ends)])  7.29 us
    pallas_call x1, Pallas kernels, on_device(): pl.pallas_call(query_kernel, out_shape=(jax.ShapeDtypeStruct((HEADS, lat,...  6.22 us
    pallas_call x1, Pallas kernels, on_device(): pl.pallas_call(output_kernel, out_shape=jax.ShapeDtypeStruct((HEADS * SLO...  4.23 us
    ppermute x2, starting transfers between devices, extended(): lax.ppermute(head, axis, [((i + 1) % count, i) for i in range(ends)])  3.31 us
    pallas_call x1, Pallas kernels, on_device(): pl.pallas_call(lambda *refs: combine_kernel(share, *refs), out_shape=jax....  2.8 us
  transfers between devices with their start and end apart: 5, of which 2 were waited for; matrix products, arithmetic and copies ran while one was open for 6% of the time, Pallas kernels for 15%

profile of v1, /device:TPU:32, one launch (start us, length us, event | category | flops | bytes accessed | tf_op | source)
XLA Modules:
  0.0 68.0 jit_solution(13922552918094403065)
XLA Ops:
  0.0 0.7 %fusion.3 = (bf16[1,56,6]{1,0,2:T(2,128)(2,1)S(1)}, bf16[1,56,6]{1,0,2:T(2,128)(2,1)S(1)}) fusion(bf16[14,56,6]{1,0,2:T(8,128)(2,1)} %param.9), kind=kLoop, calls=%fused_computation.16 | loop fusion | bytes 2688 | tf_op jit(solution)/shard_map/slice | solution.py:28
  0.7 3.5 %collective-permute-start = (bf16[1,56,6]{1,0,2:T(2,128)(2,1)S(1)}, bf16[1,56,6]{1,0,2:T(2,128)(2,1)S(1)}, u32[]{:S(2)}, u32[]{:S(2)}) collective-permute-start(bf16[1,56,6]{1,0,2:T(2,128)(2,1)S(1)} %get-tuple-element.13), channel_id=1, source_target_pairs={{0,4},{4,8},{8,12},{12,16},{16,20},{20,24},{24,28},{28,32},{32,36}... | collective-permute-start | bytes 2024 | tf_op jit(solution)/shard_map/ppermute | solution.py:31
  4.2 1.3 %collective-permute-start.1 = (bf16[1,56,6]{1,0,2:T(2,128)(2,1)S(1)}, bf16[1,56,6]{1,0,2:T(2,128)(2,1)S(1)}, u32[]{:S(2)}, u32[]{:S(2)}) collective-permute-start(bf16[1,56,6]{1,0,2:T(2,128)(2,1)S(1)} %get-tuple-element.14), channel_id=1, source_target_pairs={{4,0},{8,4},{12,8},{16,12},{20,16},{24,20},{28,24},{32,28},{36,32}... | collective-permute-start | bytes 2024 | tf_op jit(solution)/shard_map/ppermute | solution.py:33
  5.5 1.3 %reshape.17.gain_ref = f32[1,704]{1,0:T(1,128)} reshape(f32[704]{0:T(1024)} %param.11) | data formatting | bytes 5632 | tf_op jit(solution)/shard_map/reshape | solution.py:210
  6.8 1.5 %pad.4.conv_ref = bf16[64,704]{1,0:T(8,128)(2,1)} pad(bf16[54,704]{1,0:T(8,128)(2,1)} %param.10, bf16[]{:T(256)} %constant.4.clone.1), padding=0_10x0_0 | pad | bytes 166146 | tf_op jit(solution)/shard_map/jit(_pad)/pad | solution.py:209
  8.3 1.4 %collective-permute-done.1 = bf16[1,56,6]{1,0,2:T(2,128)(2,1)S(1)} collective-permute-done((bf16[1,56,6]{1,0,2:T(2,128)(2,1)S(1)}, bf16[1,56,6]{1,0,2:T(2,128)(2,1)S(1)}, u32[]{:S(2)}, u32[]{:S(2)}) %collective-permute-start.1) | collective-permute-done | bytes 704 | tf_op jit(solution)/shard_map/ppermute | solution.py:33
  9.7 0.8 %pad_maximum_fusion.2 = bf16[16,56,6]{1,0,2:T(8,128)(2,1)S(1)} fusion(bf16[1,56,6]{1,0,2:T(2,128)(2,1)S(1)} %collective-permute-done.1, bf16[14,56,6]{1,0,2:T(8,128)(2,1)} %param.9, bf16[1,56,6]{1,0,2:T(2,128)(2,1)S(1)} %collective-permute-done), kind=kLoop, calls=%fused_computation.10 | loop fusion | flops 32256 | bytes 21504 | tf_op jit(solution)/shard_map/concatenate | solution.py:29
  10.5 0.1 fusion.2
  10.5 3.8 %collective-permute-start.2 = (bf16[16,1,6]{1,0,2:T(8,128)(2,1)S(1)}, bf16[16,1,6]{1,0,2:T(8,128)(2,1)S(1)}, u32[]{:S(2)}, u32[]{:S(2)}) collective-permute-start(bf16[16,1,6]{1,0,2:T(8,128)(2,1)S(1)} %get-tuple-element.12), channel_id=1, source_target_pairs={{0,1},{1,2},{2,3},{4,5},{5,6},{6,7},{8,9},{9,10},{10,11},{12,13},{... | collective-permute-start | bytes 584 | tf_op jit(solution)/shard_map/ppermute | solution.py:31
  14.4 2.0 %collective-permute-start.3 = (bf16[16,1,6]{1,0,2:T(8,128)(2,1)S(1)}, bf16[16,1,6]{1,0,2:T(8,128)(2,1)S(1)}, u32[]{:S(2)}, u32[]{:S(2)}) collective-permute-start(bf16[16,1,6]{1,0,2:T(8,128)(2,1)S(1)} %get-tuple-element.11), channel_id=1, source_target_pairs={{1,0},{2,1},{3,2},{5,4},{6,5},{7,6},{9,8},{10,9},{11,10},{13,12},{... | collective-permute-start | bytes 584 | tf_op jit(solution)/shard_map/ppermute | solution.py:33
  16.4 0.0 copy-start.1
  16.4 6.2 %query_rows.1 = (bf16[8,512,256]{2,1,0:T(8,128)(2,1)}, bf16[128,704]{1,0:T(8,128)(2,1)}) custom-call(bf16[512,1024]{1,0:T(8,128)(2,1)} %lat_ref.1, f32[1,1024]{1,0:T(1,128)} %bitcast.7, bf16[1024,1024]{1,0:T(8,128)(2,1)} %query_ref.1, bf16[64,704]{1,0:T(8,128)(2,1)} %pad.4.conv_ref, f32[1,704]{1,0:T(1,128)} %reshape.17.gain_ref, bf16[704,1024]{1,0:T(8,128)(2,1)} %key_ref.1), custom_call_target="tpu_custom_call" | custom-call | flops 2147483648 | bytes 4194304 | tf_op jit(solution)/shard_map/query_rows/pallas_call | solution.py:212
  22.6 0.1 pad_maximum_fusion.3
  22.8 0.1 slice_dynamic-update-slice_fusion.4
  22.9 0.1 slice_dynamic-update-slice_fusion.2
  23.1 0.1 slice_dynamic-update-slice_fusion
  23.2 0.9 %copy.10 = bf16[14,56,54]{2,1,0:T(8,128)(2,1)} copy(bf16[14,56,54]{1,0,2:T(8,128)(2,1)S(1)} %slice_dynamic-update-slice_fusion) | data formatting | bytes 169344 | tf_op jit(solution)/shard_map/concatenate | solution.py:225
  24.1 12.0 %attend.1 = bf16[512,512]{1,0:T(8,128)(2,1)} custom-call(bf16[784,54]{1,0:T(8,128)(2,1)} %bitcast.6, bf16[128,704]{1,0:T(8,128)(2,1)} %get-tuple-element.7.refs_1_, bf16[8,512,256]{2,1,0:T(8,128)(2,1)} %get-tuple-element.8.refs_2_), custom_call_target="tpu_custom_call" | custom-call | flops 3758096384 | bytes 4194304 | tf_op jit(solution)/shard_map/attend/pallas_call | solution.py:235
  36.1 12.9 %all-to-all-start = ((bf16[64,8,512]{2,1,0:T(8,128)(2,1)}), bf16[64,8,512]{2,1,0:T(8,128)(2,1)S(1)}, u32[]{:S(2)}, u32[]{:S(2)}) async-start(bf16[64,8,512]{2,1,0:T(8,128)(2,1)} %bitcast.5), calls=%async_computation | async-start | bytes 1048576 | tf_op jit(solution)/shard_map/all_to_all | solution.py:251
  49.0 4.2 %value_output.1.refs_1_ = bf16[512,1024]{1,0:T(8,128)(2,1)} custom-call(bf16[64,704]{1,0:T(8,128)(2,1)} %pad.4.conv_ref, f32[1,704]{1,0:T(1,128)} %reshape.17.gain_ref, bf16[704,1024]{1,0:T(8,128)(2,1)} %value_ref.1, bf16[1024,1024]{1,0:T(8,128)(2,1)} %out_ref.1), custom_call_target="tpu_custom_call" | custom-call | flops 1073741824 | bytes 4194304 | tf_op jit(solution)/shard_map/value_output/pallas_call | solution.py:252
  53.2 1.3 %constant_dynamic-slice_fusion.refs_2_ = bf16[8,1024]{1,0:T(8,128)(2,1)} fusion(bf16[512,1024]{1,0:T(8,128)(2,1)} %lat_ref.1, s32[]{:T(128)S(6)} %select_n.3), kind=kLoop, calls=%fused_computation.14 | loop fusion | bytes 32772 | tf_op jit(solution)/shard_map/dynamic_slice | solution.py:260
  54.5 9.8 %all-to-all-done = bf16[64,8,512]{2,1,0:T(8,128)(2,1)S(1)} async-done(((bf16[64,8,512]{2,1,0:T(8,128)(2,1)}), bf16[64,8,512]{2,1,0:T(8,128)(2,1)S(1)}, u32[]{:S(2)}, u32[]{:S(2)}) %all-to-all-start) | async-done | bytes 524320 | tf_op jit(solution)/shard_map/all_to_all | solution.py:251
  64.4 0.8 %copy-done = bf16[64,8,512]{2,1,0:T(8,128)(2,1)} copy-done((bf16[64,8,512]{2,1,0:T(8,128)(2,1)}, bf16[64,8,512]{2,1,0:T(8,128)(2,1)S(1)}, u32[]{:S(2)}) %copy-start) | copy-done | bytes 524312
  65.2 2.8 %combine.1 = bf16[8,1024]{1,0:T(8,128)(2,1)} custom-call(bf16[512,512]{1,0:T(8,128)(2,1)} %bitcast.4, bf16[512,1024]{1,0:T(8,128)(2,1)} %value_output.1.refs_1_, bf16[8,1024]{1,0:T(8,128)(2,1)} %constant_dynamic-slice_fusion.refs_2_), custom_call_target="tpu_custom_call" | custom-call | flops 16777216 | bytes 2097152 | tf_op jit(solution)/shard_map/combine/pallas_call | solution.py:261
  (11 shorter events, 0.1 us)
Async XLA Ops:
  0.7 7.6 %collective-permute-start = (bf16[1,56,6]{1,0,2:T(2,128)(2,1)S(1)}, bf16[1,56,6]{1,0,2:T(2,128)(2,1)S(1)}, u32[]{:S(2)}, u32[]{:S(2)}) collective-permute-start(bf16[1,56,6]{1,0,2:T(2,128)(2,1)S(1)} %get-tuple-element.13), channel_id=1, source_target_pairs={{0,4},{4,8},{8,12},{12,16},{16,20},{20,24},{24,28},{28,32},{32,36}... | collective-permute-start | bytes 2024 | tf_op jit(solution)/shard_map/ppermute | solution.py:31
  4.2 5.5 %collective-permute-start.1 = (bf16[1,56,6]{1,0,2:T(2,128)(2,1)S(1)}, bf16[1,56,6]{1,0,2:T(2,128)(2,1)S(1)}, u32[]{:S(2)}, u32[]{:S(2)}) collective-permute-start(bf16[1,56,6]{1,0,2:T(2,128)(2,1)S(1)} %get-tuple-element.14), channel_id=1, source_target_pairs={{4,0},{8,4},{12,8},{16,12},{20,16},{24,20},{28,24},{32,28},{36,32}... | collective-permute-start | bytes 2024 | tf_op jit(solution)/shard_map/ppermute | solution.py:33
  10.5 12.1 %collective-permute-start.2 = (bf16[16,1,6]{1,0,2:T(8,128)(2,1)S(1)}, bf16[16,1,6]{1,0,2:T(8,128)(2,1)S(1)}, u32[]{:S(2)}, u32[]{:S(2)}) collective-permute-start(bf16[16,1,6]{1,0,2:T(8,128)(2,1)S(1)} %get-tuple-element.12), channel_id=1, source_target_pairs={{0,1},{1,2},{2,3},{4,5},{5,6},{6,7},{8,9},{9,10},{10,11},{12,13},{... | collective-permute-start | bytes 584 | tf_op jit(solution)/shard_map/ppermute | solution.py:31
  14.4 8.3 %collective-permute-start.3 = (bf16[16,1,6]{1,0,2:T(8,128)(2,1)S(1)}, bf16[16,1,6]{1,0,2:T(8,128)(2,1)S(1)}, u32[]{:S(2)}, u32[]{:S(2)}) collective-permute-start(bf16[16,1,6]{1,0,2:T(8,128)(2,1)S(1)} %get-tuple-element.11), channel_id=1, source_target_pairs={{1,0},{2,1},{3,2},{5,4},{6,5},{7,6},{9,8},{10,9},{11,10},{13,12},{... | collective-permute-start | bytes 584 | tf_op jit(solution)/shard_map/ppermute | solution.py:33
  16.4 6.2 %copy-start.1 = (bf16[14,56,6]{1,0,2:T(8,128)(2,1)S(1)}, bf16[14,56,6]{1,0,2:T(8,128)(2,1)}, u32[]{:S(2)}) copy-start(bf16[14,56,6]{1,0,2:T(8,128)(2,1)} %param.9) | copy-start | bytes 28228
  36.1 28.3 %all-to-all-start = ((bf16[64,8,512]{2,1,0:T(8,128)(2,1)}), bf16[64,8,512]{2,1,0:T(8,128)(2,1)S(1)}, u32[]{:S(2)}, u32[]{:S(2)}) async-start(bf16[64,8,512]{2,1,0:T(8,128)(2,1)} %bitcast.5), calls=%async_computation | async-start | bytes 1048576 | tf_op jit(solution)/shard_map/all_to_all | solution.py:251
  64.4 0.8 %copy-start = (bf16[64,8,512]{2,1,0:T(8,128)(2,1)}, bf16[64,8,512]{2,1,0:T(8,128)(2,1)S(1)}, u32[]{:S(2)}) copy-start(bf16[64,8,512]{2,1,0:T(8,128)(2,1)S(1)} %all-to-all-done) | copy-start | bytes 1572868

commit v2 on v0

v2 whole, which is shorter than its diff:
```python
import functools

import jax
import jax.numpy as jnp
from jax import lax
from jax.experimental import pallas as pl
from jax.experimental.pallas import tpu as pltpu
from jax.sharding import PartitionSpec as P

HEADS = 8
DH = 128
LANES = 128
SUB = 8
TAPS = 9
CELL = 64
LINE = 256
SPAN = 80
ONE, MASK, ONE_TOO = 72, 73, 74
SLOT = 64
TOTAL, TOP = 54, 57
BIG = 1e30
EPS = 1e-05
LOG2E = 1.4426950408889634
GROUP = ("gx", "gy")
F32 = jnp.float32
BF16 = jnp.bfloat16


def product(a, b, left, right):
    return lax.dot_general(a, b, (((left,), (right,)), ((), ())), preferred_element_type=F32)


def nn(a, b):
    return product(a, b, 1, 0)


def nt(a, b):
    return product(a, b, 1, 1)


def tn(a, b):
    return product(a, b, 0, 0)


def iota(shape, dim):
    return lax.broadcasted_iota(jnp.int32, shape, dim)


def split_up(values):
    high = values.astype(BF16)
    return high, (values - high.astype(F32)).astype(BF16)


def thrice(values):
    one = values.astype(BF16)
    rest = values - one.astype(F32)
    two, three = split_up(rest)
    return one, two, three


def pack_kernel(pixel_ref, copies_ref):
    rows, columns, channels = pixel_ref.shape
    values = pixel_ref[...].astype(F32)
    values = jnp.concatenate([values, jnp.zeros((rows, CELL - columns, channels), F32)], axis=1)
    values = values.reshape(rows * CELL, channels).astype(BF16)
    pick = jnp.where(iota((SUB, channels), 0) == iota((SUB, channels), 1), 1.0, 0.0).astype(BF16)
    packed = nt(pick, values).astype(BF16)
    for copy in range(copies_ref.shape[0]):
        copies_ref[copy] = packed


def join_kernel(columns, tiles_ref, strip_ref, first_ref, last_ref):
    tiles, _, width = tiles_ref.shape
    pairs = width // LANES
    lane = iota((pairs * SUB, LANES), 1)
    stacked = [
        jnp.concatenate([tiles_ref[tile, :, pair * LANES : (pair + 1) * LANES].astype(F32) for pair in range(pairs)], axis=0)
        for tile in range(tiles)
    ]
    for parity in range(2):
        halves = []
        for half in range(LINE // LANES):
            line = jnp.zeros((pairs * SUB, LANES), F32)
            for tile in range(tiles):
                start, end = tile * columns - half * LANES, (tile + 1) * columns - half * LANES
                if end <= 0 or start >= LANES:
                    continue
                moved = pltpu.roll(stacked[tile], (start - parity * CELL) % LANES, 1)
                line = jnp.where((lane >= start) & (lane < end), moved, line)
            halves.append(line)
        for pair in range(pairs):
            row = 2 * pair + parity
            for half, line in enumerate(halves):
                at = row * LINE + half * LANES
                strip_ref[:, at : at + LANES] = line[pair * SUB : (pair + 1) * SUB]
    first_ref[...] = strip_ref[:, :LINE].astype(BF16)
    last_ref[...] = strip_ref[:, 2 * pairs * LINE - LINE :].astype(BF16)


def spread_weight(conv_ref, copies):
    channels = conv_ref.shape[0] // TAPS
    shape = (copies, conv_ref.shape[0])
    row, tap = iota(shape, 0), iota(shape, 1)
    place = row % SPAN
    hit = (place // SUB == tap // channels) & (place % SUB == tap % channels) & (row < 3 * SPAN)
    spread = nn(jnp.where(hit, 1.0, 0.0).astype(BF16), conv_ref[...])
    return spread - jnp.mean(spread, axis=-1, keepdims=True)


def query_kernel(
    lat_ref, lat_gain_ref, conv_ref, gain_ref, query_hbm, key_hbm, rows_ref, gram_ref, wide_ref, diag_ref, query_ref, key_ref, sems
):
    width = query_ref.shape[1]
    at = pl.multiple_of(lax.axis_index("gy") * width, width)
    query_copy = pltpu.make_async_copy(query_hbm.at[:, pl.ds(at, width)], query_ref, sems.at[0])
    key_copy = pltpu.make_async_copy(key_hbm.at[:, pl.ds(at, width)], key_ref, sems.at[1])
    query_copy.start()
    key_copy.start()

    weight = spread_weight(conv_ref, LINE)
    feat = weight.shape[1]
    high, low = split_up(weight[:SPAN])
    wide_ref[...] = jnp.concatenate([high, low], axis=0)
    both = jnp.concatenate([high, low], axis=0)
    padding = jnp.zeros((LANES - SPAN, feat), BF16)
    gram = nt(both, jnp.concatenate([high, padding], axis=0)) + nt(both, jnp.concatenate([low, padding], axis=0))
    gram = (gram[:SPAN] + gram[SPAN:]) * (1.0 / feat)
    gram_ref[...] = jnp.concatenate(thrice(gram), axis=0)
    shape = (SPAN, LANES)
    diag = jnp.sum(jnp.where(iota(shape, 0) == iota(shape, 1), gram, 0.0), axis=-1, keepdims=True)
    diag_ref[...] = jnp.broadcast_to(diag, shape)

    values = lat_ref[...].astype(F32)
    centred = values - jnp.mean(values, axis=-1, keepdims=True)
    variance = jnp.mean(centred * centred, axis=-1, keepdims=True)
    gain = lat_gain_ref[...].reshape(1, -1)
    normed = (centred * lax.rsqrt(variance + EPS) * gain).astype(BF16)
    query_copy.wait()
    queries = nn(normed, query_ref[...]).astype(BF16)

    key_copy.wait()
    high, low = split_up(weight * gain_ref[...].reshape(1, -1))
    keys = (nn(high, key_ref[...]) + nn(low, key_ref[...])) * (LOG2E / DH**0.5)
    high, low = split_up(keys)
    count = values.shape[0]
    lane = iota((count, LINE), 1)
    for head in range(width // DH):
        cut = slice(head * DH, (head + 1) * DH)
        query = jnp.concatenate([queries[:, cut], queries[:, cut]], axis=1)
        rows = nt(query, jnp.concatenate([high[:, cut], low[:, cut]], axis=1))
        rows = jnp.where(lane == MASK, -1.0, rows)
        top, rest = split_up(rows)
        rows_ref[head * count : (head + 1) * count, :] = jnp.where((lane >= SPAN) & (lane < 2 * SPAN), rest, top)


def scaled_patches(patches, explicit, gram_ref, wide_ref, diag_ref):
    exact = patches.astype(BF16)
    if explicit:
        high, low = wide_ref[:SPAN], wide_ref[SPAN:]
        features = tn(high, exact) + tn(low, exact)
        variance = jnp.mean(features * features, axis=0, keepdims=True)
        lost = None
    else:
        form = nn(gram_ref[:, :SPAN], exact)
        form = form[:SPAN] + form[SPAN : 2 * SPAN] + form[2 * SPAN :]
        variance = jnp.maximum(jnp.sum(form * patches, axis=0, keepdims=True), 0.0)
        scale = jnp.sum(patches * patches * diag_ref[:, :1], axis=0, keepdims=True)
        lost = jnp.where((variance + EPS) * 128.0 < scale, 1.0, 0.0)
    return patches * lax.rsqrt(variance + EPS), lost


def pixel_block(cells, real):
    del real
    return jnp.concatenate(cells + [jnp.zeros_like(cells[0])], axis=0)


def fill_block(patches, columns, explicit, gram_ref, wide_ref, diag_ref, pixel_ref, at):
    width = patches.shape[1]
    scaled, lost = scaled_patches(patches, explicit, gram_ref, wide_ref, diag_ref)
    row, lane = iota((SPAN, width), 0), iota((SPAN, width), 1)
    real = lane % LINE < columns
    scaled = jnp.where((row == ONE) | (row == ONE_TOO), jnp.where(real, 1.0, 0.0), scaled)
    scaled = jnp.where(row == MASK, jnp.where(real, 0.0, BIG), scaled)
    high, low = split_up(scaled)
    cut = slice(at, at + width)
    pixel_ref[:SPAN, cut] = high
    pixel_ref[SPAN : 2 * SPAN, cut] = high
    pixel_ref[2 * SPAN : 3 * SPAN, cut] = low
    pixel_ref[3 * SPAN :, cut] = jnp.zeros((LINE - 3 * SPAN, width), BF16)
    return lost


def attend(blocks, rows_ref, pixel_ref, score_ref, expo_ref):
    tops, sums = {}, {}
    count = len(blocks)
    for turn in range(count + 2):
        if turn < count:
            cut = slice(blocks[turn][0], blocks[turn][1])
            score_ref[turn % 2, :, : cut.stop - cut.start] = nn(rows_ref[...], pixel_ref[:, cut])
        if 0 <= turn - 1 < count:
            block = turn - 1
            size = blocks[block][1] - blocks[block][0]
            top = jnp.max(score_ref[block % 2, :, :size], axis=-1, keepdims=True)
            expo_ref[block % 2, :, :size] = jnp.exp2(score_ref[block % 2, :, :size] - top).astype(BF16)
            tops[block] = top
        if 0 <= turn - 2 < count:
            block = turn - 2
            cut = slice(blocks[block][0], blocks[block][1])
            sums[block] = nt(expo_ref[block % 2, :, : cut.stop - cut.start], pixel_ref[:LANES, cut])
    return tops, sums


def merged(tops, sums):
    top = functools.reduce(jnp.maximum, tops)
    total = sum(jnp.exp2(t - top) * s for t, s in zip(tops, sums))
    return top, total


def inner_kernel(
    columns, size, strip_ref, rows_ref, gram_ref, wide_ref, diag_ref, sums_ref, tops_ref, pixel_ref, score_ref, expo_ref
):
    width = strip_ref.shape[1]
    inner = width - 2 * LINE
    strip = strip_ref[...]
    shifted = [pltpu.roll(strip, 1, 1), strip, pltpu.roll(strip, width - 1, 1)]
    blocks = [(at, at + size) for at in range(0, inner, size)]

    def run(explicit):
        flags = []
        for at, end in blocks:
            cells = [shifted[tap % 3][:, tap // 3 * LINE + at : tap // 3 * LINE + end] for tap in range(TAPS)]
            patches = jnp.concatenate(cells + [jnp.zeros_like(cells[0])], axis=0)
            flags.append(fill_block(patches, columns, explicit, gram_ref, wide_ref, diag_ref, pixel_ref, at))
        tops, sums = attend(blocks, rows_ref, pixel_ref, score_ref, expo_ref)
        top, total = merged(list(tops.values()), list(sums.values()))
        sums_ref[...] = total
        tops_ref[...] = jnp.broadcast_to(top, tops_ref.shape)
        return flags

    lost = jnp.max(functools.reduce(jnp.maximum, run(False)))

    @pl.when(lost > 0.5)
    def _():
        run(True)


def border_kernel(
    columns,
    strip_ref,
    before_ref,
    after_ref,
    rows_ref,
    gram_ref,
    wide_ref,
    diag_ref,
    inner_sums_ref,
    inner_tops_ref,
    sent_ref,
    pixel_ref,
    score_ref,
    expo_ref,
):
    width = strip_ref.shape[1]
    lines = jnp.concatenate(
        [
            before_ref[...].astype(F32),
            strip_ref[:, : 2 * LINE],
            strip_ref[:, width - 2 * LINE :],
            after_ref[...].astype(F32),
        ],
        axis=1,
    )
    shifted = [pltpu.roll(lines, 1, 1), lines, pltpu.roll(lines, lines.shape[1] - 1, 1)]
    cells = []
    for tap in range(TAPS):
        at = tap // 3 * LINE
        source = shifted[tap % 3]
        cells.append(jnp.concatenate([source[:, at : at + LINE], source[:, at + 3 * LINE : at + 4 * LINE]], axis=1))
    patches = jnp.concatenate(cells + [jnp.zeros_like(cells[0])], axis=0)
    count = sent_ref.shape[0]
    shape = (2 * LANES, LANES)
    row, lane = iota(shape, 0), iota(shape, 1)
    tap = row % LANES
    target = jnp.where((tap < ONE) & (tap % SUB < 6), tap // SUB * 6 + tap % SUB, -1)
    target = jnp.where(tap == ONE, TOTAL, jnp.where(tap == ONE_TOO, TOTAL + 1, target))
    place = jnp.where((target >= 0) & (lane == target + row // LANES * SLOT), 1.0, 0.0).astype(BF16)

    def run(explicit):
        lost = fill_block(patches, columns, explicit, gram_ref, wide_ref, diag_ref, pixel_ref, 0)
        tops, sums = attend([(0, patches.shape[1])], rows_ref, pixel_ref, score_ref, expo_ref)
        top, total = merged([inner_tops_ref[...], tops[0]], [inner_sums_ref[...], sums[0]])
        high = total.astype(BF16)
        low = (total - high.astype(F32)).astype(BF16)
        high = jnp.where(iota(total.shape, 1) == ONE_TOO, low, high)
        placed = nn(jnp.concatenate([high[:count], high[count:]], axis=1), place)
        lane = iota((count, LANES), 1)
        column = lane % SLOT
        one, two, three = thrice(jnp.where(lane < SLOT, top[:count], top[count:]))
        placed = jnp.where(column == TOP, one.astype(F32), placed)
        placed = jnp.where(column == TOP + 1, two.astype(F32), placed)
        placed = jnp.where(column == TOP + 2, three.astype(F32), placed)
        sent_ref[...] = placed.astype(BF16)
        return lost

    lost = jnp.max(run(False))

    @pl.when(lost > 0.5)
    def _():
        run(True)


def output_kernel(conv_ref, gain_ref, value_ref, out_ref, both_ref):
    weight = conv_ref[...].astype(F32)
    weight = (weight - jnp.mean(weight, axis=-1, keepdims=True)) * gain_ref[...].reshape(1, -1)
    weight = jnp.concatenate([weight, jnp.zeros((SLOT - weight.shape[0], weight.shape[1]), F32)], axis=0)
    both = nn(jnp.concatenate(split_up(weight), axis=0), value_ref[...])
    high, low = split_up(both[:SLOT] + both[SLOT:])
    for head in range(HEADS):
        cut = slice(head * DH, (head + 1) * DH)
        both = nn(jnp.concatenate([high[:, cut], low[:, cut]], axis=0), out_ref[cut])
        both_ref[head * SLOT : (head + 1) * SLOT, :] = (both[:SLOT] + both[SLOT:]).astype(BF16)


def combine_kernel(share, parts_ref, both_ref, own_ref, result_ref):
    count = parts_ref.shape[0]
    pairs = both_ref.shape[0] // LANES
    row, lane = iota((LANES, LANES), 0), iota((LANES, LANES), 1)
    same = row // SLOT == lane // SLOT
    column = row % SLOT
    pick_top = jnp.where(same & (column >= TOP) & (column < TOP + 3), 1.0, 0.0).astype(BF16)
    pick_one = jnp.where(same & (column >= TOTAL) & (column < TOTAL + 2), 1.0, 0.0).astype(BF16)
    parts = parts_ref[...]
    shape = (count // (pairs * share), pairs * share, LANES)
    tops = nn(parts, pick_top).reshape(shape)
    ones = nn(parts, pick_one).reshape(shape)
    factor = jnp.exp2(tops - jnp.max(tops, axis=0, keepdims=True))
    sums = jnp.sum(factor * parts.astype(F32).reshape(shape), axis=0)
    total = jnp.sum(factor * ones, axis=0)
    mean = sums / total
    mean = jnp.concatenate([mean[pair * share : (pair + 1) * share] for pair in range(pairs)], axis=1)
    high = mean.astype(BF16).astype(F32)
    result = nn(jnp.concatenate([high, mean - high], axis=0).astype(BF16), both_ref[...])
    result = own_ref[...].astype(F32) + (result[:share] + result[share:])
    result_ref[...] = result.astype(BF16)


def vmem(count):
    return [pl.BlockSpec(memory_space=pltpu.VMEM)] * count


def kernel(body, name, outs, scratch=(), others=0, count=0, cycles=1000):
    single = not isinstance(outs, (list, tuple))
    return pl.pallas_call(
        body,
        out_shape=outs,
        in_specs=vmem(count) + [pl.BlockSpec(memory_space=pl.ANY)] * others,
        out_specs=vmem(1)[0] if single else tuple(vmem(len(outs))),
        scratch_shapes=list(scratch),
        cost_estimate=pl.CostEstimate(flops=cycles * 4096, bytes_accessed=1 << 20, transcendentals=0),
        name=name,
    )


def on_device(
    pixels,
    conv_weight,
    input_gain,
    key_weight,
    value_weight,
    latents,
    latent_gain,
    query_weight,
    out_weight,
):
    tile_rows, tile_cols, _ = pixels.shape
    across, down = lax.axis_size("gy"), lax.axis_size("gx")
    columns = tile_cols * across
    feat = conv_weight.shape[1]
    lat, width = latents.shape
    heads = HEADS // across
    share = lat // (across * down)

    def shape(dims, dtype=BF16):
        return jax.ShapeDtypeStruct(dims, dtype)

    copies = kernel(pack_kernel, "pack", shape((across, SUB, tile_rows * CELL)), count=1)(pixels)
    tiles = lax.all_to_all(copies, "gy", 0, 0, tiled=True)
    rows, gram, wide, diag = kernel(
        query_kernel,
        "query_rows",
        [
            shape((heads * lat, LINE)),
            shape((3 * SPAN, LANES)),
            shape((2 * SPAN, feat)),
            shape((SPAN, LANES), F32),
        ],
        [
            pltpu.VMEM((width, heads * DH), BF16),
            pltpu.VMEM((feat, heads * DH), BF16),
            pltpu.SemaphoreType.DMA((2,)),
        ],
        others=2,
        count=4,
        cycles=6000,
    )(latents, latent_gain, conv_weight, input_gain, query_weight, key_weight)
    both = kernel(
        output_kernel, "value_output", shape((HEADS * SLOT, width)), count=4, cycles=6000
    )(conv_weight, input_gain, value_weight, out_weight)

    strip, first, last = kernel(
        functools.partial(join_kernel, tile_cols),
        "join",
        [shape((SUB, tile_rows * LINE), F32), shape((SUB, LINE)), shape((SUB, LINE))],
        count=1,
    )(tiles)
    before = lax.ppermute(last, "gx", [(i, i + 1) for i in range(down - 1)])
    after = lax.ppermute(first, "gx", [(i + 1, i) for i in range(down - 1)])
    inner = (tile_rows - 2) * LINE
    size = inner // 3
    sums, tops = kernel(
        functools.partial(inner_kernel, columns, size),
        "inner",
        [shape((heads * lat, LANES), F32), shape((heads * lat, LANES), F32)],
        [
            pltpu.VMEM((LINE, inner), BF16),
            pltpu.VMEM((2, heads * lat, size), F32),
            pltpu.VMEM((2, heads * lat, size), BF16),
        ],
        count=5,
        cycles=10000,
    )(strip, rows, gram, wide, diag)
    sent = kernel(
        functools.partial(border_kernel, columns),
        "border",
        shape((lat, heads * SLOT)),
        [
            pltpu.VMEM((LINE, 2 * LINE), BF16),
            pltpu.VMEM((2, heads * lat, 2 * LINE), F32),
            pltpu.VMEM((2, heads * lat, 2 * LINE), BF16),
        ],
        count=9,
        cycles=3000,
    )(strip, before, after, rows, gram, wide, diag, sums, tops)
    devices = across * down
    parts = lax.all_to_all(sent.reshape(devices, share, -1), GROUP, 0, 0, tiled=True)
    own = lax.dynamic_slice_in_dim(latents, lax.axis_index(GROUP) * share, share, 0)
    return kernel(
        functools.partial(combine_kernel, share), "combine", shape((share, width)), count=3
    )(parts.reshape(devices * share, -1), both, own)


def solution(mesh):
    return jax.shard_map(
        on_device,
        mesh=mesh,
        in_specs=(P(("ba", "gx"), "gy", None), P(), P(), P(), P(), P(), P(), P(), P()),
        out_specs=P(("ba", "gx", "gy"), None),
        check_vma=False,
    )
```

time: 177 us -> 57.9 us (0.33)
  waiting for transfers between devices: 53.1 us -> 4.17 us
  blocking collectives: 37.9 us -> 0 us
  matrix products: 37.3 us -> 0 us
  Pallas kernels: 0 us -> 25.4 us
  other arithmetic: 12.2 us -> 0 us
  local copies, waits for them, and re-layouts: 12.3 us -> 4.75 us
  starting transfers between devices: 17 us -> 22.6 us
  loops' own time: 5.5 us -> 0 us
    all_to_all x1 -> x2, waiting for transfers between devices: 49.4 us -> 4.17 us  [the longest x1 4.16 us: on_device(): lax.all_to_all(sent.reshape(devices, share, -1), GROUP, 0, 0, tiled=True)]
    all_to_all x1 -> x0, blocking collectives: 37.9 us -> none  [sent_to_all(): return lax.all_to_all(copies, axis, split_axis=0, concat_axis=0, tiled=True)]
    dot_general x21 -> x0, matrix products: 37.3 us -> none  [the longest x8 16.9 us: one_head(): jnp.dot(expo.astype(jnp.bfloat16), value_head, preferred_element_type=jnp...]
    pallas_call x0 -> x7, Pallas kernels: none -> 25.4 us  [the longest x1 7.21 us: on_device(): kernel(functools.partial(inner_kernel, columns, size), 'inner', [shape((h...]
    all_to_all x1 -> x2, starting transfers between devices: 6.29 us -> 17.8 us  [the longest x1 11.8 us: on_device(): lax.all_to_all(sent.reshape(devices, share, -1), GROUP, 0, 0, tiled=True)]
    reduce_sum x12 -> x0, other arithmetic: 8.21 us -> none  [the longest x8 2.47 us: one_head(): total = jnp.sum(expo, axis=-1)]
    ppermute x4 -> x2, starting transfers between devices: 10.7 us -> 4.76 us  [the longest x1 3.47 us: on_device(): before = lax.ppermute(last, 'gx', [(i, i + 1) for i in range(down - 1)])]
    another operation x1 -> x0, loops' own time: 5.5 us -> none  [on_device(): lax.map(one_head, jnp.arange(HEADS, dtype=jnp.int32))]
  transfers between devices with their start and end apart: 5 -> 4, of which waited for: 2 -> 1; matrix products, arithmetic and copies ran while one was open for 3% -> 2% of each run, Pallas kernels for 0% -> 28%
where the time goes in v2:
time: 57.9 us; the launch traced here: 57 us
  Pallas kernels  25.4 us (44%)
  starting transfers between devices  22.6 us (39%)
  local copies, waits for them, and re-layouts  4.75 us (8%)
  waiting for transfers between devices  4.17 us (7%)
    all_to_all x1, starting transfers between devices, on_device(): lax.all_to_all(sent.reshape(devices, share, -1), GROUP, 0, 0, tiled=True)  11.8 us
    pallas_call x1, Pallas kernels, on_device(): kernel(functools.partial(inner_kernel, columns, size), 'inner', [shape((h...  7.21 us
    all_to_all x1, starting transfers between devices, on_device(): tiles = lax.all_to_all(copies, 'gy', 0, 0, tiled=True)  6 us
    pallas_call x1, Pallas kernels, on_device(): kernel(query_kernel, 'query_rows', [shape((heads * lat, LINE)), shape((3...  4.77 us
    all_to_all x1, waiting for transfers between devices, on_device(): lax.all_to_all(sent.reshape(devices, share, -1), GROUP, 0, 0, tiled=True)  4.16 us
    pallas_call x1, Pallas kernels, on_device(): kernel(output_kernel, 'value_output', shape((HEADS * SLOT, width)), count...  4.06 us
    pallas_call x1, Pallas kernels, on_device(): kernel(functools.partial(border_kernel, columns), 'border', shape((lat, h...  3.74 us
    ppermute x1, starting transfers between devices, on_device(): before = lax.ppermute(last, 'gx', [(i, i + 1) for i in range(down - 1)])  3.47 us
  transfers between devices with their start and end apart: 4, of which 1 were waited for; matrix products, arithmetic and copies ran while one was open for 2% of the time, Pallas kernels for 28%

profile of v2, /device:TPU:32, one launch (start us, length us, event | category | flops | bytes accessed | tf_op | source)
XLA Modules:
  0.0 57.0 jit_solution(1887019568995372357)
XLA Ops:
  0.0 1.6 %copy.10.pixel_ref = bf16[14,56,6]{2,1,0:T(8,128)(2,1)} copy(bf16[14,56,6]{1,0,2:T(8,128)(2,1)} %param.9) | data formatting | bytes 18816 | tf_op args[0]
  1.6 1.7 %pack.1 = bf16[4,8,896]{2,1,0:T(8,128)(2,1)} custom-call(bf16[14,56,6]{2,1,0:T(8,128)(2,1)} %copy.10.pixel_ref), custom_call_target="tpu_custom_call" | custom-call | flops 4096000 | bytes 1048576 | tf_op jit(solution)/shard_map/pack/pallas_call | solution.py:386
  3.3 6.0 %all-to-all-start = ((bf16[4,8,896]{2,1,0:T(8,128)(2,1)}), bf16[4,8,896]{2,1,0:T(8,128)(2,1)S(1)}, u32[]{:S(2)}, u32[]{:S(2)}) async-start(bf16[4,8,896]{2,1,0:T(8,128)(2,1)} %pack.1), calls=%async_computation | async-start | bytes 114688 | tf_op jit(solution)/shard_map/all_to_all | solution.py:387
  9.3 4.8 %query_rows.1 = (bf16[1024,256]{1,0:T(8,128)(2,1)}, bf16[240,128]{1,0:T(8,128)(2,1)}, bf16[160,704]{1,0:T(8,128)(2,1)}, f32[80,128]{1,0:T(8,128)}) custom-call(bf16[512,1024]{1,0:T(8,128)(2,1)} %lat_ref.1, f32[1024]{0:T(1024)} %lat_gain_ref.1, bf16[54,704]{1,0:T(8,128)(2,1)} %conv_ref.3, f32[704]{0:T(1024)} %gain_ref.3, bf16[1024,1024]{1,0:T(8,128)(2,1)} %query_hbm.1, ...), custom_call_target="tpu_custom_call" | custom-call | flops 24576000 | bytes 1048576 | tf_op jit(solution)/shard_map/query_rows/pallas_call | solution.py:388
  14.1 0.0 all-to-all-done.tiles_ref
  14.1 0.0 copy-start.1
  14.1 0.6 %copy-done.1 = bf16[4,8,896]{2,1,0:T(8,128)(2,1)} copy-done((bf16[4,8,896]{2,1,0:T(8,128)(2,1)}, bf16[4,8,896]{2,1,0:T(8,128)(2,1)S(1)}, u32[]{:S(2)}) %copy-start.1) | copy-done | bytes 57368
  14.7 1.6 %join.1 = (f32[8,3584]{1,0:T(8,128)}, bf16[8,256]{1,0:T(8,128)(2,1)}, bf16[8,256]{1,0:T(8,128)(2,1)}) custom-call(bf16[4,8,896]{2,1,0:T(8,128)(2,1)} %copy-done.1), custom_call_target="tpu_custom_call" | custom-call | flops 4096000 | bytes 1048576 | tf_op jit(solution)/shard_map/join/pallas_call | solution.py:410
  16.3 3.5 %collective-permute-start = (bf16[8,256]{1,0:T(8,128)(2,1)}, bf16[8,256]{1,0:T(8,128)(2,1)S(1)}, u32[]{:S(2)}, u32[]{:S(2)}) collective-permute-start(bf16[8,256]{1,0:T(8,128)(2,1)} %get-tuple-element.15), channel_id=1, source_target_pairs={{0,4},{4,8},{8,12},{12,16},{16,20},{20,24},{24,28},{28,32},{32,36}... | collective-permute-start | bytes 12296 | tf_op jit(solution)/shard_map/ppermute | solution.py:416
  19.8 1.3 %collective-permute-start.1 = (bf16[8,256]{1,0:T(8,128)(2,1)}, bf16[8,256]{1,0:T(8,128)(2,1)S(1)}, u32[]{:S(2)}, u32[]{:S(2)}) collective-permute-start(bf16[8,256]{1,0:T(8,128)(2,1)} %get-tuple-element.16), channel_id=1, source_target_pairs={{4,0},{8,4},{12,8},{16,12},{20,16},{24,20},{28,24},{32,28},{36,32}... | collective-permute-start | bytes 12296 | tf_op jit(solution)/shard_map/ppermute | solution.py:417
  21.1 7.2 %inner.1 = (f32[1024,128]{1,0:T(8,128)}, f32[1024,128]{1,0:T(8,128)}) custom-call(f32[8,3584]{1,0:T(8,128)} %get-tuple-element.14.strip_ref, bf16[1024,256]{1,0:T(8,128)(2,1)} %get-tuple-element.17.rows_ref, bf16[240,128]{1,0:T(8,128)(2,1)} %get-tuple-element.18.gram_ref, bf16[160,704]{1,0:T(8,128)(2,1)} %get-tuple-element.19.wide_ref, ...), custom_call_target="tpu_custom_call" | custom-call | flops 40960000 | bytes 1048576 | tf_op jit(solution)/shard_map/inner/pallas_call | solution.py:420
  28.3 0.0 collective-permute-done.before_ref
  28.3 0.0 copy-start.2
  28.3 0.0 collective-permute-done.1.after_ref
  28.3 0.0 copy-start.3
  28.3 0.6 %copy-done.2 = bf16[8,256]{1,0:T(8,128)(2,1)} copy-done((bf16[8,256]{1,0:T(8,128)(2,1)}, bf16[8,256]{1,0:T(8,128)(2,1)S(1)}, u32[]{:S(2)}) %copy-start.2) | copy-done | bytes 4120
  28.9 0.0 copy-done.3
  28.9 3.7 %border.1 = bf16[512,128]{1,0:T(8,128)(2,1)} custom-call(f32[8,3584]{1,0:T(8,128)} %get-tuple-element.14.strip_ref, bf16[8,256]{1,0:T(8,128)(2,1)} %copy-done.2, bf16[8,256]{1,0:T(8,128)(2,1)} %copy-done.3, bf16[1024,256]{1,0:T(8,128)(2,1)} %get-tuple-element.17.rows_ref, bf16[240,128]{1,0:T(8,128)(2,1)} %get-tuple-element.18.gram_ref, ...), custom_call_target="tpu_custom_call" | custom-call | flops 12288000 | bytes 1048576 | tf_op jit(solution)/shard_map/border/pallas_call | solution.py:432
  32.6 11.8 %all-to-all-start.1 = ((bf16[64,8,128]{2,1,0:T(8,128)(2,1)}), bf16[64,8,128]{2,1,0:T(8,128)(2,1)S(1)}, u32[]{:S(2)}, u32[]{:S(2)}) async-start(bf16[64,8,128]{2,1,0:T(8,128)(2,1)} %bitcast.2), calls=%async_computation.1 | async-start | bytes 262144 | tf_op jit(solution)/shard_map/all_to_all | solution.py:445
  44.5 4.1 %value_output.1.both_ref = bf16[512,1024]{1,0:T(8,128)(2,1)} custom-call(bf16[54,704]{1,0:T(8,128)(2,1)} %conv_ref.3, f32[704]{0:T(1024)} %gain_ref.3, bf16[704,1024]{1,0:T(8,128)(2,1)} %value_ref.1, bf16[1024,1024]{1,0:T(8,128)(2,1)} %out_ref.1), custom_call_target="tpu_custom_call" | custom-call | flops 24576000 | bytes 1048576 | tf_op jit(solution)/shard_map/value_output/pallas_call | solution.py:406
  48.5 1.3 %constant_dynamic-slice_fusion.own_ref = bf16[8,1024]{1,0:T(8,128)(2,1)} fusion(bf16[512,1024]{1,0:T(8,128)(2,1)} %lat_ref.1, s32[]{:T(128)S(6)} %select_n.3), kind=kLoop, calls=%fused_computation | loop fusion | bytes 32772 | tf_op jit(solution)/shard_map/dynamic_slice | solution.py:446
  49.8 4.2 %all-to-all-done.1 = bf16[64,8,128]{2,1,0:T(8,128)(2,1)S(1)} async-done(((bf16[64,8,128]{2,1,0:T(8,128)(2,1)}), bf16[64,8,128]{2,1,0:T(8,128)(2,1)S(1)}, u32[]{:S(2)}, u32[]{:S(2)}) %all-to-all-start.1) | async-done | bytes 131104 | tf_op jit(solution)/shard_map/all_to_all | solution.py:445
  54.0 0.6 %copy-done = bf16[64,8,128]{2,1,0:T(8,128)(2,1)} copy-done((bf16[64,8,128]{2,1,0:T(8,128)(2,1)}, bf16[64,8,128]{2,1,0:T(8,128)(2,1)S(1)}, u32[]{:S(2)}) %copy-start) | copy-done | bytes 131096
  54.7 2.3 %combine.1 = bf16[8,1024]{1,0:T(8,128)(2,1)} custom-call(bf16[512,128]{1,0:T(8,128)(2,1)} %bitcast.3, bf16[512,1024]{1,0:T(8,128)(2,1)} %value_output.1.both_ref, bf16[8,1024]{1,0:T(8,128)(2,1)} %constant_dynamic-slice_fusion.own_ref), custom_call_target="tpu_custom_call" | custom-call | flops 4096000 | bytes 1048576 | tf_op jit(solution)/shard_map/combine/pallas_call | solution.py:447
  (1 shorter events, 0.0 us)
Async XLA Ops:
  3.3 10.8 %all-to-all-start = ((bf16[4,8,896]{2,1,0:T(8,128)(2,1)}), bf16[4,8,896]{2,1,0:T(8,128)(2,1)S(1)}, u32[]{:S(2)}, u32[]{:S(2)}) async-start(bf16[4,8,896]{2,1,0:T(8,128)(2,1)} %pack.1), calls=%async_computation | async-start | bytes 114688 | tf_op jit(solution)/shard_map/all_to_all | solution.py:387
  14.1 0.6 %copy-start.1 = (bf16[4,8,896]{2,1,0:T(8,128)(2,1)}, bf16[4,8,896]{2,1,0:T(8,128)(2,1)S(1)}, u32[]{:S(2)}) copy-start(bf16[4,8,896]{2,1,0:T(8,128)(2,1)S(1)} %all-to-all-done.tiles_ref) | copy-start | bytes 172036
  16.3 12.0 %collective-permute-start = (bf16[8,256]{1,0:T(8,128)(2,1)}, bf16[8,256]{1,0:T(8,128)(2,1)S(1)}, u32[]{:S(2)}, u32[]{:S(2)}) collective-permute-start(bf16[8,256]{1,0:T(8,128)(2,1)} %get-tuple-element.15), channel_id=1, source_target_pairs={{0,4},{4,8},{8,12},{12,16},{16,20},{20,24},{24,28},{28,32},{32,36}... | collective-permute-start | bytes 12296 | tf_op jit(solution)/shard_map/ppermute | solution.py:416
  19.8 8.5 %collective-permute-start.1 = (bf16[8,256]{1,0:T(8,128)(2,1)}, bf16[8,256]{1,0:T(8,128)(2,1)S(1)}, u32[]{:S(2)}, u32[]{:S(2)}) collective-permute-start(bf16[8,256]{1,0:T(8,128)(2,1)} %get-tuple-element.16), channel_id=1, source_target_pairs={{4,0},{8,4},{12,8},{16,12},{20,16},{24,20},{28,24},{32,28},{36,32}... | collective-permute-start | bytes 12296 | tf_op jit(solution)/shard_map/ppermute | solution.py:417
  28.3 0.6 %copy-start.2 = (bf16[8,256]{1,0:T(8,128)(2,1)}, bf16[8,256]{1,0:T(8,128)(2,1)S(1)}, u32[]{:S(2)}) copy-start(bf16[8,256]{1,0:T(8,128)(2,1)S(1)} %collective-permute-done.before_ref) | copy-start | bytes 12292
  28.3 0.6 %copy-start.3 = (bf16[8,256]{1,0:T(8,128)(2,1)}, bf16[8,256]{1,0:T(8,128)(2,1)S(1)}, u32[]{:S(2)}) copy-start(bf16[8,256]{1,0:T(8,128)(2,1)S(1)} %collective-permute-done.1.after_ref) | copy-start | bytes 12292
  32.6 21.4 %all-to-all-start.1 = ((bf16[64,8,128]{2,1,0:T(8,128)(2,1)}), bf16[64,8,128]{2,1,0:T(8,128)(2,1)S(1)}, u32[]{:S(2)}, u32[]{:S(2)}) async-start(bf16[64,8,128]{2,1,0:T(8,128)(2,1)} %bitcast.2), calls=%async_computation.1 | async-start | bytes 262144 | tf_op jit(solution)/shard_map/all_to_all | solution.py:445
  54.0 0.6 %copy-start = (bf16[64,8,128]{2,1,0:T(8,128)(2,1)}, bf16[64,8,128]{2,1,0:T(8,128)(2,1)S(1)}, u32[]{:S(2)}) copy-start(bf16[64,8,128]{2,1,0:T(8,128)(2,1)S(1)} %all-to-all-done.1) | copy-start | bytes 393220

commit v3 on v2

--- a/solution.py
+++ b/solution.py
@@ -348,15 +348,16 @@
     return [pl.BlockSpec(memory_space=pltpu.VMEM)] * count
 
 
-def kernel(body, name, outs, scratch=(), others=0, count=0, cycles=1000):
+def kernel(body, name, outs, scratch=(), others=0, count=0, cycles=1000, room=4):
     single = not isinstance(outs, (list, tuple))
     return pl.pallas_call(
         body,
         out_shape=outs,
-        in_specs=vmem(count) + [pl.BlockSpec(memory_space=pl.ANY)] * others,
+        in_specs=vmem(count) + [pl.BlockSpec(memory_space=pltpu.HBM)] * others,
         out_specs=vmem(1)[0] if single else tuple(vmem(len(outs))),
         scratch_shapes=list(scratch),
         cost_estimate=pl.CostEstimate(flops=cycles * 4096, bytes_accessed=1 << 20, transcendentals=0),
+        compiler_params=pltpu.CompilerParams(vmem_limit_bytes=room << 20),
         name=name,
     )
 
@@ -402,9 +403,10 @@
         others=2,
         count=4,
         cycles=6000,
+        room=14,
     )(latents, latent_gain, conv_weight, input_gain, query_weight, key_weight)
     both = kernel(
-        output_kernel, "value_output", shape((HEADS * SLOT, width)), count=4, cycles=6000
+        output_kernel, "value_output", shape((HEADS * SLOT, width)), count=4, cycles=6000, room=10
     )(conv_weight, input_gain, value_weight, out_weight)
 
     strip, first, last = kernel(
@@ -428,6 +430,7 @@
         ],
         count=5,
         cycles=10000,
+        room=34,
     )(strip, rows, gram, wide, diag)
     sent = kernel(
         functools.partial(border_kernel, columns),
@@ -440,12 +443,13 @@
         ],
         count=9,
         cycles=3000,
+        room=16,
     )(strip, before, after, rows, gram, wide, diag, sums, tops)
     devices = across * down
     parts = lax.all_to_all(sent.reshape(devices, share, -1), GROUP, 0, 0, tiled=True)
     own = lax.dynamic_slice_in_dim(latents, lax.axis_index(GROUP) * share, share, 0)
     return kernel(
-        functools.partial(combine_kernel, share), "combine", shape((share, width)), count=3
+        functools.partial(combine_kernel, share), "combine", shape((share, width)), count=3, room=6
     )(parts.reshape(devices * share, -1), both, own)
 
 

time: 57.9 us -> 52.9 us (0.914)
  Pallas kernels: 25.4 us -> 13.2 us
  local copies, waits for them, and re-layouts: 4.75 us -> 9.46 us
  waiting for transfers between devices: 4.17 us -> 6.43 us
    unnamed x9 -> x21, local copies, waits for them, and re-layouts: 3.44 us -> 8.74 us
    pallas_call x1, Pallas kernels: 4.06 us -> 0.99 us  [on_device(): kernel(output_kernel, 'value_output', shape((HEADS * SLOT, width)), count...]
    all_to_all x1, waiting for transfers between devices: 4.16 us -> 6.42 us  [on_device(): lax.all_to_all(sent.reshape(devices, share, -1), GROUP, 0, 0, tiled=True)]
    pallas_call x1, Pallas kernels: 7.21 us -> 5.11 us  [on_device(): kernel(functools.partial(inner_kernel, columns, size), 'inner', [shape((h...]
    pallas_call x1, Pallas kernels: 4.77 us -> 2.85 us  [on_device(): kernel(query_kernel, 'query_rows', [shape((heads * lat, LINE)), shape((3...]
    pallas_call x1, Pallas kernels: 3.74 us -> 2.25 us  [on_device(): kernel(functools.partial(border_kernel, columns), 'border', shape((lat, h...]
    pallas_call x1, Pallas kernels: 1.57 us -> 0.1 us  [on_device(): kernel(functools.partial(join_kernel, tile_cols), 'join', [shape((SUB, ti...]
    pallas_call x1, Pallas kernels: 2.33 us -> 1.11 us  [on_device(): kernel(functools.partial(combine_kernel, share), 'combine', shape((share,...]
  transfers between devices with their start and end apart: 4 -> 4, of which waited for: 1 -> 1; matrix products, arithmetic and copies ran while one was open for 2% -> 1% of each run, Pallas kernels for 28% -> 17%
where the time goes in v3:
time: 52.9 us; the launch traced here: 52 us
  starting transfers between devices  22.7 us (43%)
  Pallas kernels  13.2 us (25%)
  local copies, waits for them, and re-layouts  9.46 us (18%)
  waiting for transfers between devices  6.43 us (12%)
    all_to_all x1, starting transfers between devices, on_device(): lax.all_to_all(sent.reshape(devices, share, -1), GROUP, 0, 0, tiled=True)  11.8 us
    unnamed x21, local copies, waits for them, and re-layouts  8.74 us
    all_to_all x1, waiting for transfers between devices, on_device(): lax.all_to_all(sent.reshape(devices, share, -1), GROUP, 0, 0, tiled=True)  6.42 us
    all_to_all x1, starting transfers between devices, on_device(): tiles = lax.all_to_all(copies, 'gy', 0, 0, tiled=True)  6 us
    pallas_call x1, Pallas kernels, on_device(): kernel(functools.partial(inner_kernel, columns, size), 'inner', [shape((h...  5.11 us
    ppermute x1, starting transfers between devices, on_device(): before = lax.ppermute(last, 'gx', [(i, i + 1) for i in range(down - 1)])  3.6 us
    pallas_call x1, Pallas kernels, on_device(): kernel(query_kernel, 'query_rows', [shape((heads * lat, LINE)), shape((3...  2.85 us
    pallas_call x1, Pallas kernels, on_device(): kernel(functools.partial(border_kernel, columns), 'border', shape((lat, h...  2.25 us
  transfers between devices with their start and end apart: 4, of which 1 were waited for; matrix products, arithmetic and copies ran while one was open for 1% of the time, Pallas kernels for 17%

profile of v3, /device:TPU:32, one launch (start us, length us, event | category | flops | bytes accessed | tf_op | source)
XLA Modules:
  0.0 52.0 jit_solution(2103910096026933402)
XLA Ops:
  0.0 0.9 %copy.10.pixel_ref = bf16[14,56,6]{2,1,0:T(8,128)(2,1)S(1)} copy(bf16[14,56,6]{1,0,2:T(8,128)(2,1)} %param.9) | data formatting | bytes 18816 | tf_op args[0]
  0.9 0.8 %pack.1 = bf16[4,8,896]{2,1,0:T(8,128)(2,1)} custom-call(bf16[14,56,6]{2,1,0:T(8,128)(2,1)S(1)} %copy.10.pixel_ref), custom_call_target="tpu_custom_call" | custom-call | flops 4096000 | bytes 1048576 | tf_op jit(solution)/shard_map/pack/pallas_call | solution.py:387
  1.7 6.0 %all-to-all-start = ((bf16[4,8,896]{2,1,0:T(8,128)(2,1)}), bf16[4,8,896]{2,1,0:T(8,128)(2,1)S(1)}, u32[]{:S(2)}, u32[]{:S(2)}) async-start(bf16[4,8,896]{2,1,0:T(8,128)(2,1)} %pack.1), calls=%async_computation | async-start | bytes 114688 | tf_op jit(solution)/shard_map/all_to_all | solution.py:388
  7.7 1.6 %copy-done.1 = bf16[1024,1024]{1,0:T(8,128)(2,1)S(1)} copy-done((bf16[1024,1024]{1,0:T(8,128)(2,1)S(1)}, bf16[1024,1024]{1,0:T(8,128)(2,1)}, u32[]{:S(2)}) %copy-start.1) | copy-done | bytes 2097176
  9.3 1.4 %copy-done.2 = bf16[704,1024]{1,0:T(8,128)(2,1)S(1)} copy-done((bf16[704,1024]{1,0:T(8,128)(2,1)S(1)}, bf16[704,1024]{1,0:T(8,128)(2,1)}, u32[]{:S(2)}) %copy-start.2) | copy-done | bytes 1441816
  10.7 1.2 %copy-done.4 = bf16[512,1024]{1,0:T(8,128)(2,1)S(1)} copy-done((bf16[512,1024]{1,0:T(8,128)(2,1)S(1)}, bf16[512,1024]{1,0:T(8,128)(2,1)}, u32[]{:S(2)}) %copy-start.4) | copy-done | bytes 1048600
  11.9 0.9 %copy-done.5 = bf16[54,704]{1,0:T(8,128)(2,1)S(1)} copy-done((bf16[54,704]{1,0:T(8,128)(2,1)S(1)}, bf16[54,704]{1,0:T(8,128)(2,1)}, u32[]{:S(2)}) %copy-start.5) | copy-done | bytes 76056
  12.8 0.7 %copy-done.7 = f32[704]{0:T(1024)S(1)} copy-done((f32[704]{0:T(1024)S(1)}, f32[704]{0:T(1024)}, u32[]{:S(2)}) %copy-start.7) | copy-done | bytes 2840
  13.5 0.7 %copy-done.9 = f32[1024]{0:T(1024)S(1)} copy-done((f32[1024]{0:T(1024)S(1)}, f32[1024]{0:T(1024)}, u32[]{:S(2)}) %copy-start.9) | copy-done | bytes 4120
  14.2 2.9 %query_rows.1 = (bf16[1024,256]{1,0:T(8,128)(2,1)S(1)}, bf16[240,128]{1,0:T(8,128)(2,1)S(1)}, bf16[160,704]{1,0:T(8,128)(2,1)S(1)}, f32[80,128]{1,0:T(8,128)S(1)}) custom-call(bf16[512,1024]{1,0:T(8,128)(2,1)S(1)} %copy-done.4, f32[1024]{0:T(1024)S(1)} %copy-done.9, bf16[54,704]{1,0:T(8,128)(2,1)S(1)} %copy-done.5, f32[704]{0:T(1024)S(1)} %copy-done.7, ...), custom_call_target="tpu_custom_call" | custom-call | flops 24576000 | bytes 1048576 | tf_op jit(solution)/shard_map/query_rows/pallas_call | solution.py:389
  17.0 0.0 copy-start
  17.1 0.0 copy-start.6
  17.1 0.0 copy-start.8
  17.1 0.1 join.1
  17.2 3.6 %collective-permute-start = (bf16[8,256]{1,0:T(8,128)(2,1)S(1)}, bf16[8,256]{1,0:T(8,128)(2,1)S(1)}, u32[]{:S(2)}, u32[]{:S(2)}) collective-permute-start(bf16[8,256]{1,0:T(8,128)(2,1)S(1)} %get-tuple-element.15), channel_id=1, source_target_pairs={{0,4},{4,8},{8,12},{12,16},{16,20},{20,24},{24,28},{28,32},{32,36}... | collective-permute-start | bytes 12296 | tf_op jit(solution)/shard_map/ppermute | solution.py:418
  20.8 1.3 %collective-permute-start.1 = (bf16[8,256]{1,0:T(8,128)(2,1)S(1)}, bf16[8,256]{1,0:T(8,128)(2,1)S(1)}, u32[]{:S(2)}, u32[]{:S(2)}) collective-permute-start(bf16[8,256]{1,0:T(8,128)(2,1)S(1)} %get-tuple-element.16), channel_id=1, source_target_pairs={{4,0},{8,4},{12,8},{16,12},{20,16},{24,20},{28,24},{32,28},{36,32}... | collective-permute-start | bytes 12296 | tf_op jit(solution)/shard_map/ppermute | solution.py:419
  22.1 5.1 %inner.1 = (f32[1024,128]{1,0:T(8,128)S(1)}, f32[1024,128]{1,0:T(8,128)S(1)}) custom-call(f32[8,3584]{1,0:T(8,128)S(1)} %get-tuple-element.14.strip_ref, bf16[1024,256]{1,0:T(8,128)(2,1)S(1)} %get-tuple-element.17.rows_ref, bf16[240,128]{1,0:T(8,128)(2,1)S(1)} %get-tuple-element.18.gram_ref, bf16[160,704]{1,0:T(8,128)(2,1)S(1)} %get-tuple-element.19.wide_ref, ...), custom_call_target="tpu_custom_call" | custom-call | flops 40960000 | bytes 1048576 | tf_op jit(solution)/shard_map/inner/pallas_call | solution.py:422
  27.2 2.2 %border.1 = bf16[512,128]{1,0:T(8,128)(2,1)} custom-call(f32[8,3584]{1,0:T(8,128)S(1)} %get-tuple-element.14.strip_ref, bf16[8,256]{1,0:T(8,128)(2,1)S(1)} %collective-permute-done.before_ref, bf16[8,256]{1,0:T(8,128)(2,1)S(1)} %collective-permute-done.1.after_ref, bf16[1024,256]{1,0:T(8,128)(2,1)S(1)} %get-tuple-element.17.rows_ref, ...), custom_call_target="tpu_custom_call" | custom-call | flops 12288000 | bytes 1048576 | tf_op jit(solution)/shard_map/border/pallas_call | solution.py:435
  29.5 11.8 %all-to-all-start.1 = ((bf16[64,8,128]{2,1,0:T(8,128)(2,1)}), bf16[64,8,128]{2,1,0:T(8,128)(2,1)S(1)}, u32[]{:S(2)}, u32[]{:S(2)}) async-start(bf16[64,8,128]{2,1,0:T(8,128)(2,1)} %bitcast), calls=%async_computation.1 | async-start | bytes 262144 | tf_op jit(solution)/shard_map/all_to_all | solution.py:449
  41.4 1.4 %copy-done.3 = bf16[704,1024]{1,0:T(8,128)(2,1)S(1)} copy-done((bf16[704,1024]{1,0:T(8,128)(2,1)S(1)}, bf16[704,1024]{1,0:T(8,128)(2,1)}, u32[]{:S(2)}) %copy-start.3) | copy-done | bytes 1441816
  42.7 1.0 %value_output.1.both_ref = bf16[512,1024]{1,0:T(8,128)(2,1)S(1)} custom-call(bf16[54,704]{1,0:T(8,128)(2,1)S(1)} %copy-done.6, f32[704]{0:T(1024)S(1)} %copy-done.8, bf16[704,1024]{1,0:T(8,128)(2,1)S(1)} %copy-done.3, bf16[1024,1024]{1,0:T(8,128)(2,1)S(1)} %copy-done), custom_call_target="tpu_custom_call" | custom-call | flops 24576000 | bytes 1048576 | tf_op jit(solution)/shard_map/value_output/pallas_call | solution.py:408
  43.7 0.7 %constant_dynamic-slice_fusion.own_ref = bf16[8,1024]{1,0:T(8,128)(2,1)S(1)} fusion(bf16[512,1024]{1,0:T(8,128)(2,1)} %lat_ref.1, s32[]{:T(128)S(6)} %select_n.3), kind=kLoop, calls=%fused_computation | loop fusion | bytes 32772 | tf_op jit(solution)/shard_map/dynamic_slice | solution.py:450
  44.5 6.4 %all-to-all-done.1 = bf16[64,8,128]{2,1,0:T(8,128)(2,1)S(1)} async-done(((bf16[64,8,128]{2,1,0:T(8,128)(2,1)}), bf16[64,8,128]{2,1,0:T(8,128)(2,1)S(1)}, u32[]{:S(2)}, u32[]{:S(2)}) %all-to-all-start.1) | async-done | bytes 131104 | tf_op jit(solution)/shard_map/all_to_all | solution.py:449
  50.9 1.1 %combine.1 = bf16[8,1024]{1,0:T(8,128)(2,1)} custom-call(bf16[512,128]{1,0:T(8,128)(2,1)S(1)} %bitcast.2, bf16[512,1024]{1,0:T(8,128)(2,1)S(1)} %value_output.1.both_ref, bf16[8,1024]{1,0:T(8,128)(2,1)S(1)} %constant_dynamic-slice_fusion.own_ref), custom_call_target="tpu_custom_call" | custom-call | flops 4096000 | bytes 1048576 | tf_op jit(solution)/shard_map/combine/pallas_call | solution.py:451
  (13 shorter events, 0.0 us)
Async XLA Ops:
  1.7 15.3 %all-to-all-start = ((bf16[4,8,896]{2,1,0:T(8,128)(2,1)}), bf16[4,8,896]{2,1,0:T(8,128)(2,1)S(1)}, u32[]{:S(2)}, u32[]{:S(2)}) async-start(bf16[4,8,896]{2,1,0:T(8,128)(2,1)} %pack.1), calls=%async_computation | async-start | bytes 114688 | tf_op jit(solution)/shard_map/all_to_all | solution.py:388
  7.7 1.6 %copy-start.1 = (bf16[1024,1024]{1,0:T(8,128)(2,1)S(1)}, bf16[1024,1024]{1,0:T(8,128)(2,1)}, u32[]{:S(2)}) copy-start(bf16[1024,1024]{1,0:T(8,128)(2,1)} %query_hbm.1) | copy-start | bytes 6291460
  9.3 1.4 %copy-start.2 = (bf16[704,1024]{1,0:T(8,128)(2,1)S(1)}, bf16[704,1024]{1,0:T(8,128)(2,1)}, u32[]{:S(2)}) copy-start(bf16[704,1024]{1,0:T(8,128)(2,1)} %key_hbm.1) | copy-start | bytes 4325380
  10.7 1.2 %copy-start.4 = (bf16[512,1024]{1,0:T(8,128)(2,1)S(1)}, bf16[512,1024]{1,0:T(8,128)(2,1)}, u32[]{:S(2)}) copy-start(bf16[512,1024]{1,0:T(8,128)(2,1)} %lat_ref.1) | copy-start | bytes 3145732
  11.9 0.9 %copy-start.5 = (bf16[54,704]{1,0:T(8,128)(2,1)S(1)}, bf16[54,704]{1,0:T(8,128)(2,1)}, u32[]{:S(2)}) copy-start(bf16[54,704]{1,0:T(8,128)(2,1)} %conv_ref.3) | copy-start | bytes 228100
  12.8 0.7 %copy-start.7 = (f32[704]{0:T(1024)S(1)}, f32[704]{0:T(1024)}, u32[]{:S(2)}) copy-start(f32[704]{0:T(1024)} %gain_ref.3) | copy-start | bytes 8452
  13.5 0.7 %copy-start.9 = (f32[1024]{0:T(1024)S(1)}, f32[1024]{0:T(1024)}, u32[]{:S(2)}) copy-start(f32[1024]{0:T(1024)} %lat_gain_ref.1) | copy-start | bytes 12292
  17.0 24.3 %copy-start = (bf16[1024,1024]{1,0:T(8,128)(2,1)S(1)}, bf16[1024,1024]{1,0:T(8,128)(2,1)}, u32[]{:S(2)}) copy-start(bf16[1024,1024]{1,0:T(8,128)(2,1)} %out_ref.1) | copy-start | bytes 6291460
  17.1 24.3 %copy-start.6 = (bf16[54,704]{1,0:T(8,128)(2,1)S(1)}, bf16[54,704]{1,0:T(8,128)(2,1)}, u32[]{:S(2)}) copy-start(bf16[54,704]{1,0:T(8,128)(2,1)} %conv_ref.3) | copy-start | bytes 228100
  17.1 24.3 %copy-start.8 = (f32[704]{0:T(1024)S(1)}, f32[704]{0:T(1024)}, u32[]{:S(2)}) copy-start(f32[704]{0:T(1024)} %gain_ref.3) | copy-start | bytes 8452
  17.2 10.0 %collective-permute-start = (bf16[8,256]{1,0:T(8,128)(2,1)S(1)}, bf16[8,256]{1,0:T(8,128)(2,1)S(1)}, u32[]{:S(2)}, u32[]{:S(2)}) collective-permute-start(bf16[8,256]{1,0:T(8,128)(2,1)S(1)} %get-tuple-element.15), channel_id=1, source_target_pairs={{0,4},{4,8},{8,12},{12,16},{16,20},{20,24},{24,28},{28,32},{32,36}... | collective-permute-start | bytes 12296 | tf_op jit(solution)/shard_map/ppermute | solution.py:418
  20.8 6.4 %collective-permute-start.1 = (bf16[8,256]{1,0:T(8,128)(2,1)S(1)}, bf16[8,256]{1,0:T(8,128)(2,1)S(1)}, u32[]{:S(2)}, u32[]{:S(2)}) collective-permute-start(bf16[8,256]{1,0:T(8,128)(2,1)S(1)} %get-tuple-element.16), channel_id=1, source_target_pairs={{4,0},{8,4},{12,8},{16,12},{20,16},{24,20},{28,24},{32,28},{36,32}... | collective-permute-start | bytes 12296 | tf_op jit(solution)/shard_map/ppermute | solution.py:419
  29.5 21.4 %all-to-all-start.1 = ((bf16[64,8,128]{2,1,0:T(8,128)(2,1)}), bf16[64,8,128]{2,1,0:T(8,128)(2,1)S(1)}, u32[]{:S(2)}, u32[]{:S(2)}) async-start(bf16[64,8,128]{2,1,0:T(8,128)(2,1)} %bitcast), calls=%async_computation.1 | async-start | bytes 262144 | tf_op jit(solution)/shard_map/all_to_all | solution.py:449
  41.4 1.4 %copy-start.3 = (bf16[704,1024]{1,0:T(8,128)(2,1)S(1)}, bf16[704,1024]{1,0:T(8,128)(2,1)}, u32[]{:S(2)}) copy-start(bf16[704,1024]{1,0:T(8,128)(2,1)} %value_ref.1) | copy-start | bytes 4325380

commit v4 on v3

--- a/solution.py
+++ b/solution.py
@@ -58,15 +58,18 @@
     return one, two, three
 
 
-def pack_kernel(pixel_ref, copies_ref):
-    rows, columns, channels = pixel_ref.shape
-    values = pixel_ref[...].astype(F32)
-    values = jnp.concatenate([values, jnp.zeros((rows, CELL - columns, channels), F32)], axis=1)
-    values = values.reshape(rows * CELL, channels).astype(BF16)
-    pick = jnp.where(iota((SUB, channels), 0) == iota((SUB, channels), 1), 1.0, 0.0).astype(BF16)
-    packed = nt(pick, values).astype(BF16)
-    for copy in range(copies_ref.shape[0]):
-        copies_ref[copy] = packed
+def pack_kernel(pixel_ref, copies_ref, plane_ref):
+    channels, rows, columns = pixel_ref.shape
+    pitch = plane_ref.shape[0] // SUB
+    plane_ref[...] = jnp.zeros(plane_ref.shape, F32)
+    for channel in range(channels):
+        plane_ref[channel * pitch : channel * pitch + rows, :columns] = pixel_ref[channel].astype(F32)
+    for pair in range(rows // 2):
+        even = plane_ref[pl.ds(2 * pair, SUB, stride=pitch), :]
+        odd = plane_ref[pl.ds(2 * pair + 1, SUB, stride=pitch), :]
+        packed = (even + pltpu.roll(odd, CELL, 1)).astype(BF16)
+        for copy in range(copies_ref.shape[0]):
+            copies_ref[copy, :, pair * LANES : (pair + 1) * LANES] = packed
 
 
 def join_kernel(columns, tiles_ref, strip_ref, first_ref, last_ref):
@@ -108,29 +111,32 @@
 
 
 def query_kernel(
-    lat_ref, lat_gain_ref, conv_ref, gain_ref, query_hbm, key_hbm, rows_ref, gram_ref, wide_ref, diag_ref, query_ref, key_ref, sems
+    conv_ref, gain_ref, lat_gain_ref, lat_hbm, query_hbm, key_hbm, rows_ref, lat_ref, query_ref, key_ref, sems
 ):
-    width = query_ref.shape[1]
-    at = pl.multiple_of(lax.axis_index("gy") * width, width)
-    query_copy = pltpu.make_async_copy(query_hbm.at[:, pl.ds(at, width)], query_ref, sems.at[0])
-    key_copy = pltpu.make_async_copy(key_hbm.at[:, pl.ds(at, width)], key_ref, sems.at[1])
+    lat_copy = pltpu.make_async_copy(lat_hbm.at[:, lax.axis_index("gy")], lat_ref, sems.at[0])
+    query_copy = pltpu.make_async_copy(query_hbm, query_ref, sems.at[1])
+    key_copy = pltpu.make_async_copy(key_hbm, key_ref, sems.at[2])
+    lat_copy.start()
     query_copy.start()
     key_copy.start()
 
-    weight = spread_weight(conv_ref, LINE)
+    weight = spread_weight(conv_ref, SPAN)
     feat = weight.shape[1]
-    high, low = split_up(weight[:SPAN])
-    wide_ref[...] = jnp.concatenate([high, low], axis=0)
+    high, low = split_up(weight)
     both = jnp.concatenate([high, low], axis=0)
+    held = HEADS * lat_ref.shape[0] * lat_ref.shape[1]
+    for part, at in enumerate(range(0, feat, LINE)):
+        end = min(at + LINE, feat)
+        first = held + LINE + part * 2 * SPAN
+        rows_ref[first : first + 2 * SPAN, : end - at] = both[:, at:end]
     padding = jnp.zeros((LANES - SPAN, feat), BF16)
     gram = nt(both, jnp.concatenate([high, padding], axis=0)) + nt(both, jnp.concatenate([low, padding], axis=0))
     gram = (gram[:SPAN] + gram[SPAN:]) * (1.0 / feat)
-    gram_ref[...] = jnp.concatenate(thrice(gram), axis=0)
-    shape = (SPAN, LANES)
-    diag = jnp.sum(jnp.where(iota(shape, 0) == iota(shape, 1), gram, 0.0), axis=-1, keepdims=True)
-    diag_ref[...] = jnp.broadcast_to(diag, shape)
-
+    rows_ref[held : held + 3 * SPAN, :LANES] = jnp.concatenate(thrice(gram), axis=0)
+
+    lat_copy.wait()
     values = lat_ref[...].astype(F32)
+    values = values.reshape(values.shape[0] * values.shape[1], values.shape[2])
     centred = values - jnp.mean(values, axis=-1, keepdims=True)
     variance = jnp.mean(centred * centred, axis=-1, keepdims=True)
     gain = lat_gain_ref[...].reshape(1, -1)
@@ -139,44 +145,54 @@
     queries = nn(normed, query_ref[...]).astype(BF16)
 
     key_copy.wait()
-    high, low = split_up(weight * gain_ref[...].reshape(1, -1))
-    keys = (nn(high, key_ref[...]) + nn(low, key_ref[...])) * (LOG2E / DH**0.5)
-    high, low = split_up(keys)
+    keys = nn(jnp.concatenate(split_up(weight * gain_ref[...].reshape(1, -1)), axis=0), key_ref[...])
+    high, low = split_up((keys[:SPAN] + keys[SPAN:]) * (LOG2E / DH**0.5))
     count = values.shape[0]
     lane = iota((count, LINE), 1)
-    for head in range(width // DH):
+    padding = jnp.zeros((LINE - 3 * SPAN, 2 * DH), BF16)
+    for head in range(HEADS):
         cut = slice(head * DH, (head + 1) * DH)
         query = jnp.concatenate([queries[:, cut], queries[:, cut]], axis=1)
-        rows = nt(query, jnp.concatenate([high[:, cut], low[:, cut]], axis=1))
+        key = jnp.concatenate([high[:, cut], low[:, cut]], axis=1)
+        rows = nt(query, jnp.concatenate([key, key, key, padding], axis=0))
         rows = jnp.where(lane == MASK, -1.0, rows)
         top, rest = split_up(rows)
         rows_ref[head * count : (head + 1) * count, :] = jnp.where((lane >= SPAN) & (lane < 2 * SPAN), rest, top)
 
 
-def scaled_patches(patches, explicit, gram_ref, wide_ref, diag_ref):
+def table_rows(feat):
+    return LINE + -(-feat // LINE) * 2 * SPAN
+
+
+def scaled_patches(patches, explicit, feat, rows_ref):
     exact = patches.astype(BF16)
+    held = rows_ref.shape[0] - table_rows(feat)
     if explicit:
-        high, low = wide_ref[:SPAN], wide_ref[SPAN:]
-        features = tn(high, exact) + tn(low, exact)
-        variance = jnp.mean(features * features, axis=0, keepdims=True)
+        total = 0.0
+        for part, at in enumerate(range(0, feat, LINE)):
+            end = min(at + LINE, feat)
+            first = held + LINE + part * 2 * SPAN
+            wide = rows_ref[first : first + 2 * SPAN, : end - at]
+            features = tn(wide[:SPAN], exact) + tn(wide[SPAN:], exact)
+            total = total + jnp.sum(features * features, axis=0, keepdims=True)
+        variance = total * (1.0 / feat)
         lost = None
     else:
-        form = nn(gram_ref[:, :SPAN], exact)
+        gram = rows_ref[held : held + 3 * SPAN, :LANES]
+        form = nn(gram[:, :SPAN], exact)
         form = form[:SPAN] + form[SPAN : 2 * SPAN] + form[2 * SPAN :]
         variance = jnp.maximum(jnp.sum(form * patches, axis=0, keepdims=True), 0.0)
-        scale = jnp.sum(patches * patches * diag_ref[:, :1], axis=0, keepdims=True)
+        shape = (SPAN, LANES)
+        diag = jnp.where(iota(shape, 0) == iota(shape, 1), gram[:SPAN].astype(F32), 0.0)
+        diag = jnp.sum(diag, axis=-1, keepdims=True)
+        scale = jnp.sum(patches * patches * diag, axis=0, keepdims=True)
         lost = jnp.where((variance + EPS) * 128.0 < scale, 1.0, 0.0)
     return patches * lax.rsqrt(variance + EPS), lost
 
 
-def pixel_block(cells, real):
-    del real
-    return jnp.concatenate(cells + [jnp.zeros_like(cells[0])], axis=0)
-
-
-def fill_block(patches, columns, explicit, gram_ref, wide_ref, diag_ref, pixel_ref, at):
+def fill_block(patches, columns, explicit, feat, rows_ref, pixel_ref, at):
     width = patches.shape[1]
-    scaled, lost = scaled_patches(patches, explicit, gram_ref, wide_ref, diag_ref)
+    scaled, lost = scaled_patches(patches, explicit, feat, rows_ref)
     row, lane = iota((SPAN, width), 0), iota((SPAN, width), 1)
     real = lane % LINE < columns
     scaled = jnp.where((row == ONE) | (row == ONE_TOO), jnp.where(real, 1.0, 0.0), scaled)
@@ -196,7 +212,7 @@
     for turn in range(count + 2):
         if turn < count:
             cut = slice(blocks[turn][0], blocks[turn][1])
-            score_ref[turn % 2, :, : cut.stop - cut.start] = nn(rows_ref[...], pixel_ref[:, cut])
+            score_ref[turn % 2, :, : cut.stop - cut.start] = nn(rows_ref[: score_ref.shape[1]], pixel_ref[:, cut])
         if 0 <= turn - 1 < count:
             block = turn - 1
             size = blocks[block][1] - blocks[block][0]
@@ -217,7 +233,7 @@
 
 
 def inner_kernel(
-    columns, size, strip_ref, rows_ref, gram_ref, wide_ref, diag_ref, sums_ref, tops_ref, pixel_ref, score_ref, expo_ref
+    columns, size, feat, strip_ref, rows_ref, sums_ref, tops_ref, pixel_ref, score_ref, expo_ref
 ):
     width = strip_ref.shape[1]
     inner = width - 2 * LINE
@@ -230,7 +246,7 @@
         for at, end in blocks:
             cells = [shifted[tap % 3][:, tap // 3 * LINE + at : tap // 3 * LINE + end] for tap in range(TAPS)]
             patches = jnp.concatenate(cells + [jnp.zeros_like(cells[0])], axis=0)
-            flags.append(fill_block(patches, columns, explicit, gram_ref, wide_ref, diag_ref, pixel_ref, at))
+            flags.append(fill_block(patches, columns, explicit, feat, rows_ref, pixel_ref, at))
         tops, sums = attend(blocks, rows_ref, pixel_ref, score_ref, expo_ref)
         top, total = merged(list(tops.values()), list(sums.values()))
         sums_ref[...] = total
@@ -246,13 +262,11 @@
 
 def border_kernel(
     columns,
+    feat,
     strip_ref,
     before_ref,
     after_ref,
     rows_ref,
-    gram_ref,
-    wide_ref,
-    diag_ref,
     inner_sums_ref,
     inner_tops_ref,
     sent_ref,
@@ -286,20 +300,26 @@
     place = jnp.where((target >= 0) & (lane == target + row // LANES * SLOT), 1.0, 0.0).astype(BF16)
 
     def run(explicit):
-        lost = fill_block(patches, columns, explicit, gram_ref, wide_ref, diag_ref, pixel_ref, 0)
+        lost = fill_block(patches, columns, explicit, feat, rows_ref, pixel_ref, 0)
         tops, sums = attend([(0, patches.shape[1])], rows_ref, pixel_ref, score_ref, expo_ref)
         top, total = merged([inner_tops_ref[...], tops[0]], [inner_sums_ref[...], sums[0]])
         high = total.astype(BF16)
         low = (total - high.astype(F32)).astype(BF16)
         high = jnp.where(iota(total.shape, 1) == ONE_TOO, low, high)
-        placed = nn(jnp.concatenate([high[:count], high[count:]], axis=1), place)
-        lane = iota((count, LANES), 1)
+
+        def side(values, odd):
+            heads = range(odd, HEADS, 2)
+            return jnp.concatenate([values[head * count : (head + 1) * count] for head in heads], axis=0)
+
+        placed = nn(jnp.concatenate([side(high, 0), side(high, 1)], axis=1), place)
+        lane = iota(placed.shape, 1)
         column = lane % SLOT
-        one, two, three = thrice(jnp.where(lane < SLOT, top[:count], top[count:]))
+        one, two, three = thrice(jnp.where(lane < SLOT, side(top, 0), side(top, 1)))
         placed = jnp.where(column == TOP, one.astype(F32), placed)
         placed = jnp.where(column == TOP + 1, two.astype(F32), placed)
-        placed = jnp.where(column == TOP + 2, three.astype(F32), placed)
-        sent_ref[...] = placed.astype(BF16)
+        placed = jnp.where(column == TOP + 2, three.astype(F32), placed).astype(BF16)
+        for pair in range(HEADS // 2):
+            sent_ref[:, pair * LANES : (pair + 1) * LANES] = placed[pair * count : (pair + 1) * count]
         return lost
 
     lost = jnp.max(run(False))
@@ -321,23 +341,22 @@
         both_ref[head * SLOT : (head + 1) * SLOT, :] = (both[:SLOT] + both[SLOT:]).astype(BF16)
 
 
-def combine_kernel(share, parts_ref, both_ref, own_ref, result_ref):
-    count = parts_ref.shape[0]
-    pairs = both_ref.shape[0] // LANES
+def combine_kernel(parts_ref, both_ref, own_ref, result_ref):
+    count, share, width = parts_ref.shape
     row, lane = iota((LANES, LANES), 0), iota((LANES, LANES), 1)
     same = row // SLOT == lane // SLOT
     column = row % SLOT
     pick_top = jnp.where(same & (column >= TOP) & (column < TOP + 3), 1.0, 0.0).astype(BF16)
     pick_one = jnp.where(same & (column >= TOTAL) & (column < TOTAL + 2), 1.0, 0.0).astype(BF16)
-    parts = parts_ref[...]
-    shape = (count // (pairs * share), pairs * share, LANES)
-    tops = nn(parts, pick_top).reshape(shape)
-    ones = nn(parts, pick_one).reshape(shape)
-    factor = jnp.exp2(tops - jnp.max(tops, axis=0, keepdims=True))
-    sums = jnp.sum(factor * parts.astype(F32).reshape(shape), axis=0)
-    total = jnp.sum(factor * ones, axis=0)
-    mean = sums / total
-    mean = jnp.concatenate([mean[pair * share : (pair + 1) * share] for pair in range(pairs)], axis=1)
+    means = []
+    for at in range(0, width, LANES):
+        values = parts_ref[:, :, at : at + LANES].astype(F32)
+        parts = values.reshape(count * share, LANES).astype(BF16)
+        tops = nn(parts, pick_top).reshape(values.shape)
+        ones = nn(parts, pick_one).reshape(values.shape)
+        factor = jnp.exp2(tops - jnp.max(tops, axis=0, keepdims=True))
+        means.append(jnp.sum(factor * values, axis=0) / jnp.sum(factor * ones, axis=0))
+    mean = jnp.concatenate(means, axis=1)
     high = mean.astype(BF16).astype(F32)
     result = nn(jnp.concatenate([high, mean - high], axis=0).astype(BF16), both_ref[...])
     result = own_ref[...].astype(F32) + (result[:share] + result[share:])
@@ -378,79 +397,80 @@
     columns = tile_cols * across
     feat = conv_weight.shape[1]
     lat, width = latents.shape
-    heads = HEADS // across
     share = lat // (across * down)
+    held = lat // across
 
     def shape(dims, dtype=BF16):
         return jax.ShapeDtypeStruct(dims, dtype)
 
-    copies = kernel(pack_kernel, "pack", shape((across, SUB, tile_rows * CELL)), count=1)(pixels)
+    copies = kernel(
+        pack_kernel,
+        "pack",
+        shape((across, SUB, tile_rows * CELL)),
+        [pltpu.VMEM((SUB * 16, LANES), F32)],
+        count=1,
+    )(pixels.transpose(2, 0, 1))
     tiles = lax.all_to_all(copies, "gy", 0, 0, tiled=True)
-    rows, gram, wide, diag = kernel(
+    rows = kernel(
         query_kernel,
         "query_rows",
+        shape((HEADS * held + table_rows(feat), LINE)),
         [
-            shape((heads * lat, LINE)),
-            shape((3 * SPAN, LANES)),
-            shape((2 * SPAN, feat)),
-            shape((SPAN, LANES), F32),
+            pltpu.VMEM((down, share, width), BF16),
+            pltpu.VMEM(query_weight.shape, BF16),
+            pltpu.VMEM(key_weight.shape, BF16),
+            pltpu.SemaphoreType.DMA((3,)),
         ],
-        [
-            pltpu.VMEM((width, heads * DH), BF16),
-            pltpu.VMEM((feat, heads * DH), BF16),
-            pltpu.SemaphoreType.DMA((2,)),
-        ],
-        others=2,
-        count=4,
+        others=3,
+        count=3,
         cycles=6000,
-        room=14,
-    )(latents, latent_gain, conv_weight, input_gain, query_weight, key_weight)
+        room=60,
+    )(conv_weight, input_gain, latent_gain, latents.reshape(down, across, share, width), query_weight, key_weight)
     both = kernel(
         output_kernel, "value_output", shape((HEADS * SLOT, width)), count=4, cycles=6000, room=10
     )(conv_weight, input_gain, value_weight, out_weight)
 
+    tiles, rows = lax.optimization_barrier((tiles, rows))
     strip, first, last = kernel(
         functools.partial(join_kernel, tile_cols),
         "join",
         [shape((SUB, tile_rows * LINE), F32), shape((SUB, LINE)), shape((SUB, LINE))],
         count=1,
+        cycles=200000,
     )(tiles)
     before = lax.ppermute(last, "gx", [(i, i + 1) for i in range(down - 1)])
     after = lax.ppermute(first, "gx", [(i + 1, i) for i in range(down - 1)])
     inner = (tile_rows - 2) * LINE
     size = inner // 3
     sums, tops = kernel(
-        functools.partial(inner_kernel, columns, size),
+        functools.partial(inner_kernel, columns, size, feat),
         "inner",
-        [shape((heads * lat, LANES), F32), shape((heads * lat, LANES), F32)],
+        [shape((HEADS * held, LANES), F32), shape((HEADS * held, LANES), F32)],
         [
             pltpu.VMEM((LINE, inner), BF16),
-            pltpu.VMEM((2, heads * lat, size), F32),
-            pltpu.VMEM((2, heads * lat, size), BF16),
+            pltpu.VMEM((2, HEADS * held, size), F32),
+            pltpu.VMEM((2, HEADS * held, size), BF16),
         ],
-        count=5,
+        count=2,
         cycles=10000,
         room=34,
-    )(strip, rows, gram, wide, diag)
+    )(strip, rows)
     sent = kernel(
-        functools.partial(border_kernel, columns),
+        functools.partial(border_kernel, columns, feat),
         "border",
-        shape((lat, heads * SLOT)),
+        shape((held, HEADS * SLOT)),
         [
             pltpu.VMEM((LINE, 2 * LINE), BF16),
-            pltpu.VMEM((2, heads * lat, 2 * LINE), F32),
-            pltpu.VMEM((2, heads * lat, 2 * LINE), BF16),
+            pltpu.VMEM((2, HEADS * held, 2 * LINE), F32),
+            pltpu.VMEM((2, HEADS * held, 2 * LINE), BF16),
         ],
-        count=9,
+        count=6,
         cycles=3000,
         room=16,
-    )(strip, before, after, rows, gram, wide, diag, sums, tops)
-    devices = across * down
-    parts = lax.all_to_all(sent.reshape(devices, share, -1), GROUP, 0, 0, tiled=True)
+    )(strip, before, after, rows, sums, tops)
+    parts = lax.all_to_all(sent.reshape(down, share, -1), "gx", 0, 0, tiled=True)
     own = lax.dynamic_slice_in_dim(latents, lax.axis_index(GROUP) * share, share, 0)
-    return kernel(
-        functools.partial(combine_kernel, share), "combine", shape((share, width)), count=3, room=6
-    )(parts.reshape(devices * share, -1), both, own)
+    return kernel(combine_kernel, "combine", shape((share, width)), count=3, room=6)(parts, both, own)
 
 
 def solution(mesh):

time: 52.9 us -> 42.4 us (0.80)
  local copies, waits for them, and re-layouts: 9.46 us -> 2.84 us
  starting transfers between devices: 22.7 us -> 19.1 us
  Pallas kernels: 13.2 us -> 15.1 us
  waiting for transfers between devices: 6.43 us -> 4.72 us
    unnamed x21 -> x12, local copies, waits for them, and re-layouts: 8.74 us -> 2.12 us
    all_to_all x1, starting transfers between devices: 11.8 us -> 8.1 us  [on_device(): lax.all_to_all(sent.reshape(down, share, -1), 'gx', 0, 0, tiled=True)]
    pallas_call x5, Pallas kernels: 12.1 us -> 14 us  [the longest x1 5.12 us: on_device(): kernel(functools.partial(inner_kernel, columns, size, feat), 'inner', [sh...]
    all_to_all x1, waiting for transfers between devices: 6.42 us -> 4.71 us  [on_device(): lax.all_to_all(sent.reshape(down, share, -1), 'gx', 0, 0, tiled=True)]
  transfers between devices with their start and end apart: 4 -> 4, of which waited for: 1 -> 1; matrix products, arithmetic and copies ran while one was open for 1% -> 2% of each run, Pallas kernels for 17% -> 26%
where the time goes in v4:
time: 42.4 us; the launch traced here: 42 us
  starting transfers between devices  19.1 us (45%)
  Pallas kernels  15.1 us (36%)
  waiting for transfers between devices  4.72 us (11%)
  local copies, waits for them, and re-layouts  2.84 us (7%)
    all_to_all x1, starting transfers between devices, on_device(): lax.all_to_all(sent.reshape(down, share, -1), 'gx', 0, 0, tiled=True)  8.1 us
    all_to_all x1, starting transfers between devices, on_device(): tiles = lax.all_to_all(copies, 'gy', 0, 0, tiled=True)  6 us
    pallas_call x1, Pallas kernels, on_device(): kernel(functools.partial(inner_kernel, columns, size, feat), 'inner', [sh...  5.12 us
    pallas_call x1, Pallas kernels, on_device(): kernel(query_kernel, 'query_rows', shape((HEADS * held + table_rows(feat)...  4.88 us
    all_to_all x1, waiting for transfers between devices, on_device(): lax.all_to_all(sent.reshape(down, share, -1), 'gx', 0, 0, tiled=True)  4.71 us
    ppermute x1, starting transfers between devices, on_device(): before = lax.ppermute(last, 'gx', [(i, i + 1) for i in range(down - 1)])  3.74 us
    pallas_call x1, Pallas kernels, on_device(): kernel(functools.partial(border_kernel, columns, feat), 'border', shape((...  2.24 us
    unnamed x12, local copies, waits for them, and re-layouts  2.12 us
  transfers between devices with their start and end apart: 4, of which 1 were waited for; matrix products, arithmetic and copies ran while one was open for 2% of the time, Pallas kernels for 26%

profile of v4, /device:TPU:32, one launch (start us, length us, event | category | flops | bytes accessed | tf_op | source)
XLA Modules:
  0.0 42.0 jit_solution(4708330875655785270)
XLA Ops:
  0.0 0.7 %copy-done.4 = bf16[14,56,6]{1,0,2:T(8,128)(2,1)S(1)} copy-done((bf16[14,56,6]{1,0,2:T(8,128)(2,1)S(1)}, bf16[14,56,6]{1,0,2:T(8,128)(2,1)}, u32[]{:S(2)}) %copy-start.4) | copy-done | bytes 9432
  0.7 0.7 %pack.1 = bf16[4,8,896]{2,1,0:T(8,128)(2,1)} custom-call(bf16[6,14,56]{2,1,0:T(8,128)(2,1)S(1)} %bitcast.3), custom_call_target="tpu_custom_call" | custom-call | flops 4096000 | bytes 1048576 | tf_op jit(solution)/shard_map/pack/pallas_call | solution.py:406
  1.4 6.0 %all-to-all-start = ((bf16[4,8,896]{2,1,0:T(8,128)(2,1)}), bf16[4,8,896]{2,1,0:T(8,128)(2,1)S(1)}, u32[]{:S(2)}, u32[]{:S(2)}) async-start(bf16[4,8,896]{2,1,0:T(8,128)(2,1)} %pack.1), calls=%async_computation | async-start | bytes 114688 | tf_op jit(solution)/shard_map/all_to_all | solution.py:413
  7.4 4.9 %query_rows.1.rows_ref = bf16[1760,256]{1,0:T(8,128)(2,1)} custom-call(bf16[54,704]{1,0:T(8,128)(2,1)} %conv_ref.3, f32[704]{0:T(1024)} %gain_ref.3, f32[1024]{0:T(1024)} %lat_gain_ref.1, bf16[16,4,8,1024]{3,2,1,0:T(8,128)(2,1)} %bitcast.4, bf16[1024,1024]{1,0:T(8,128)(2,1)} %query_hbm.1, bf16[704,1024]{1,0:T(8,128)(2,1)} %key_hbm.1), custom_call_target="tpu_custom_call" | custom-call | flops 24576000 | bytes 1048576 | tf_op jit(solution)/shard_map/query_rows/pallas_call | solution.py:414
  12.3 0.0 copy-start
  12.3 0.0 all-to-all-done.tiles_ref
  12.4 0.1 join.1
  12.5 0.0 copy-start.1
  12.5 0.0 copy-start.3
  12.5 0.0 copy-start.5
  12.5 3.7 %collective-permute-start = (bf16[8,256]{1,0:T(8,128)(2,1)S(1)}, bf16[8,256]{1,0:T(8,128)(2,1)S(1)}, u32[]{:S(2)}, u32[]{:S(2)}) collective-permute-start(bf16[8,256]{1,0:T(8,128)(2,1)S(1)} %get-tuple-element.14), channel_id=1, source_target_pairs={{0,4},{4,8},{8,12},{12,16},{16,20},{20,24},{24,28},{28,32},{32,36}... | collective-permute-start | bytes 12296 | tf_op jit(solution)/shard_map/ppermute | solution.py:441
  16.2 1.3 %collective-permute-start.1 = (bf16[8,256]{1,0:T(8,128)(2,1)S(1)}, bf16[8,256]{1,0:T(8,128)(2,1)S(1)}, u32[]{:S(2)}, u32[]{:S(2)}) collective-permute-start(bf16[8,256]{1,0:T(8,128)(2,1)S(1)} %get-tuple-element.15), channel_id=1, source_target_pairs={{4,0},{8,4},{12,8},{16,12},{20,16},{24,20},{28,24},{32,28},{36,32}... | collective-permute-start | bytes 12296 | tf_op jit(solution)/shard_map/ppermute | solution.py:442
  17.5 0.0 copy-done
  17.6 5.1 %inner.1 = (f32[1024,128]{1,0:T(8,128)S(1)}, f32[1024,128]{1,0:T(8,128)S(1)}) custom-call(f32[8,3584]{1,0:T(8,128)S(1)} %get-tuple-element.13.strip_ref, bf16[1760,256]{1,0:T(8,128)(2,1)S(1)} %copy-done), custom_call_target="tpu_custom_call" | custom-call | flops 40960000 | bytes 1048576 | tf_op jit(solution)/shard_map/inner/pallas_call | solution.py:445
  22.7 0.0 collective-permute-done.before_ref
  22.7 0.0 collective-permute-done.1.after_ref
  22.7 2.2 %border.1 = bf16[128,512]{1,0:T(8,128)(2,1)} custom-call(f32[8,3584]{1,0:T(8,128)S(1)} %get-tuple-element.13.strip_ref, bf16[8,256]{1,0:T(8,128)(2,1)S(1)} %collective-permute-done.before_ref, bf16[8,256]{1,0:T(8,128)(2,1)S(1)} %collective-permute-done.1.after_ref, bf16[1760,256]{1,0:T(8,128)(2,1)S(1)} %copy-done, ...), custom_call_target="tpu_custom_call" | custom-call | flops 12288000 | bytes 1048576 | tf_op jit(solution)/shard_map/border/pallas_call | solution.py:458
  25.0 8.1 %all-to-all-start.1 = ((bf16[16,8,512]{2,1,0:T(8,128)(2,1)}), bf16[16,8,512]{2,1,0:T(8,128)(2,1)S(1)}, u32[]{:S(2)}, u32[]{:S(2)}) async-start(bf16[16,8,512]{2,1,0:T(8,128)(2,1)} %bitcast.2), calls=%async_computation.1 | async-start | bytes 262144 | tf_op jit(solution)/shard_map/all_to_all | solution.py:471
  33.1 0.0 copy-start.2
  33.1 1.4 %copy-done.2 = bf16[704,1024]{1,0:T(8,128)(2,1)S(1)} copy-done((bf16[704,1024]{1,0:T(8,128)(2,1)S(1)}, bf16[704,1024]{1,0:T(8,128)(2,1)}, u32[]{:S(2)}) %copy-start.2) | copy-done | bytes 1441816
  34.5 1.0 %value_output.1.both_ref = bf16[512,1024]{1,0:T(8,128)(2,1)S(1)} custom-call(bf16[54,704]{1,0:T(8,128)(2,1)S(1)} %copy-done.3, f32[704]{0:T(1024)S(1)} %copy-done.5, bf16[704,1024]{1,0:T(8,128)(2,1)S(1)} %copy-done.2, bf16[1024,1024]{1,0:T(8,128)(2,1)S(1)} %copy-done.1), custom_call_target="tpu_custom_call" | custom-call | flops 24576000 | bytes 1048576 | tf_op jit(solution)/shard_map/value_output/pallas_call | solution.py:429
  35.5 0.7 %constant_dynamic-slice_fusion.own_ref = bf16[8,1024]{1,0:T(8,128)(2,1)S(1)} fusion(bf16[512,1024]{1,0:T(8,128)(2,1)} %param.14, s32[]{:T(128)S(6)} %select_n.3), kind=kLoop, calls=%fused_computation | loop fusion | bytes 32772 | tf_op jit(solution)/shard_map/dynamic_slice | solution.py:472
  36.2 4.7 %all-to-all-done.1.parts_ref = bf16[16,8,512]{2,1,0:T(8,128)(2,1)S(1)} async-done(((bf16[16,8,512]{2,1,0:T(8,128)(2,1)}), bf16[16,8,512]{2,1,0:T(8,128)(2,1)S(1)}, u32[]{:S(2)}, u32[]{:S(2)}) %all-to-all-start.1) | async-done | bytes 131104 | tf_op jit(solution)/shard_map/all_to_all | solution.py:471
  40.9 1.1 %combine.1 = bf16[8,1024]{1,0:T(8,128)(2,1)} custom-call(bf16[16,8,512]{2,1,0:T(8,128)(2,1)S(1)} %all-to-all-done.1.parts_ref, bf16[512,1024]{1,0:T(8,128)(2,1)S(1)} %value_output.1.both_ref, bf16[8,1024]{1,0:T(8,128)(2,1)S(1)} %constant_dynamic-slice_fusion.own_ref), custom_call_target="tpu_custom_call" | custom-call | flops 4096000 | bytes 1048576 | tf_op jit(solution)/shard_map/combine/pallas_call | solution.py:473
  (4 shorter events, 0.0 us)
Async XLA Ops:
  0.0 0.7 %copy-start.4 = (bf16[14,56,6]{1,0,2:T(8,128)(2,1)S(1)}, bf16[14,56,6]{1,0,2:T(8,128)(2,1)}, u32[]{:S(2)}) copy-start(bf16[14,56,6]{1,0,2:T(8,128)(2,1)} %param.9) | copy-start | bytes 28228
  1.4 10.9 %all-to-all-start = ((bf16[4,8,896]{2,1,0:T(8,128)(2,1)}), bf16[4,8,896]{2,1,0:T(8,128)(2,1)S(1)}, u32[]{:S(2)}, u32[]{:S(2)}) async-start(bf16[4,8,896]{2,1,0:T(8,128)(2,1)} %pack.1), calls=%async_computation | async-start | bytes 114688 | tf_op jit(solution)/shard_map/all_to_all | solution.py:413
  12.3 5.2 %copy-start = (bf16[1760,256]{1,0:T(8,128)(2,1)S(1)}, bf16[1760,256]{1,0:T(8,128)(2,1)}, u32[]{:S(2)}) copy-start(bf16[1760,256]{1,0:T(8,128)(2,1)} %query_rows.1.rows_ref) | copy-start | bytes 2703364
  12.5 20.6 %copy-start.1 = (bf16[1024,1024]{1,0:T(8,128)(2,1)S(1)}, bf16[1024,1024]{1,0:T(8,128)(2,1)}, u32[]{:S(2)}) copy-start(bf16[1024,1024]{1,0:T(8,128)(2,1)} %out_ref.1) | copy-start | bytes 6291460
  12.5 20.6 %copy-start.3 = (bf16[54,704]{1,0:T(8,128)(2,1)S(1)}, bf16[54,704]{1,0:T(8,128)(2,1)}, u32[]{:S(2)}) copy-start(bf16[54,704]{1,0:T(8,128)(2,1)} %conv_ref.3) | copy-start | bytes 228100
  12.5 20.6 %copy-start.5 = (f32[704]{0:T(1024)S(1)}, f32[704]{0:T(1024)}, u32[]{:S(2)}) copy-start(f32[704]{0:T(1024)} %gain_ref.3) | copy-start | bytes 8452
  12.5 10.2 %collective-permute-start = (bf16[8,256]{1,0:T(8,128)(2,1)S(1)}, bf16[8,256]{1,0:T(8,128)(2,1)S(1)}, u32[]{:S(2)}, u32[]{:S(2)}) collective-permute-start(bf16[8,256]{1,0:T(8,128)(2,1)S(1)} %get-tuple-element.14), channel_id=1, source_target_pairs={{0,4},{4,8},{8,12},{12,16},{16,20},{20,24},{24,28},{28,32},{32,36}... | collective-permute-start | bytes 12296 | tf_op jit(solution)/shard_map/ppermute | solution.py:441
  16.2 6.5 %collective-permute-start.1 = (bf16[8,256]{1,0:T(8,128)(2,1)S(1)}, bf16[8,256]{1,0:T(8,128)(2,1)S(1)}, u32[]{:S(2)}, u32[]{:S(2)}) collective-permute-start(bf16[8,256]{1,0:T(8,128)(2,1)S(1)} %get-tuple-element.15), channel_id=1, source_target_pairs={{4,0},{8,4},{12,8},{16,12},{20,16},{24,20},{28,24},{32,28},{36,32}... | collective-permute-start | bytes 12296 | tf_op jit(solution)/shard_map/ppermute | solution.py:442
  25.0 16.0 %all-to-all-start.1 = ((bf16[16,8,512]{2,1,0:T(8,128)(2,1)}), bf16[16,8,512]{2,1,0:T(8,128)(2,1)S(1)}, u32[]{:S(2)}, u32[]{:S(2)}) async-start(bf16[16,8,512]{2,1,0:T(8,128)(2,1)} %bitcast.2), calls=%async_computation.1 | async-start | bytes 262144 | tf_op jit(solution)/shard_map/all_to_all | solution.py:471
  33.1 1.4 %copy-start.2 = (bf16[704,1024]{1,0:T(8,128)(2,1)S(1)}, bf16[704,1024]{1,0:T(8,128)(2,1)}, u32[]{:S(2)}) copy-start(bf16[704,1024]{1,0:T(8,128)(2,1)} %value_ref.1) | copy-start | bytes 4325380

commit v5 on v4

--- a/solution.py
+++ b/solution.py
@@ -72,7 +72,7 @@
             copies_ref[copy, :, pair * LANES : (pair + 1) * LANES] = packed
 
 
-def join_kernel(columns, tiles_ref, strip_ref, first_ref, last_ref):
+def join_kernel(columns, tiles_ref, strip_ref, last_ref):
     tiles, _, width = tiles_ref.shape
     pairs = width // LANES
     lane = iota((pairs * SUB, LANES), 1)
@@ -96,8 +96,7 @@
             for half, line in enumerate(halves):
                 at = row * LINE + half * LANES
                 strip_ref[:, at : at + LANES] = line[pair * SUB : (pair + 1) * SUB]
-    first_ref[...] = strip_ref[:, :LINE].astype(BF16)
-    last_ref[...] = strip_ref[:, 2 * pairs * LINE - LINE :].astype(BF16)
+    last_ref[...] = strip_ref[:, 2 * pairs * LINE - 2 * LINE :].astype(BF16)
 
 
 def spread_weight(conv_ref, copies):
@@ -190,11 +189,10 @@
     return patches * lax.rsqrt(variance + EPS), lost
 
 
-def fill_block(patches, columns, explicit, feat, rows_ref, pixel_ref, at):
+def fill_block(patches, real, explicit, feat, rows_ref, pixel_ref, at):
     width = patches.shape[1]
     scaled, lost = scaled_patches(patches, explicit, feat, rows_ref)
-    row, lane = iota((SPAN, width), 0), iota((SPAN, width), 1)
-    real = lane % LINE < columns
+    row = iota((SPAN, width), 0)
     scaled = jnp.where((row == ONE) | (row == ONE_TOO), jnp.where(real, 1.0, 0.0), scaled)
     scaled = jnp.where(row == MASK, jnp.where(real, 0.0, BIG), scaled)
     high, low = split_up(scaled)
@@ -207,22 +205,22 @@
 
 
 def attend(blocks, rows_ref, pixel_ref, score_ref, expo_ref):
-    tops, sums = {}, {}
+    tops, sums = [], []
     count = len(blocks)
     for turn in range(count + 2):
         if turn < count:
-            cut = slice(blocks[turn][0], blocks[turn][1])
-            score_ref[turn % 2, :, : cut.stop - cut.start] = nn(rows_ref[: score_ref.shape[1]], pixel_ref[:, cut])
+            rows, cut = blocks[turn]
+            score_ref[turn % 2, rows, : cut.stop - cut.start] = nn(rows_ref[rows], pixel_ref[:, cut])
         if 0 <= turn - 1 < count:
-            block = turn - 1
-            size = blocks[block][1] - blocks[block][0]
-            top = jnp.max(score_ref[block % 2, :, :size], axis=-1, keepdims=True)
-            expo_ref[block % 2, :, :size] = jnp.exp2(score_ref[block % 2, :, :size] - top).astype(BF16)
-            tops[block] = top
+            rows, cut = blocks[turn - 1]
+            at = ((turn - 1) % 2, rows, slice(0, cut.stop - cut.start))
+            top = jnp.max(score_ref[at], axis=-1, keepdims=True)
+            expo_ref[at] = jnp.exp2(score_ref[at] - top).astype(BF16)
+            tops.append(top)
         if 0 <= turn - 2 < count:
-            block = turn - 2
-            cut = slice(blocks[block][0], blocks[block][1])
-            sums[block] = nt(expo_ref[block % 2, :, : cut.stop - cut.start], pixel_ref[:LANES, cut])
+            rows, cut = blocks[turn - 2]
+            at = ((turn - 2) % 2, rows, slice(0, cut.stop - cut.start))
+            sums.append(nt(expo_ref[at], pixel_ref[:LANES, cut]))
     return tops, sums
 
 
@@ -239,16 +237,19 @@
     inner = width - 2 * LINE
     strip = strip_ref[...]
     shifted = [pltpu.roll(strip, 1, 1), strip, pltpu.roll(strip, width - 1, 1)]
-    blocks = [(at, at + size) for at in range(0, inner, size)]
+    count = sums_ref.shape[0]
+    blocks = [(slice(0, count), slice(at, at + size)) for at in range(0, inner, size)]
 
     def run(explicit):
         flags = []
-        for at, end in blocks:
+        for at in range(0, inner, size):
+            end = at + size
             cells = [shifted[tap % 3][:, tap // 3 * LINE + at : tap // 3 * LINE + end] for tap in range(TAPS)]
             patches = jnp.concatenate(cells + [jnp.zeros_like(cells[0])], axis=0)
-            flags.append(fill_block(patches, columns, explicit, feat, rows_ref, pixel_ref, at))
+            real = iota(patches.shape, 1) % LINE < columns
+            flags.append(fill_block(patches, real, explicit, feat, rows_ref, pixel_ref, at))
         tops, sums = attend(blocks, rows_ref, pixel_ref, score_ref, expo_ref)
-        top, total = merged(list(tops.values()), list(sums.values()))
+        top, total = merged(tops, sums)
         sums_ref[...] = total
         tops_ref[...] = jnp.broadcast_to(top, tops_ref.shape)
         return flags
@@ -265,7 +266,6 @@
     feat,
     strip_ref,
     before_ref,
-    after_ref,
     rows_ref,
     inner_sums_ref,
     inner_tops_ref,
@@ -280,7 +280,7 @@
             before_ref[...].astype(F32),
             strip_ref[:, : 2 * LINE],
             strip_ref[:, width - 2 * LINE :],
-            after_ref[...].astype(F32),
+            jnp.zeros((SUB, LINE), F32),
         ],
         axis=1,
     )
@@ -289,9 +289,17 @@
     for tap in range(TAPS):
         at = tap // 3 * LINE
         source = shifted[tap % 3]
-        cells.append(jnp.concatenate([source[:, at : at + LINE], source[:, at + 3 * LINE : at + 4 * LINE]], axis=1))
+        cells.append(jnp.concatenate([source[:, at : at + 2 * LINE], source[:, at + 4 * LINE : at + 5 * LINE]], axis=1))
     patches = jnp.concatenate(cells + [jnp.zeros_like(cells[0])], axis=0)
+    lane = iota(patches.shape, 1)
+    place = lax.axis_index("gx")
+    above = (place > 0).astype(jnp.int32)
+    final = (place == lax.axis_size("gx") - 1).astype(jnp.int32)
+    shown = jnp.where(lane < LINE, above, jnp.where(lane < 2 * LINE, 1, final))
+    real = (lane % LINE < columns) & (shown > 0)
     count = sent_ref.shape[0]
+    half = score_ref.shape[1] // 2
+    blocks = [(slice(at, at + half), slice(0, patches.shape[1])) for at in (0, half)]
     shape = (2 * LANES, LANES)
     row, lane = iota(shape, 0), iota(shape, 1)
     tap = row % LANES
@@ -300,9 +308,10 @@
     place = jnp.where((target >= 0) & (lane == target + row // LANES * SLOT), 1.0, 0.0).astype(BF16)
 
     def run(explicit):
-        lost = fill_block(patches, columns, explicit, feat, rows_ref, pixel_ref, 0)
-        tops, sums = attend([(0, patches.shape[1])], rows_ref, pixel_ref, score_ref, expo_ref)
-        top, total = merged([inner_tops_ref[...], tops[0]], [inner_sums_ref[...], sums[0]])
+        lost = fill_block(patches, real, explicit, feat, rows_ref, pixel_ref, 0)
+        tops, sums = attend(blocks, rows_ref, pixel_ref, score_ref, expo_ref)
+        tops, sums = jnp.concatenate(tops, axis=0), jnp.concatenate(sums, axis=0)
+        top, total = merged([inner_tops_ref[...], tops], [inner_sums_ref[...], sums])
         high = total.astype(BF16)
         low = (total - high.astype(F32)).astype(BF16)
         high = jnp.where(iota(total.shape, 1) == ONE_TOO, low, high)
@@ -431,15 +440,14 @@
     )(conv_weight, input_gain, value_weight, out_weight)
 
     tiles, rows = lax.optimization_barrier((tiles, rows))
-    strip, first, last = kernel(
+    strip, last = kernel(
         functools.partial(join_kernel, tile_cols),
         "join",
-        [shape((SUB, tile_rows * LINE), F32), shape((SUB, LINE)), shape((SUB, LINE))],
+        [shape((SUB, tile_rows * LINE), F32), shape((SUB, 2 * LINE))],
         count=1,
         cycles=200000,
     )(tiles)
     before = lax.ppermute(last, "gx", [(i, i + 1) for i in range(down - 1)])
-    after = lax.ppermute(first, "gx", [(i + 1, i) for i in range(down - 1)])
     inner = (tile_rows - 2) * LINE
     size = inner // 3
     sums, tops = kernel(
@@ -460,14 +468,14 @@
         "border",
         shape((held, HEADS * SLOT)),
         [
-            pltpu.VMEM((LINE, 2 * LINE), BF16),
-            pltpu.VMEM((2, HEADS * held, 2 * LINE), F32),
-            pltpu.VMEM((2, HEADS * held, 2 * LINE), BF16),
+            pltpu.VMEM((LINE, 3 * LINE), BF16),
+            pltpu.VMEM((2, HEADS * held, 3 * LINE), F32),
+            pltpu.VMEM((2, HEADS * held, 3 * LINE), BF16),
         ],
-        count=6,
+        count=5,
         cycles=3000,
-        room=16,
-    )(strip, before, after, rows, sums, tops)
+        room=24,
+    )(strip, before, rows, sums, tops)
     parts = lax.all_to_all(sent.reshape(down, share, -1), "gx", 0, 0, tiled=True)
     own = lax.dynamic_slice_in_dim(latents, lax.axis_index(GROUP) * share, share, 0)
     return kernel(combine_kernel, "combine", shape((share, width)), count=3, room=6)(parts, both, own)

time: 42.4 us -> 39.9 us (0.941)
  starting transfers between devices: 19.1 us -> 16.5 us
    all_to_all x1, starting transfers between devices: 8.1 us -> 6.75 us  [on_device(): lax.all_to_all(sent.reshape(down, share, -1), 'gx', 0, 0, tiled=True)]
    ppermute x1 -> x0, starting transfers between devices: 1.29 us -> none  [on_device(): after = lax.ppermute(first, 'gx', [(i + 1, i) for i in range(down - 1)])]
  transfers between devices with their start and end apart: 4 -> 3, of which waited for: 1 -> 1; matrix products, arithmetic and copies ran while one was open for 2% -> 2% of each run, Pallas kernels for 26% -> 28%
where the time goes in v5:
time: 39.9 us; the launch traced here: 39.4 us
  starting transfers between devices  16.5 us (41%)
  Pallas kernels  15.2 us (38%)
  waiting for transfers between devices  4.72 us (12%)
  local copies, waits for them, and re-layouts  2.84 us (7%)
    all_to_all x1, starting transfers between devices, on_device(): lax.all_to_all(sent.reshape(down, share, -1), 'gx', 0, 0, tiled=True)  6.75 us
    all_to_all x1, starting transfers between devices, on_device(): tiles = lax.all_to_all(copies, 'gy', 0, 0, tiled=True)  6 us
    pallas_call x1, Pallas kernels, on_device(): kernel(functools.partial(inner_kernel, columns, size, feat), 'inner', [sh...  5.12 us
    pallas_call x1, Pallas kernels, on_device(): kernel(query_kernel, 'query_rows', shape((HEADS * held + table_rows(feat)...  4.88 us
    all_to_all x1, waiting for transfers between devices, on_device(): lax.all_to_all(sent.reshape(down, share, -1), 'gx', 0, 0, tiled=True)  4.71 us
    ppermute x1, starting transfers between devices, on_device(): before = lax.ppermute(last, 'gx', [(i, i + 1) for i in range(down - 1)])  3.74 us
    pallas_call x1, Pallas kernels, on_device(): kernel(functools.partial(border_kernel, columns, feat), 'border', shape((...  2.36 us
    unnamed x12, local copies, waits for them, and re-layouts  2.12 us
  transfers between devices with their start and end apart: 3, of which 1 were waited for; matrix products, arithmetic and copies ran while one was open for 2% of the time, Pallas kernels for 28%

profile of v5, /device:TPU:32, one launch (start us, length us, event | category | flops | bytes accessed | tf_op | source)
XLA Modules:
  0.0 39.4 jit_solution(8313580094961497585)
XLA Ops:
  0.0 0.7 %copy-done.4 = bf16[14,56,6]{1,0,2:T(8,128)(2,1)S(1)} copy-done((bf16[14,56,6]{1,0,2:T(8,128)(2,1)S(1)}, bf16[14,56,6]{1,0,2:T(8,128)(2,1)}, u32[]{:S(2)}) %copy-start.4) | copy-done | bytes 9432
  0.7 0.7 %pack.1 = bf16[4,8,896]{2,1,0:T(8,128)(2,1)} custom-call(bf16[6,14,56]{2,1,0:T(8,128)(2,1)S(1)} %bitcast.3), custom_call_target="tpu_custom_call" | custom-call | flops 4096000 | bytes 1048576 | tf_op jit(solution)/shard_map/pack/pallas_call | solution.py:415
  1.4 6.0 %all-to-all-start = ((bf16[4,8,896]{2,1,0:T(8,128)(2,1)}), bf16[4,8,896]{2,1,0:T(8,128)(2,1)S(1)}, u32[]{:S(2)}, u32[]{:S(2)}) async-start(bf16[4,8,896]{2,1,0:T(8,128)(2,1)} %pack.1), calls=%async_computation | async-start | bytes 114688 | tf_op jit(solution)/shard_map/all_to_all | solution.py:422
  7.4 4.9 %query_rows.1.rows_ref = bf16[1760,256]{1,0:T(8,128)(2,1)} custom-call(bf16[54,704]{1,0:T(8,128)(2,1)} %conv_ref.3, f32[704]{0:T(1024)} %gain_ref.3, f32[1024]{0:T(1024)} %lat_gain_ref.1, bf16[16,4,8,1024]{3,2,1,0:T(8,128)(2,1)} %bitcast.4, bf16[1024,1024]{1,0:T(8,128)(2,1)} %query_hbm.1, bf16[704,1024]{1,0:T(8,128)(2,1)} %key_hbm.1), custom_call_target="tpu_custom_call" | custom-call | flops 24576000 | bytes 1048576 | tf_op jit(solution)/shard_map/query_rows/pallas_call | solution.py:423
  12.3 0.0 copy-start
  12.3 0.0 all-to-all-done.tiles_ref
  12.4 0.1 join.1
  12.5 0.0 copy-start.1
  12.5 0.0 copy-start.3
  12.5 0.0 copy-start.5
  12.5 3.7 %collective-permute-start = (bf16[8,512]{1,0:T(8,128)(2,1)S(1)}, bf16[8,512]{1,0:T(8,128)(2,1)S(1)}, u32[]{:S(2)}, u32[]{:S(2)}) collective-permute-start(bf16[8,512]{1,0:T(8,128)(2,1)S(1)} %get-tuple-element.13), channel_id=1, source_target_pairs={{0,4},{4,8},{8,12},{12,16},{16,20},{20,24},{24,28},{28,32},{32,36}... | collective-permute-start | bytes 24584 | tf_op jit(solution)/shard_map/ppermute | solution.py:450
  16.2 0.0 copy-done
  16.3 5.1 %inner.1 = (f32[1024,128]{1,0:T(8,128)S(1)}, f32[1024,128]{1,0:T(8,128)S(1)}) custom-call(f32[8,3584]{1,0:T(8,128)S(1)} %get-tuple-element.12.strip_ref, bf16[1760,256]{1,0:T(8,128)(2,1)S(1)} %copy-done), custom_call_target="tpu_custom_call" | custom-call | flops 40960000 | bytes 1048576 | tf_op jit(solution)/shard_map/inner/pallas_call | solution.py:453
  21.4 0.0 collective-permute-done.before_ref
  21.4 2.4 %border.1 = bf16[128,512]{1,0:T(8,128)(2,1)} custom-call(f32[8,3584]{1,0:T(8,128)S(1)} %get-tuple-element.12.strip_ref, bf16[8,512]{1,0:T(8,128)(2,1)S(1)} %collective-permute-done.before_ref, bf16[1760,256]{1,0:T(8,128)(2,1)S(1)} %copy-done, f32[1024,128]{1,0:T(8,128)S(1)} %get-tuple-element.15.inner_sums_ref, f32[1024,128]{1,0:T(8,128)S(1)} %get-tuple-element.16.inner_tops_ref), custom_call_target="tpu_custom_call" | custom-call | flops 12288000 | bytes 1048576 | tf_op jit(solution)/shard_map/border/pallas_call | solution.py:466
  23.8 6.8 %all-to-all-start.1 = ((bf16[16,8,512]{2,1,0:T(8,128)(2,1)}), bf16[16,8,512]{2,1,0:T(8,128)(2,1)S(1)}, u32[]{:S(2)}, u32[]{:S(2)}) async-start(bf16[16,8,512]{2,1,0:T(8,128)(2,1)} %bitcast.2), calls=%async_computation.1 | async-start | bytes 262144 | tf_op jit(solution)/shard_map/all_to_all | solution.py:479
  30.5 0.0 copy-done.1
  30.5 0.0 copy-done.3
  30.6 0.0 copy-start.2
  30.6 1.4 %copy-done.2 = bf16[704,1024]{1,0:T(8,128)(2,1)S(1)} copy-done((bf16[704,1024]{1,0:T(8,128)(2,1)S(1)}, bf16[704,1024]{1,0:T(8,128)(2,1)}, u32[]{:S(2)}) %copy-start.2) | copy-done | bytes 1441816
  31.9 1.0 %value_output.1.both_ref = bf16[512,1024]{1,0:T(8,128)(2,1)S(1)} custom-call(bf16[54,704]{1,0:T(8,128)(2,1)S(1)} %copy-done.3, f32[704]{0:T(1024)S(1)} %copy-done.5, bf16[704,1024]{1,0:T(8,128)(2,1)S(1)} %copy-done.2, bf16[1024,1024]{1,0:T(8,128)(2,1)S(1)} %copy-done.1), custom_call_target="tpu_custom_call" | custom-call | flops 24576000 | bytes 1048576 | tf_op jit(solution)/shard_map/value_output/pallas_call | solution.py:438
  32.9 0.7 %constant_dynamic-slice_fusion.own_ref = bf16[8,1024]{1,0:T(8,128)(2,1)S(1)} fusion(bf16[512,1024]{1,0:T(8,128)(2,1)} %param.14, s32[]{:T(128)S(6)} %select_n.3), kind=kLoop, calls=%fused_computation | loop fusion | bytes 32772 | tf_op jit(solution)/shard_map/dynamic_slice | solution.py:480
  33.6 4.7 %all-to-all-done.1.parts_ref = bf16[16,8,512]{2,1,0:T(8,128)(2,1)S(1)} async-done(((bf16[16,8,512]{2,1,0:T(8,128)(2,1)}), bf16[16,8,512]{2,1,0:T(8,128)(2,1)S(1)}, u32[]{:S(2)}, u32[]{:S(2)}) %all-to-all-start.1) | async-done | bytes 131104 | tf_op jit(solution)/shard_map/all_to_all | solution.py:479
  38.4 1.1 %combine.1 = bf16[8,1024]{1,0:T(8,128)(2,1)} custom-call(bf16[16,8,512]{2,1,0:T(8,128)(2,1)S(1)} %all-to-all-done.1.parts_ref, bf16[512,1024]{1,0:T(8,128)(2,1)S(1)} %value_output.1.both_ref, bf16[8,1024]{1,0:T(8,128)(2,1)S(1)} %constant_dynamic-slice_fusion.own_ref), custom_call_target="tpu_custom_call" | custom-call | flops 4096000 | bytes 1048576 | tf_op jit(solution)/shard_map/combine/pallas_call | solution.py:481
  (2 shorter events, 0.0 us)
Async XLA Ops:
  0.0 0.7 %copy-start.4 = (bf16[14,56,6]{1,0,2:T(8,128)(2,1)S(1)}, bf16[14,56,6]{1,0,2:T(8,128)(2,1)}, u32[]{:S(2)}) copy-start(bf16[14,56,6]{1,0,2:T(8,128)(2,1)} %param.9) | copy-start | bytes 28228
  1.4 10.9 %all-to-all-start = ((bf16[4,8,896]{2,1,0:T(8,128)(2,1)}), bf16[4,8,896]{2,1,0:T(8,128)(2,1)S(1)}, u32[]{:S(2)}, u32[]{:S(2)}) async-start(bf16[4,8,896]{2,1,0:T(8,128)(2,1)} %pack.1), calls=%async_computation | async-start | bytes 114688 | tf_op jit(solution)/shard_map/all_to_all | solution.py:422
  12.3 3.9 %copy-start = (bf16[1760,256]{1,0:T(8,128)(2,1)S(1)}, bf16[1760,256]{1,0:T(8,128)(2,1)}, u32[]{:S(2)}) copy-start(bf16[1760,256]{1,0:T(8,128)(2,1)} %query_rows.1.rows_ref) | copy-start | bytes 2703364
  12.5 18.1 %copy-start.1 = (bf16[1024,1024]{1,0:T(8,128)(2,1)S(1)}, bf16[1024,1024]{1,0:T(8,128)(2,1)}, u32[]{:S(2)}) copy-start(bf16[1024,1024]{1,0:T(8,128)(2,1)} %out_ref.1) | copy-start | bytes 6291460
  12.5 18.1 %copy-start.3 = (bf16[54,704]{1,0:T(8,128)(2,1)S(1)}, bf16[54,704]{1,0:T(8,128)(2,1)}, u32[]{:S(2)}) copy-start(bf16[54,704]{1,0:T(8,128)(2,1)} %conv_ref.3) | copy-start | bytes 228100
  12.5 18.1 %copy-start.5 = (f32[704]{0:T(1024)S(1)}, f32[704]{0:T(1024)}, u32[]{:S(2)}) copy-start(f32[704]{0:T(1024)} %gain_ref.3) | copy-start | bytes 8452
  12.5 8.9 %collective-permute-start = (bf16[8,512]{1,0:T(8,128)(2,1)S(1)}, bf16[8,512]{1,0:T(8,128)(2,1)S(1)}, u32[]{:S(2)}, u32[]{:S(2)}) collective-permute-start(bf16[8,512]{1,0:T(8,128)(2,1)S(1)} %get-tuple-element.13), channel_id=1, source_target_pairs={{0,4},{4,8},{8,12},{12,16},{16,20},{20,24},{24,28},{28,32},{32,36}... | collective-permute-start | bytes 24584 | tf_op jit(solution)/shard_map/ppermute | solution.py:450
  23.8 14.6 %all-to-all-start.1 = ((bf16[16,8,512]{2,1,0:T(8,128)(2,1)}), bf16[16,8,512]{2,1,0:T(8,128)(2,1)S(1)}, u32[]{:S(2)}, u32[]{:S(2)}) async-start(bf16[16,8,512]{2,1,0:T(8,128)(2,1)} %bitcast.2), calls=%async_computation.1 | async-start | bytes 262144 | tf_op jit(solution)/shard_map/all_to_all | solution.py:479
  30.6 1.4 %copy-start.2 = (bf16[704,1024]{1,0:T(8,128)(2,1)S(1)}, bf16[704,1024]{1,0:T(8,128)(2,1)}, u32[]{:S(2)}) copy-start(bf16[704,1024]{1,0:T(8,128)(2,1)} %value_ref.1) | copy-start | bytes 4325380

commit v6 on v5

--- a/solution.py
+++ b/solution.py
@@ -115,9 +115,9 @@
     lat_copy = pltpu.make_async_copy(lat_hbm.at[:, lax.axis_index("gy")], lat_ref, sems.at[0])
     query_copy = pltpu.make_async_copy(query_hbm, query_ref, sems.at[1])
     key_copy = pltpu.make_async_copy(key_hbm, key_ref, sems.at[2])
+    key_copy.start()
     lat_copy.start()
     query_copy.start()
-    key_copy.start()
 
     weight = spread_weight(conv_ref, SPAN)
     feat = weight.shape[1]
@@ -131,7 +131,12 @@
     padding = jnp.zeros((LANES - SPAN, feat), BF16)
     gram = nt(both, jnp.concatenate([high, padding], axis=0)) + nt(both, jnp.concatenate([low, padding], axis=0))
     gram = (gram[:SPAN] + gram[SPAN:]) * (1.0 / feat)
-    rows_ref[held : held + 3 * SPAN, :LANES] = jnp.concatenate(thrice(gram), axis=0)
+    for part, piece in enumerate(thrice(gram)):
+        rows_ref[held : held + SPAN, part * SPAN : (part + 1) * SPAN] = piece[:, :SPAN]
+
+    key_copy.wait()
+    keys = nn(jnp.concatenate(split_up(weight * gain_ref[...].reshape(1, -1)), axis=0), key_ref[...])
+    high, low = split_up((keys[:SPAN] + keys[SPAN:]) * (LOG2E / DH**0.5))
 
     lat_copy.wait()
     values = lat_ref[...].astype(F32)
@@ -143,9 +148,6 @@
     query_copy.wait()
     queries = nn(normed, query_ref[...]).astype(BF16)
 
-    key_copy.wait()
-    keys = nn(jnp.concatenate(split_up(weight * gain_ref[...].reshape(1, -1)), axis=0), key_ref[...])
-    high, low = split_up((keys[:SPAN] + keys[SPAN:]) * (LOG2E / DH**0.5))
     count = values.shape[0]
     lane = iota((count, LINE), 1)
     padding = jnp.zeros((LINE - 3 * SPAN, 2 * DH), BF16)
@@ -177,12 +179,10 @@
         variance = total * (1.0 / feat)
         lost = None
     else:
-        gram = rows_ref[held : held + 3 * SPAN, :LANES]
-        form = nn(gram[:, :SPAN], exact)
-        form = form[:SPAN] + form[SPAN : 2 * SPAN] + form[2 * SPAN :]
+        gram = rows_ref[held : held + SPAN, : 3 * SPAN]
+        form = nn(gram, jnp.concatenate([exact, exact, exact], axis=0))
         variance = jnp.maximum(jnp.sum(form * patches, axis=0, keepdims=True), 0.0)
-        shape = (SPAN, LANES)
-        diag = jnp.where(iota(shape, 0) == iota(shape, 1), gram[:SPAN].astype(F32), 0.0)
+        diag = jnp.where(iota(gram.shape, 0) == iota(gram.shape, 1), gram.astype(F32), 0.0)
         diag = jnp.sum(diag, axis=-1, keepdims=True)
         scale = jnp.sum(patches * patches * diag, axis=0, keepdims=True)
         lost = jnp.where((variance + EPS) * 128.0 < scale, 1.0, 0.0)
@@ -239,22 +239,30 @@
     shifted = [pltpu.roll(strip, 1, 1), strip, pltpu.roll(strip, width - 1, 1)]
     count = sums_ref.shape[0]
     blocks = [(slice(0, count), slice(at, at + size)) for at in range(0, inner, size)]
+    half = count // 2
+    halves = [(slice(r, r + half), b) for _, b in blocks for r in (0, half)]
 
     def run(explicit):
         flags = []
-        for at in range(0, inner, size):
-            end = at + size
+
+        def fill(turn):
+            at, end = blocks[turn][1].start, blocks[turn][1].stop
             cells = [shifted[tap % 3][:, tap // 3 * LINE + at : tap // 3 * LINE + end] for tap in range(TAPS)]
             patches = jnp.concatenate(cells + [jnp.zeros_like(cells[0])], axis=0)
-            real = iota(patches.shape, 1) % LINE < columns
+            real = (iota(patches.shape, 1) + at) % LINE < columns
             flags.append(fill_block(patches, real, explicit, feat, rows_ref, pixel_ref, at))
-        tops, sums = attend(blocks, rows_ref, pixel_ref, score_ref, expo_ref)
+
+        for turn in range(len(blocks)):
+            fill(turn)
+        tops, sums = attend(halves, rows_ref, pixel_ref, score_ref, expo_ref)
+        tops = [jnp.concatenate(tops[i : i + 2], axis=0) for i in range(0, len(tops), 2)]
+        sums = [jnp.concatenate(sums[i : i + 2], axis=0) for i in range(0, len(sums), 2)]
         top, total = merged(tops, sums)
         sums_ref[...] = total
         tops_ref[...] = jnp.broadcast_to(top, tops_ref.shape)
-        return flags
-
-    lost = jnp.max(functools.reduce(jnp.maximum, run(False)))
+        return [jnp.max(flag) for flag in flags if flag is not None]
+
+    lost = functools.reduce(jnp.maximum, run(False))
 
     @pl.when(lost > 0.5)
     def _():
@@ -449,7 +457,7 @@
     )(tiles)
     before = lax.ppermute(last, "gx", [(i, i + 1) for i in range(down - 1)])
     inner = (tile_rows - 2) * LINE
-    size = inner // 3
+    size = inner // 2
     sums, tops = kernel(
         functools.partial(inner_kernel, columns, size, feat),
         "inner",
@@ -461,7 +469,7 @@
         ],
         count=2,
         cycles=10000,
-        room=34,
+        room=44,
     )(strip, rows)
     sent = kernel(
         functools.partial(border_kernel, columns, feat),

time: 39.9 us -> 39.4 us (0.987)
  Pallas kernels: 15.2 us -> 14.7 us
  transfers between devices with their start and end apart: 3 -> 3, of which waited for: 1 -> 1; matrix products, arithmetic and copies ran while one was open for 2% -> 2% of each run, Pallas kernels for 28% -> 27%
where the time goes in v6:
time: 39.4 us; the launch traced here: 38.9 us
  starting transfers between devices  16.5 us (42%)
  Pallas kernels  14.7 us (37%)
  waiting for transfers between devices  4.72 us (12%)
  local copies, waits for them, and re-layouts  2.84 us (7%)
    all_to_all x1, starting transfers between devices, on_device(): lax.all_to_all(sent.reshape(down, share, -1), 'gx', 0, 0, tiled=True)  6.74 us
    all_to_all x1, starting transfers between devices, on_device(): tiles = lax.all_to_all(copies, 'gy', 0, 0, tiled=True)  6 us
    pallas_call x1, Pallas kernels, on_device(): kernel(query_kernel, 'query_rows', shape((HEADS * held + table_rows(feat)...  4.79 us
    pallas_call x1, Pallas kernels, on_device(): kernel(functools.partial(inner_kernel, columns, size, feat), 'inner', [sh...  4.73 us
    all_to_all x1, waiting for transfers between devices, on_device(): lax.all_to_all(sent.reshape(down, share, -1), 'gx', 0, 0, tiled=True)  4.71 us
    ppermute x1, starting transfers between devices, on_device(): before = lax.ppermute(last, 'gx', [(i, i + 1) for i in range(down - 1)])  3.74 us
    pallas_call x1, Pallas kernels, on_device(): kernel(functools.partial(border_kernel, columns, feat), 'border', shape((...  2.36 us
    unnamed x12, local copies, waits for them, and re-layouts  2.12 us
  transfers between devices with their start and end apart: 3, of which 1 were waited for; matrix products, arithmetic and copies ran while one was open for 2% of the time, Pallas kernels for 27%

profile of v6, /device:TPU:32, one launch (start us, length us, event | category | flops | bytes accessed | tf_op | source)
XLA Modules:
  0.0 38.9 jit_solution(14637113445038400772)
XLA Ops:
  0.0 0.7 %copy-done.4 = bf16[14,56,6]{1,0,2:T(8,128)(2,1)S(1)} copy-done((bf16[14,56,6]{1,0,2:T(8,128)(2,1)S(1)}, bf16[14,56,6]{1,0,2:T(8,128)(2,1)}, u32[]{:S(2)}) %copy-start.4) | copy-done | bytes 9432
  0.7 0.7 %pack.1 = bf16[4,8,896]{2,1,0:T(8,128)(2,1)} custom-call(bf16[6,14,56]{2,1,0:T(8,128)(2,1)S(1)} %bitcast.3), custom_call_target="tpu_custom_call" | custom-call | flops 4096000 | bytes 1048576 | tf_op jit(solution)/shard_map/pack/pallas_call | solution.py:423
  1.4 6.0 %all-to-all-start = ((bf16[4,8,896]{2,1,0:T(8,128)(2,1)}), bf16[4,8,896]{2,1,0:T(8,128)(2,1)S(1)}, u32[]{:S(2)}, u32[]{:S(2)}) async-start(bf16[4,8,896]{2,1,0:T(8,128)(2,1)} %pack.1), calls=%async_computation | async-start | bytes 114688 | tf_op jit(solution)/shard_map/all_to_all | solution.py:430
  7.4 4.8 %query_rows.1.rows_ref = bf16[1760,256]{1,0:T(8,128)(2,1)} custom-call(bf16[54,704]{1,0:T(8,128)(2,1)} %conv_ref.3, f32[704]{0:T(1024)} %gain_ref.3, f32[1024]{0:T(1024)} %lat_gain_ref.1, bf16[16,4,8,1024]{3,2,1,0:T(8,128)(2,1)} %bitcast.4, bf16[1024,1024]{1,0:T(8,128)(2,1)} %query_hbm.1, bf16[704,1024]{1,0:T(8,128)(2,1)} %key_hbm.1), custom_call_target="tpu_custom_call" | custom-call | flops 24576000 | bytes 1048576 | tf_op jit(solution)/shard_map/query_rows/pallas_call | solution.py:431
  12.2 0.0 copy-start
  12.3 0.0 all-to-all-done.tiles_ref
  12.3 0.1 join.1
  12.4 0.0 copy-start.1
  12.4 0.0 copy-start.3
  12.4 0.0 copy-start.5
  12.4 3.7 %collective-permute-start = (bf16[8,512]{1,0:T(8,128)(2,1)S(1)}, bf16[8,512]{1,0:T(8,128)(2,1)S(1)}, u32[]{:S(2)}, u32[]{:S(2)}) collective-permute-start(bf16[8,512]{1,0:T(8,128)(2,1)S(1)} %get-tuple-element.13), channel_id=1, source_target_pairs={{0,4},{4,8},{8,12},{12,16},{16,20},{20,24},{24,28},{28,32},{32,36}... | collective-permute-start | bytes 24584 | tf_op jit(solution)/shard_map/ppermute | solution.py:458
  16.2 4.7 %inner.1 = (f32[1024,128]{1,0:T(8,128)S(1)}, f32[1024,128]{1,0:T(8,128)S(1)}) custom-call(f32[8,3584]{1,0:T(8,128)S(1)} %get-tuple-element.12.strip_ref, bf16[1760,256]{1,0:T(8,128)(2,1)S(1)} %copy-done), custom_call_target="tpu_custom_call" | custom-call | flops 40960000 | bytes 1048576 | tf_op jit(solution)/shard_map/inner/pallas_call | solution.py:461
  20.9 0.0 collective-permute-done.before_ref
  20.9 2.4 %border.1 = bf16[128,512]{1,0:T(8,128)(2,1)} custom-call(f32[8,3584]{1,0:T(8,128)S(1)} %get-tuple-element.12.strip_ref, bf16[8,512]{1,0:T(8,128)(2,1)S(1)} %collective-permute-done.before_ref, bf16[1760,256]{1,0:T(8,128)(2,1)S(1)} %copy-done, f32[1024,128]{1,0:T(8,128)S(1)} %get-tuple-element.15.inner_sums_ref, f32[1024,128]{1,0:T(8,128)S(1)} %get-tuple-element.16.inner_tops_ref), custom_call_target="tpu_custom_call" | custom-call | flops 12288000 | bytes 1048576 | tf_op jit(solution)/shard_map/border/pallas_call | solution.py:474
  23.3 6.7 %all-to-all-start.1 = ((bf16[16,8,512]{2,1,0:T(8,128)(2,1)}), bf16[16,8,512]{2,1,0:T(8,128)(2,1)S(1)}, u32[]{:S(2)}, u32[]{:S(2)}) async-start(bf16[16,8,512]{2,1,0:T(8,128)(2,1)} %bitcast.2), calls=%async_computation.1 | async-start | bytes 262144 | tf_op jit(solution)/shard_map/all_to_all | solution.py:487
  30.0 0.0 copy-done.1
  30.0 0.0 copy-done.3
  30.1 0.0 copy-done.5
  30.1 0.0 copy-start.2
  30.1 1.4 %copy-done.2 = bf16[704,1024]{1,0:T(8,128)(2,1)S(1)} copy-done((bf16[704,1024]{1,0:T(8,128)(2,1)S(1)}, bf16[704,1024]{1,0:T(8,128)(2,1)}, u32[]{:S(2)}) %copy-start.2) | copy-done | bytes 1441816
  31.4 1.0 %value_output.1.both_ref = bf16[512,1024]{1,0:T(8,128)(2,1)S(1)} custom-call(bf16[54,704]{1,0:T(8,128)(2,1)S(1)} %copy-done.3, f32[704]{0:T(1024)S(1)} %copy-done.5, bf16[704,1024]{1,0:T(8,128)(2,1)S(1)} %copy-done.2, bf16[1024,1024]{1,0:T(8,128)(2,1)S(1)} %copy-done.1), custom_call_target="tpu_custom_call" | custom-call | flops 24576000 | bytes 1048576 | tf_op jit(solution)/shard_map/value_output/pallas_call | solution.py:446
  32.4 0.7 %constant_dynamic-slice_fusion.own_ref = bf16[8,1024]{1,0:T(8,128)(2,1)S(1)} fusion(bf16[512,1024]{1,0:T(8,128)(2,1)} %param.14, s32[]{:T(128)S(6)} %select_n.3), kind=kLoop, calls=%fused_computation | loop fusion | bytes 32772 | tf_op jit(solution)/shard_map/dynamic_slice | solution.py:488
  33.2 4.7 %all-to-all-done.1.parts_ref = bf16[16,8,512]{2,1,0:T(8,128)(2,1)S(1)} async-done(((bf16[16,8,512]{2,1,0:T(8,128)(2,1)}), bf16[16,8,512]{2,1,0:T(8,128)(2,1)S(1)}, u32[]{:S(2)}, u32[]{:S(2)}) %all-to-all-start.1) | async-done | bytes 131104 | tf_op jit(solution)/shard_map/all_to_all | solution.py:487
  37.9 1.1 %combine.1 = bf16[8,1024]{1,0:T(8,128)(2,1)} custom-call(bf16[16,8,512]{2,1,0:T(8,128)(2,1)S(1)} %all-to-all-done.1.parts_ref, bf16[512,1024]{1,0:T(8,128)(2,1)S(1)} %value_output.1.both_ref, bf16[8,1024]{1,0:T(8,128)(2,1)S(1)} %constant_dynamic-slice_fusion.own_ref), custom_call_target="tpu_custom_call" | custom-call | flops 4096000 | bytes 1048576 | tf_op jit(solution)/shard_map/combine/pallas_call | solution.py:489
  (2 shorter events, 0.0 us)
Async XLA Ops:
  0.0 0.7 %copy-start.4 = (bf16[14,56,6]{1,0,2:T(8,128)(2,1)S(1)}, bf16[14,56,6]{1,0,2:T(8,128)(2,1)}, u32[]{:S(2)}) copy-start(bf16[14,56,6]{1,0,2:T(8,128)(2,1)} %param.9) | copy-start | bytes 28228
  1.4 10.8 %all-to-all-start = ((bf16[4,8,896]{2,1,0:T(8,128)(2,1)}), bf16[4,8,896]{2,1,0:T(8,128)(2,1)S(1)}, u32[]{:S(2)}, u32[]{:S(2)}) async-start(bf16[4,8,896]{2,1,0:T(8,128)(2,1)} %pack.1), calls=%async_computation | async-start | bytes 114688 | tf_op jit(solution)/shard_map/all_to_all | solution.py:430
  12.2 3.9 %copy-start = (bf16[1760,256]{1,0:T(8,128)(2,1)S(1)}, bf16[1760,256]{1,0:T(8,128)(2,1)}, u32[]{:S(2)}) copy-start(bf16[1760,256]{1,0:T(8,128)(2,1)} %query_rows.1.rows_ref) | copy-start | bytes 2703364
  12.4 17.7 %copy-start.1 = (bf16[1024,1024]{1,0:T(8,128)(2,1)S(1)}, bf16[1024,1024]{1,0:T(8,128)(2,1)}, u32[]{:S(2)}) copy-start(bf16[1024,1024]{1,0:T(8,128)(2,1)} %out_ref.1) | copy-start | bytes 6291460
  12.4 17.7 %copy-start.3 = (bf16[54,704]{1,0:T(8,128)(2,1)S(1)}, bf16[54,704]{1,0:T(8,128)(2,1)}, u32[]{:S(2)}) copy-start(bf16[54,704]{1,0:T(8,128)(2,1)} %conv_ref.3) | copy-start | bytes 228100
  12.4 17.7 %copy-start.5 = (f32[704]{0:T(1024)S(1)}, f32[704]{0:T(1024)}, u32[]{:S(2)}) copy-start(f32[704]{0:T(1024)} %gain_ref.3) | copy-start | bytes 8452
  12.4 8.5 %collective-permute-start = (bf16[8,512]{1,0:T(8,128)(2,1)S(1)}, bf16[8,512]{1,0:T(8,128)(2,1)S(1)}, u32[]{:S(2)}, u32[]{:S(2)}) collective-permute-start(bf16[8,512]{1,0:T(8,128)(2,1)S(1)} %get-tuple-element.13), channel_id=1, source_target_pairs={{0,4},{4,8},{8,12},{12,16},{16,20},{20,24},{24,28},{28,32},{32,36}... | collective-permute-start | bytes 24584 | tf_op jit(solution)/shard_map/ppermute | solution.py:458
  23.3 14.6 %all-to-all-start.1 = ((bf16[16,8,512]{2,1,0:T(8,128)(2,1)}), bf16[16,8,512]{2,1,0:T(8,128)(2,1)S(1)}, u32[]{:S(2)}, u32[]{:S(2)}) async-start(bf16[16,8,512]{2,1,0:T(8,128)(2,1)} %bitcast.2), calls=%async_computation.1 | async-start | bytes 262144 | tf_op jit(solution)/shard_map/all_to_all | solution.py:487
  30.1 1.4 %copy-start.2 = (bf16[704,1024]{1,0:T(8,128)(2,1)S(1)}, bf16[704,1024]{1,0:T(8,128)(2,1)}, u32[]{:S(2)}) copy-start(bf16[704,1024]{1,0:T(8,128)(2,1)} %value_ref.1) | copy-start | bytes 4325380

commit v7 on v6

--- a/solution.py
+++ b/solution.py
@@ -72,7 +72,7 @@
             copies_ref[copy, :, pair * LANES : (pair + 1) * LANES] = packed
 
 
-def join_kernel(columns, tiles_ref, strip_ref, last_ref):
+def join_kernel(columns, tiles_ref, strip_ref, first_ref):
     tiles, _, width = tiles_ref.shape
     pairs = width // LANES
     lane = iota((pairs * SUB, LANES), 1)
@@ -96,7 +96,7 @@
             for half, line in enumerate(halves):
                 at = row * LINE + half * LANES
                 strip_ref[:, at : at + LANES] = line[pair * SUB : (pair + 1) * SUB]
-    last_ref[...] = strip_ref[:, 2 * pairs * LINE - 2 * LINE :].astype(BF16)
+    first_ref[...] = strip_ref[:, : 2 * LINE].astype(BF16)
 
 
 def spread_weight(conv_ref, copies):
@@ -110,15 +110,16 @@
 
 
 def query_kernel(
-    conv_ref, gain_ref, lat_gain_ref, lat_hbm, query_hbm, key_hbm, rows_ref, lat_ref, query_ref, key_ref, sems
+    key_hbm, conv_hbm, gain_hbm, lat_hbm, lat_gain_hbm, query_hbm, rows_ref,
+    key_ref, conv_ref, gain_ref, lat_ref, lat_gain_ref, query_ref, sems,
 ):
-    lat_copy = pltpu.make_async_copy(lat_hbm.at[:, lax.axis_index("gy")], lat_ref, sems.at[0])
-    query_copy = pltpu.make_async_copy(query_hbm, query_ref, sems.at[1])
-    key_copy = pltpu.make_async_copy(key_hbm, key_ref, sems.at[2])
-    key_copy.start()
-    lat_copy.start()
-    query_copy.start()
-
+    sources = [key_hbm, conv_hbm, gain_hbm, lat_hbm.at[:, lax.axis_index("gy")], lat_gain_hbm, query_hbm]
+    targets = [key_ref, conv_ref, gain_ref, lat_ref, lat_gain_ref, query_ref]
+    copies = [pltpu.make_async_copy(*pair, sems.at[i]) for i, pair in enumerate(zip(sources, targets))]
+    for copy in copies:
+        copy.start()
+
+    copies[1].wait()
     weight = spread_weight(conv_ref, SPAN)
     feat = weight.shape[1]
     high, low = split_up(weight)
@@ -134,18 +135,20 @@
     for part, piece in enumerate(thrice(gram)):
         rows_ref[held : held + SPAN, part * SPAN : (part + 1) * SPAN] = piece[:, :SPAN]
 
-    key_copy.wait()
+    copies[2].wait()
+    copies[0].wait()
     keys = nn(jnp.concatenate(split_up(weight * gain_ref[...].reshape(1, -1)), axis=0), key_ref[...])
     high, low = split_up((keys[:SPAN] + keys[SPAN:]) * (LOG2E / DH**0.5))
 
-    lat_copy.wait()
+    copies[3].wait()
+    copies[4].wait()
     values = lat_ref[...].astype(F32)
     values = values.reshape(values.shape[0] * values.shape[1], values.shape[2])
     centred = values - jnp.mean(values, axis=-1, keepdims=True)
     variance = jnp.mean(centred * centred, axis=-1, keepdims=True)
     gain = lat_gain_ref[...].reshape(1, -1)
     normed = (centred * lax.rsqrt(variance + EPS) * gain).astype(BF16)
-    query_copy.wait()
+    copies[5].wait()
     queries = nn(normed, query_ref[...]).astype(BF16)
 
     count = values.shape[0]
@@ -273,7 +276,7 @@
     columns,
     feat,
     strip_ref,
-    before_ref,
+    after_ref,
     rows_ref,
     inner_sums_ref,
     inner_tops_ref,
@@ -285,29 +288,18 @@
     width = strip_ref.shape[1]
     lines = jnp.concatenate(
         [
-            before_ref[...].astype(F32),
+            strip_ref[:, width - 2 * LINE :],
+            after_ref[...].astype(F32),
+            jnp.zeros((SUB, LINE), F32),
             strip_ref[:, : 2 * LINE],
-            strip_ref[:, width - 2 * LINE :],
-            jnp.zeros((SUB, LINE), F32),
         ],
         axis=1,
     )
     shifted = [pltpu.roll(lines, 1, 1), lines, pltpu.roll(lines, lines.shape[1] - 1, 1)]
-    cells = []
-    for tap in range(TAPS):
-        at = tap // 3 * LINE
-        source = shifted[tap % 3]
-        cells.append(jnp.concatenate([source[:, at : at + 2 * LINE], source[:, at + 4 * LINE : at + 5 * LINE]], axis=1))
-    patches = jnp.concatenate(cells + [jnp.zeros_like(cells[0])], axis=0)
-    lane = iota(patches.shape, 1)
-    place = lax.axis_index("gx")
-    above = (place > 0).astype(jnp.int32)
-    final = (place == lax.axis_size("gx") - 1).astype(jnp.int32)
-    shown = jnp.where(lane < LINE, above, jnp.where(lane < 2 * LINE, 1, final))
-    real = (lane % LINE < columns) & (shown > 0)
+    place_x = lax.axis_index("gx")
+    below = (place_x < lax.axis_size("gx") - 1).astype(jnp.int32)
     count = sent_ref.shape[0]
     half = score_ref.shape[1] // 2
-    blocks = [(slice(at, at + half), slice(0, patches.shape[1])) for at in (0, half)]
     shape = (2 * LANES, LANES)
     row, lane = iota(shape, 0), iota(shape, 1)
     tap = row % LANES
@@ -315,8 +307,17 @@
     target = jnp.where(tap == ONE, TOTAL, jnp.where(tap == ONE_TOO, TOTAL + 1, target))
     place = jnp.where((target >= 0) & (lane == target + row // LANES * SLOT), 1.0, 0.0).astype(BF16)
 
-    def run(explicit):
+    def run(explicit, starts):
+        cells = []
+        for tap in range(TAPS):
+            at = tap // 3 * LINE
+            source = shifted[tap % 3]
+            cells.append(jnp.concatenate([source[:, start + at : start + at + LINE] for start in starts], axis=1))
+        patches = jnp.concatenate(cells + [jnp.zeros_like(cells[0])], axis=0)
+        lane = iota(patches.shape, 1)
+        real = (lane % LINE < columns) & (jnp.where(lane // LINE == 1, below, 1) > 0)
         lost = fill_block(patches, real, explicit, feat, rows_ref, pixel_ref, 0)
+        blocks = [(slice(at, at + half), slice(0, patches.shape[1])) for at in (0, half)]
         tops, sums = attend(blocks, rows_ref, pixel_ref, score_ref, expo_ref)
         tops, sums = jnp.concatenate(tops, axis=0), jnp.concatenate(sums, axis=0)
         top, total = merged([inner_tops_ref[...], tops], [inner_sums_ref[...], sums])
@@ -339,11 +340,20 @@
             sent_ref[:, pair * LANES : (pair + 1) * LANES] = placed[pair * count : (pair + 1) * count]
         return lost
 
-    lost = jnp.max(run(False))
-
-    @pl.when(lost > 0.5)
+    def checked(starts):
+        lost = jnp.max(run(False, starts))
+
+        @pl.when(lost > 0.5)
+        def _():
+            run(True, starts)
+
+    @pl.when(place_x > 0)
     def _():
-        run(True)
+        checked([0, LINE])
+
+    @pl.when(place_x == 0)
+    def _():
+        checked([0, LINE, 4 * LINE])
 
 
 def output_kernel(conv_ref, gain_ref, value_ref, out_ref, both_ref):
@@ -433,29 +443,31 @@
         "query_rows",
         shape((HEADS * held + table_rows(feat), LINE)),
         [
+            pltpu.VMEM(key_weight.shape, BF16),
+            pltpu.VMEM(conv_weight.shape, BF16),
+            pltpu.VMEM(input_gain.shape, F32),
             pltpu.VMEM((down, share, width), BF16),
+            pltpu.VMEM(latent_gain.shape, F32),
             pltpu.VMEM(query_weight.shape, BF16),
-            pltpu.VMEM(key_weight.shape, BF16),
-            pltpu.SemaphoreType.DMA((3,)),
+            pltpu.SemaphoreType.DMA((6,)),
         ],
-        others=3,
-        count=3,
+        others=6,
         cycles=6000,
         room=60,
-    )(conv_weight, input_gain, latent_gain, latents.reshape(down, across, share, width), query_weight, key_weight)
+    )(key_weight, conv_weight, input_gain, latents.reshape(down, across, share, width), latent_gain, query_weight)
     both = kernel(
         output_kernel, "value_output", shape((HEADS * SLOT, width)), count=4, cycles=6000, room=10
     )(conv_weight, input_gain, value_weight, out_weight)
 
     tiles, rows = lax.optimization_barrier((tiles, rows))
-    strip, last = kernel(
+    strip, first = kernel(
         functools.partial(join_kernel, tile_cols),
         "join",
         [shape((SUB, tile_rows * LINE), F32), shape((SUB, 2 * LINE))],
         count=1,
         cycles=200000,
     )(tiles)
-    before = lax.ppermute(last, "gx", [(i, i + 1) for i in range(down - 1)])
+    after = lax.ppermute(first, "gx", [(i + 1, i) for i in range(down - 1)])
     inner = (tile_rows - 2) * LINE
     size = inner // 2
     sums, tops = kernel(
@@ -483,7 +495,7 @@
         count=5,
         cycles=3000,
         room=24,
-    )(strip, before, rows, sums, tops)
+    )(strip, after, rows, sums, tops)
     parts = lax.all_to_all(sent.reshape(down, share, -1), "gx", 0, 0, tiled=True)
     own = lax.dynamic_slice_in_dim(latents, lax.axis_index(GROUP) * share, share, 0)
     return kernel(combine_kernel, "combine", shape((share, width)), count=3, room=6)(parts, both, own)

time: 39.4 us -> 38.5 us (0.977)
  starting transfers between devices: 16.5 us -> 15.7 us
    ppermute x1, starting transfers between devices: 3.74 us -> 1.56 us  [on_device(): after = lax.ppermute(first, 'gx', [(i + 1, i) for i in range(down - 1)])]
    all_to_all x1, starting transfers between devices: 6.74 us -> 8.18 us  [on_device(): lax.all_to_all(sent.reshape(down, share, -1), 'gx', 0, 0, tiled=True)]
where the time goes in v7:
time: 38.5 us; the launch traced here: 38 us
  starting transfers between devices  15.7 us (41%)
  Pallas kernels  14.6 us (38%)
  waiting for transfers between devices  4.72 us (12%)
  local copies, waits for them, and re-layouts  2.84 us (7%)
    all_to_all x1, starting transfers between devices, on_device(): lax.all_to_all(sent.reshape(down, share, -1), 'gx', 0, 0, tiled=True)  8.18 us
    all_to_all x1, starting transfers between devices, on_device(): tiles = lax.all_to_all(copies, 'gy', 0, 0, tiled=True)  6 us
    pallas_call x1, Pallas kernels, on_device(): kernel(functools.partial(inner_kernel, columns, size, feat), 'inner', [sh...  4.73 us
    all_to_all x1, waiting for transfers between devices, on_device(): lax.all_to_all(sent.reshape(down, share, -1), 'gx', 0, 0, tiled=True)  4.71 us
    pallas_call x1, Pallas kernels, on_device(): kernel(query_kernel, 'query_rows', shape((HEADS * held + table_rows(feat)...  4.61 us
    pallas_call x1, Pallas kernels, on_device(): kernel(functools.partial(border_kernel, columns, feat), 'border', shape((...  2.38 us
    unnamed x12, local copies, waits for them, and re-layouts  2.12 us
    ppermute x1, starting transfers between devices, on_device(): after = lax.ppermute(first, 'gx', [(i + 1, i) for i in range(down - 1)])  1.56 us
  transfers between devices with their start and end apart: 3, of which 1 were waited for; matrix products, arithmetic and copies ran while one was open for 2% of the time, Pallas kernels for 27%

profile of v7, /device:TPU:32, one launch (start us, length us, event | category | flops | bytes accessed | tf_op | source)
XLA Modules:
  0.0 38.0 jit_solution(2539620966862441005)
XLA Ops:
  0.0 0.7 %copy-done.4 = bf16[14,56,6]{1,0,2:T(8,128)(2,1)S(1)} copy-done((bf16[14,56,6]{1,0,2:T(8,128)(2,1)S(1)}, bf16[14,56,6]{1,0,2:T(8,128)(2,1)}, u32[]{:S(2)}) %copy-start.4) | copy-done | bytes 9432
  0.7 0.7 %pack.1 = bf16[4,8,896]{2,1,0:T(8,128)(2,1)} custom-call(bf16[6,14,56]{2,1,0:T(8,128)(2,1)S(1)} %bitcast.3), custom_call_target="tpu_custom_call" | custom-call | flops 4096000 | bytes 1048576 | tf_op jit(solution)/shard_map/pack/pallas_call | solution.py:433
  1.4 6.0 %all-to-all-start = ((bf16[4,8,896]{2,1,0:T(8,128)(2,1)}), bf16[4,8,896]{2,1,0:T(8,128)(2,1)S(1)}, u32[]{:S(2)}, u32[]{:S(2)}) async-start(bf16[4,8,896]{2,1,0:T(8,128)(2,1)} %pack.1), calls=%async_computation | async-start | bytes 114688 | tf_op jit(solution)/shard_map/all_to_all | solution.py:440
  7.4 4.6 %query_rows.1.rows_ref = bf16[1760,256]{1,0:T(8,128)(2,1)} custom-call(bf16[704,1024]{1,0:T(8,128)(2,1)} %key_hbm.1, bf16[54,704]{1,0:T(8,128)(2,1)} %conv_ref.1, f32[704]{0:T(1024)} %gain_ref.1, bf16[16,4,8,1024]{3,2,1,0:T(8,128)(2,1)} %bitcast.4, f32[1024]{0:T(1024)} %lat_gain_hbm.1, bf16[1024,1024]{1,0:T(8,128)(2,1)} %query_hbm.1), custom_call_target="tpu_custom_call" | custom-call | flops 24576000 | bytes 1048576 | tf_op jit(solution)/shard_map/query_rows/pallas_call | solution.py:441
  12.1 0.0 copy-start
  12.1 0.0 all-to-all-done.tiles_ref
  12.1 0.1 join.1
  12.2 0.0 copy-start.1
  12.2 0.0 copy-start.3
  12.2 0.0 copy-start.5
  12.2 1.6 %collective-permute-start = (bf16[8,512]{1,0:T(8,128)(2,1)S(1)}, bf16[8,512]{1,0:T(8,128)(2,1)S(1)}, u32[]{:S(2)}, u32[]{:S(2)}) collective-permute-start(bf16[8,512]{1,0:T(8,128)(2,1)S(1)} %get-tuple-element.13), channel_id=1, source_target_pairs={{4,0},{8,4},{12,8},{16,12},{20,16},{24,20},{28,24},{32,28},{36,32}... | collective-permute-start | bytes 24584 | tf_op jit(solution)/shard_map/ppermute | solution.py:470
  13.8 0.0 copy-done
  13.8 4.7 %inner.1 = (f32[1024,128]{1,0:T(8,128)S(1)}, f32[1024,128]{1,0:T(8,128)S(1)}) custom-call(f32[8,3584]{1,0:T(8,128)S(1)} %get-tuple-element.12.strip_ref, bf16[1760,256]{1,0:T(8,128)(2,1)S(1)} %copy-done), custom_call_target="tpu_custom_call" | custom-call | flops 40960000 | bytes 1048576 | tf_op jit(solution)/shard_map/inner/pallas_call | solution.py:473
  18.5 0.0 collective-permute-done.after_ref
  18.5 2.4 %border.1 = bf16[128,512]{1,0:T(8,128)(2,1)} custom-call(f32[8,3584]{1,0:T(8,128)S(1)} %get-tuple-element.12.strip_ref, bf16[8,512]{1,0:T(8,128)(2,1)S(1)} %collective-permute-done.after_ref, bf16[1760,256]{1,0:T(8,128)(2,1)S(1)} %copy-done, f32[1024,128]{1,0:T(8,128)S(1)} %get-tuple-element.15.inner_sums_ref, f32[1024,128]{1,0:T(8,128)S(1)} %get-tuple-element.16.inner_tops_ref), custom_call_target="tpu_custom_call" | custom-call | flops 12288000 | bytes 1048576 | tf_op jit(solution)/shard_map/border/pallas_call | solution.py:486
  20.9 8.2 %all-to-all-start.1 = ((bf16[16,8,512]{2,1,0:T(8,128)(2,1)}), bf16[16,8,512]{2,1,0:T(8,128)(2,1)S(1)}, u32[]{:S(2)}, u32[]{:S(2)}) async-start(bf16[16,8,512]{2,1,0:T(8,128)(2,1)} %bitcast.2), calls=%async_computation.1 | async-start | bytes 262144 | tf_op jit(solution)/shard_map/all_to_all | solution.py:499
  29.1 0.0 copy-done.1
  29.1 0.0 copy-done.3
  29.2 0.0 copy-start.2
  29.2 1.4 %copy-done.2 = bf16[704,1024]{1,0:T(8,128)(2,1)S(1)} copy-done((bf16[704,1024]{1,0:T(8,128)(2,1)S(1)}, bf16[704,1024]{1,0:T(8,128)(2,1)}, u32[]{:S(2)}) %copy-start.2) | copy-done | bytes 1441816
  30.5 1.0 %value_output.1.both_ref = bf16[512,1024]{1,0:T(8,128)(2,1)S(1)} custom-call(bf16[54,704]{1,0:T(8,128)(2,1)S(1)} %copy-done.3, f32[704]{0:T(1024)S(1)} %copy-done.5, bf16[704,1024]{1,0:T(8,128)(2,1)S(1)} %copy-done.2, bf16[1024,1024]{1,0:T(8,128)(2,1)S(1)} %copy-done.1), custom_call_target="tpu_custom_call" | custom-call | flops 24576000 | bytes 1048576 | tf_op jit(solution)/shard_map/value_output/pallas_call | solution.py:458
  31.5 0.7 %constant_dynamic-slice_fusion.own_ref = bf16[8,1024]{1,0:T(8,128)(2,1)S(1)} fusion(bf16[512,1024]{1,0:T(8,128)(2,1)} %param.14, s32[]{:T(128)S(6)} %select_n.3), kind=kLoop, calls=%fused_computation | loop fusion | bytes 32772 | tf_op jit(solution)/shard_map/dynamic_slice | solution.py:500
  32.2 4.7 %all-to-all-done.1.parts_ref = bf16[16,8,512]{2,1,0:T(8,128)(2,1)S(1)} async-done(((bf16[16,8,512]{2,1,0:T(8,128)(2,1)}), bf16[16,8,512]{2,1,0:T(8,128)(2,1)S(1)}, u32[]{:S(2)}, u32[]{:S(2)}) %all-to-all-start.1) | async-done | bytes 131104 | tf_op jit(solution)/shard_map/all_to_all | solution.py:499
  37.0 1.1 %combine.1 = bf16[8,1024]{1,0:T(8,128)(2,1)} custom-call(bf16[16,8,512]{2,1,0:T(8,128)(2,1)S(1)} %all-to-all-done.1.parts_ref, bf16[512,1024]{1,0:T(8,128)(2,1)S(1)} %value_output.1.both_ref, bf16[8,1024]{1,0:T(8,128)(2,1)S(1)} %constant_dynamic-slice_fusion.own_ref), custom_call_target="tpu_custom_call" | custom-call | flops 4096000 | bytes 1048576 | tf_op jit(solution)/shard_map/combine/pallas_call | solution.py:501
  (2 shorter events, 0.0 us)
Async XLA Ops:
  0.0 0.7 %copy-start.4 = (bf16[14,56,6]{1,0,2:T(8,128)(2,1)S(1)}, bf16[14,56,6]{1,0,2:T(8,128)(2,1)}, u32[]{:S(2)}) copy-start(bf16[14,56,6]{1,0,2:T(8,128)(2,1)} %param.9) | copy-start | bytes 28228
  1.4 10.6 %all-to-all-start = ((bf16[4,8,896]{2,1,0:T(8,128)(2,1)}), bf16[4,8,896]{2,1,0:T(8,128)(2,1)S(1)}, u32[]{:S(2)}, u32[]{:S(2)}) async-start(bf16[4,8,896]{2,1,0:T(8,128)(2,1)} %pack.1), calls=%async_computation | async-start | bytes 114688 | tf_op jit(solution)/shard_map/all_to_all | solution.py:440
  12.1 1.7 %copy-start = (bf16[1760,256]{1,0:T(8,128)(2,1)S(1)}, bf16[1760,256]{1,0:T(8,128)(2,1)}, u32[]{:S(2)}) copy-start(bf16[1760,256]{1,0:T(8,128)(2,1)} %query_rows.1.rows_ref) | copy-start | bytes 2703364
  12.2 16.9 %copy-start.1 = (bf16[1024,1024]{1,0:T(8,128)(2,1)S(1)}, bf16[1024,1024]{1,0:T(8,128)(2,1)}, u32[]{:S(2)}) copy-start(bf16[1024,1024]{1,0:T(8,128)(2,1)} %out_ref.1) | copy-start | bytes 6291460
  12.2 16.9 %copy-start.3 = (bf16[54,704]{1,0:T(8,128)(2,1)S(1)}, bf16[54,704]{1,0:T(8,128)(2,1)}, u32[]{:S(2)}) copy-start(bf16[54,704]{1,0:T(8,128)(2,1)} %conv_ref.1) | copy-start | bytes 228100
  12.2 16.9 %copy-start.5 = (f32[704]{0:T(1024)S(1)}, f32[704]{0:T(1024)}, u32[]{:S(2)}) copy-start(f32[704]{0:T(1024)} %gain_ref.1) | copy-start | bytes 8452
  12.2 6.3 %collective-permute-start = (bf16[8,512]{1,0:T(8,128)(2,1)S(1)}, bf16[8,512]{1,0:T(8,128)(2,1)S(1)}, u32[]{:S(2)}, u32[]{:S(2)}) collective-permute-start(bf16[8,512]{1,0:T(8,128)(2,1)S(1)} %get-tuple-element.13), channel_id=1, source_target_pairs={{4,0},{8,4},{12,8},{16,12},{20,16},{24,20},{28,24},{32,28},{36,32}... | collective-permute-start | bytes 24584 | tf_op jit(solution)/shard_map/ppermute | solution.py:470
  20.9 16.0 %all-to-all-start.1 = ((bf16[16,8,512]{2,1,0:T(8,128)(2,1)}), bf16[16,8,512]{2,1,0:T(8,128)(2,1)S(1)}, u32[]{:S(2)}, u32[]{:S(2)}) async-start(bf16[16,8,512]{2,1,0:T(8,128)(2,1)} %bitcast.2), calls=%async_computation.1 | async-start | bytes 262144 | tf_op jit(solution)/shard_map/all_to_all | solution.py:499
  29.2 1.4 %copy-start.2 = (bf16[704,1024]{1,0:T(8,128)(2,1)S(1)}, bf16[704,1024]{1,0:T(8,128)(2,1)}, u32[]{:S(2)}) copy-start(bf16[704,1024]{1,0:T(8,128)(2,1)} %value_ref.1) | copy-start | bytes 4325380

commit v8 on v7

--- a/solution.py
+++ b/solution.py
@@ -403,7 +403,7 @@
         out_specs=vmem(1)[0] if single else tuple(vmem(len(outs))),
         scratch_shapes=list(scratch),
         cost_estimate=pl.CostEstimate(flops=cycles * 4096, bytes_accessed=1 << 20, transcendentals=0),
-        compiler_params=pltpu.CompilerParams(vmem_limit_bytes=room << 20),
+        compiler_params=pltpu.CompilerParams(vmem_limit_bytes=int(room * 1024) << 10),
         name=name,
     )
 
@@ -436,6 +436,7 @@
         shape((across, SUB, tile_rows * CELL)),
         [pltpu.VMEM((SUB * 16, LANES), F32)],
         count=1,
+        cycles=1000000,
     )(pixels.transpose(2, 0, 1))
     tiles = lax.all_to_all(copies, "gy", 0, 0, tiled=True)
     rows = kernel(
@@ -453,7 +454,7 @@
         ],
         others=6,
         cycles=6000,
-        room=60,
+        room=52.7,
     )(key_weight, conv_weight, input_gain, latents.reshape(down, across, share, width), latent_gain, query_weight)
     both = kernel(
         output_kernel, "value_output", shape((HEADS * SLOT, width)), count=4, cycles=6000, room=10

time: 38.5 us -> 38.3 us (level)
  Pallas kernels: 14.6 us -> 13 us
  waiting for transfers between devices: 4.72 us -> 6.29 us
    pallas_call x1, Pallas kernels: 4.61 us -> 3 us  [on_device(): kernel(query_kernel, 'query_rows', shape((HEADS * held + table_rows(feat)...]
    all_to_all x1, waiting for transfers between devices: 0.01 us -> 1.56 us  [on_device(): tiles = lax.all_to_all(copies, 'gy', 0, 0, tiled=True)]
  transfers between devices with their start and end apart: 3 -> 3, of which waited for: 1 -> 2; matrix products, arithmetic and copies ran while one was open for 2% -> 2% of each run, Pallas kernels for 27% -> 23%
where the time goes in v8:
time: 38.3 us; the launch traced here: 37.8 us
  starting transfers between devices  15.6 us (41%)
  Pallas kernels  13 us (34%)
  waiting for transfers between devices  6.29 us (16%)
  local copies, waits for them, and re-layouts  2.84 us (7%)
    all_to_all x1, starting transfers between devices, on_device(): lax.all_to_all(sent.reshape(down, share, -1), 'gx', 0, 0, tiled=True)  8.2 us
    all_to_all x1, starting transfers between devices, on_device(): tiles = lax.all_to_all(copies, 'gy', 0, 0, tiled=True)  6 us
    pallas_call x1, Pallas kernels, on_device(): kernel(functools.partial(inner_kernel, columns, size, feat), 'inner', [sh...  4.73 us
    all_to_all x1, waiting for transfers between devices, on_device(): lax.all_to_all(sent.reshape(down, share, -1), 'gx', 0, 0, tiled=True)  4.73 us
    pallas_call x1, Pallas kernels, on_device(): kernel(query_kernel, 'query_rows', shape((HEADS * held + table_rows(feat)...  3 us
    pallas_call x1, Pallas kernels, on_device(): kernel(functools.partial(border_kernel, columns, feat), 'border', shape((...  2.38 us
    unnamed x12, local copies, waits for them, and re-layouts  2.11 us
    all_to_all x1, waiting for transfers between devices, on_device(): tiles = lax.all_to_all(copies, 'gy', 0, 0, tiled=True)  1.56 us
  transfers between devices with their start and end apart: 3, of which 2 were waited for; matrix products, arithmetic and copies ran while one was open for 2% of the time, Pallas kernels for 23%

profile of v8, /device:TPU:32, one launch (start us, length us, event | category | flops | bytes accessed | tf_op | source)
XLA Modules:
  0.0 37.8 jit_solution(10677334592378971243)
XLA Ops:
  0.0 0.0 copy-start.5
  0.0 0.7 %copy-done.5 = bf16[14,56,6]{1,0,2:T(8,128)(2,1)S(1)} copy-done((bf16[14,56,6]{1,0,2:T(8,128)(2,1)S(1)}, bf16[14,56,6]{1,0,2:T(8,128)(2,1)}, u32[]{:S(2)}) %copy-start.5) | copy-done | bytes 9432
  0.7 0.0 copy-start.2
  0.7 0.7 %pack.1 = bf16[4,8,896]{2,1,0:T(8,128)(2,1)} custom-call(bf16[6,14,56]{2,1,0:T(8,128)(2,1)S(1)} %bitcast.3), custom_call_target="tpu_custom_call" | custom-call | flops 4096000000 | bytes 1048576 | tf_op jit(solution)/shard_map/pack/pallas_call | solution.py:433
  1.5 6.0 %all-to-all-start = ((bf16[4,8,896]{2,1,0:T(8,128)(2,1)}), bf16[4,8,896]{2,1,0:T(8,128)(2,1)S(1)}, u32[]{:S(2)}, u32[]{:S(2)}) async-start(bf16[4,8,896]{2,1,0:T(8,128)(2,1)} %pack.1), calls=%async_computation | async-start | bytes 114688 | tf_op jit(solution)/shard_map/all_to_all | solution.py:441
  7.5 0.0 copy-done.2
  7.5 0.0 copy-done.3
  7.5 0.0 copy-done.4
  7.5 3.0 %query_rows.1.rows_ref = bf16[1760,256]{1,0:T(8,128)(2,1)S(1)} custom-call(bf16[704,1024]{1,0:T(8,128)(2,1)} %key_hbm.1, bf16[54,704]{1,0:T(8,128)(2,1)S(1)} %copy-done.2, f32[704]{0:T(1024)S(1)} %copy-done.3, bf16[16,4,8,1024]{3,2,1,0:T(8,128)(2,1)} %bitcast.4, f32[1024]{0:T(1024)S(1)} %copy-done.4, bf16[1024,1024]{1,0:T(8,128)(2,1)} %query_hbm.1), custom_call_target="tpu_custom_call" | custom-call | flops 24576000 | bytes 1048576 | tf_op jit(solution)/shard_map/query_rows/pallas_call | solution.py:442
  10.5 1.6 %all-to-all-done.tiles_ref = bf16[4,8,896]{2,1,0:T(8,128)(2,1)S(1)} async-done(((bf16[4,8,896]{2,1,0:T(8,128)(2,1)}), bf16[4,8,896]{2,1,0:T(8,128)(2,1)S(1)}, u32[]{:S(2)}, u32[]{:S(2)}) %all-to-all-start) | async-done | bytes 57376 | tf_op jit(solution)/shard_map/all_to_all | solution.py:441
  12.0 0.1 join.1
  12.1 0.0 copy-start
  12.1 1.4 %collective-permute-start = (bf16[8,512]{1,0:T(8,128)(2,1)S(1)}, bf16[8,512]{1,0:T(8,128)(2,1)S(1)}, u32[]{:S(2)}, u32[]{:S(2)}) collective-permute-start(bf16[8,512]{1,0:T(8,128)(2,1)S(1)} %get-tuple-element.13), channel_id=1, source_target_pairs={{4,0},{8,4},{12,8},{16,12},{20,16},{24,20},{28,24},{32,28},{36,32}... | collective-permute-start | bytes 24584 | tf_op jit(solution)/shard_map/ppermute | solution.py:471
  13.6 4.7 %inner.1 = (f32[1024,128]{1,0:T(8,128)S(1)}, f32[1024,128]{1,0:T(8,128)S(1)}) custom-call(f32[8,3584]{1,0:T(8,128)S(1)} %get-tuple-element.12.strip_ref, bf16[1760,256]{1,0:T(8,128)(2,1)S(1)} %query_rows.1.rows_ref), custom_call_target="tpu_custom_call" | custom-call | flops 40960000 | bytes 1048576 | tf_op jit(solution)/shard_map/inner/pallas_call | solution.py:474
  18.3 0.0 collective-permute-done.after_ref
  18.3 2.4 %border.1 = bf16[128,512]{1,0:T(8,128)(2,1)} custom-call(f32[8,3584]{1,0:T(8,128)S(1)} %get-tuple-element.12.strip_ref, bf16[8,512]{1,0:T(8,128)(2,1)S(1)} %collective-permute-done.after_ref, bf16[1760,256]{1,0:T(8,128)(2,1)S(1)} %query_rows.1.rows_ref, f32[1024,128]{1,0:T(8,128)S(1)} %get-tuple-element.15.inner_sums_ref, ...), custom_call_target="tpu_custom_call" | custom-call | flops 12288000 | bytes 1048576 | tf_op jit(solution)/shard_map/border/pallas_call | solution.py:487
  20.7 8.2 %all-to-all-start.1 = ((bf16[16,8,512]{2,1,0:T(8,128)(2,1)}), bf16[16,8,512]{2,1,0:T(8,128)(2,1)S(1)}, u32[]{:S(2)}, u32[]{:S(2)}) async-start(bf16[16,8,512]{2,1,0:T(8,128)(2,1)} %bitcast.2), calls=%async_computation.1 | async-start | bytes 262144 | tf_op jit(solution)/shard_map/all_to_all | solution.py:500
  28.9 0.0 copy-done
  28.9 0.0 copy-start.1
  28.9 1.4 %copy-done.1 = bf16[704,1024]{1,0:T(8,128)(2,1)S(1)} copy-done((bf16[704,1024]{1,0:T(8,128)(2,1)S(1)}, bf16[704,1024]{1,0:T(8,128)(2,1)}, u32[]{:S(2)}) %copy-start.1) | copy-done | bytes 1441816
  30.3 1.0 %value_output.1.both_ref = bf16[512,1024]{1,0:T(8,128)(2,1)S(1)} custom-call(bf16[54,704]{1,0:T(8,128)(2,1)S(1)} %copy-done.2, f32[704]{0:T(1024)S(1)} %copy-done.3, bf16[704,1024]{1,0:T(8,128)(2,1)S(1)} %copy-done.1, bf16[1024,1024]{1,0:T(8,128)(2,1)S(1)} %copy-done), custom_call_target="tpu_custom_call" | custom-call | flops 24576000 | bytes 1048576 | tf_op jit(solution)/shard_map/value_output/pallas_call | solution.py:459
  31.3 0.7 %constant_dynamic-slice_fusion.own_ref = bf16[8,1024]{1,0:T(8,128)(2,1)S(1)} fusion(bf16[512,1024]{1,0:T(8,128)(2,1)} %param.14, s32[]{:T(128)S(6)} %select_n.3), kind=kLoop, calls=%fused_computation | loop fusion | bytes 32772 | tf_op jit(solution)/shard_map/dynamic_slice | solution.py:501
  32.0 4.7 %all-to-all-done.1.parts_ref = bf16[16,8,512]{2,1,0:T(8,128)(2,1)S(1)} async-done(((bf16[16,8,512]{2,1,0:T(8,128)(2,1)}), bf16[16,8,512]{2,1,0:T(8,128)(2,1)S(1)}, u32[]{:S(2)}, u32[]{:S(2)}) %all-to-all-start.1) | async-done | bytes 131104 | tf_op jit(solution)/shard_map/all_to_all | solution.py:500
  36.7 1.1 %combine.1 = bf16[8,1024]{1,0:T(8,128)(2,1)} custom-call(bf16[16,8,512]{2,1,0:T(8,128)(2,1)S(1)} %all-to-all-done.1.parts_ref, bf16[512,1024]{1,0:T(8,128)(2,1)S(1)} %value_output.1.both_ref, bf16[8,1024]{1,0:T(8,128)(2,1)S(1)} %constant_dynamic-slice_fusion.own_ref), custom_call_target="tpu_custom_call" | custom-call | flops 4096000 | bytes 1048576 | tf_op jit(solution)/shard_map/combine/pallas_call | solution.py:502
  (2 shorter events, 0.0 us)
Async XLA Ops:
  0.0 0.7 %copy-start.5 = (bf16[14,56,6]{1,0,2:T(8,128)(2,1)S(1)}, bf16[14,56,6]{1,0,2:T(8,128)(2,1)}, u32[]{:S(2)}) copy-start(bf16[14,56,6]{1,0,2:T(8,128)(2,1)} %param.9) | copy-start | bytes 28228
  0.7 6.7 %copy-start.2 = (bf16[54,704]{1,0:T(8,128)(2,1)S(1)}, bf16[54,704]{1,0:T(8,128)(2,1)}, u32[]{:S(2)}) copy-start(bf16[54,704]{1,0:T(8,128)(2,1)} %conv_ref.1) | copy-start | bytes 228100
  0.7 6.7 %copy-start.3 = (f32[704]{0:T(1024)S(1)}, f32[704]{0:T(1024)}, u32[]{:S(2)}) copy-start(f32[704]{0:T(1024)} %gain_ref.1) | copy-start | bytes 8452
  0.7 6.7 %copy-start.4 = (f32[1024]{0:T(1024)S(1)}, f32[1024]{0:T(1024)}, u32[]{:S(2)}) copy-start(f32[1024]{0:T(1024)} %lat_gain_hbm.1) | copy-start | bytes 12292
  1.5 10.6 %all-to-all-start = ((bf16[4,8,896]{2,1,0:T(8,128)(2,1)}), bf16[4,8,896]{2,1,0:T(8,128)(2,1)S(1)}, u32[]{:S(2)}, u32[]{:S(2)}) async-start(bf16[4,8,896]{2,1,0:T(8,128)(2,1)} %pack.1), calls=%async_computation | async-start | bytes 114688 | tf_op jit(solution)/shard_map/all_to_all | solution.py:441
  12.1 16.8 %copy-start = (bf16[1024,1024]{1,0:T(8,128)(2,1)S(1)}, bf16[1024,1024]{1,0:T(8,128)(2,1)}, u32[]{:S(2)}) copy-start(bf16[1024,1024]{1,0:T(8,128)(2,1)} %out_ref.1) | copy-start | bytes 6291460
  12.1 6.2 %collective-permute-start = (bf16[8,512]{1,0:T(8,128)(2,1)S(1)}, bf16[8,512]{1,0:T(8,128)(2,1)S(1)}, u32[]{:S(2)}, u32[]{:S(2)}) collective-permute-start(bf16[8,512]{1,0:T(8,128)(2,1)S(1)} %get-tuple-element.13), channel_id=1, source_target_pairs={{4,0},{8,4},{12,8},{16,12},{20,16},{24,20},{28,24},{32,28},{36,32}... | collective-permute-start | bytes 24584 | tf_op jit(solution)/shard_map/ppermute | solution.py:471
  20.7 16.0 %all-to-all-start.1 = ((bf16[16,8,512]{2,1,0:T(8,128)(2,1)}), bf16[16,8,512]{2,1,0:T(8,128)(2,1)S(1)}, u32[]{:S(2)}, u32[]{:S(2)}) async-start(bf16[16,8,512]{2,1,0:T(8,128)(2,1)} %bitcast.2), calls=%async_computation.1 | async-start | bytes 262144 | tf_op jit(solution)/shard_map/all_to_all | solution.py:500
  28.9 1.4 %copy-start.1 = (bf16[704,1024]{1,0:T(8,128)(2,1)S(1)}, bf16[704,1024]{1,0:T(8,128)(2,1)}, u32[]{:S(2)}) copy-start(bf16[704,1024]{1,0:T(8,128)(2,1)} %value_ref.1) | copy-start | bytes 4325380

commit v9 on v8

--- a/solution.py
+++ b/solution.py
@@ -207,8 +207,8 @@
     return lost
 
 
-def attend(blocks, rows_ref, pixel_ref, score_ref, expo_ref):
-    tops, sums = [], []
+def attend(blocks, rows_ref, pixel_ref, score_ref, expo_ref, take):
+    tops = []
     count = len(blocks)
     for turn in range(count + 2):
         if turn < count:
@@ -223,14 +223,12 @@
         if 0 <= turn - 2 < count:
             rows, cut = blocks[turn - 2]
             at = ((turn - 2) % 2, rows, slice(0, cut.stop - cut.start))
-            sums.append(nt(expo_ref[at], pixel_ref[:LANES, cut]))
-    return tops, sums
-
-
-def merged(tops, sums):
-    top = functools.reduce(jnp.maximum, tops)
-    total = sum(jnp.exp2(t - top) * s for t, s in zip(tops, sums))
-    return top, total
+            take(turn - 2, tops[turn - 2], nt(expo_ref[at], pixel_ref[:LANES, cut]))
+
+
+def merged(old_top, old_sums, top, sums):
+    new = jnp.maximum(old_top, top)
+    return new, jnp.exp2(old_top - new) * old_sums + jnp.exp2(top - new) * sums
 
 
 def inner_kernel(
@@ -257,12 +255,14 @@
 
         for turn in range(len(blocks)):
             fill(turn)
-        tops, sums = attend(halves, rows_ref, pixel_ref, score_ref, expo_ref)
-        tops = [jnp.concatenate(tops[i : i + 2], axis=0) for i in range(0, len(tops), 2)]
-        sums = [jnp.concatenate(sums[i : i + 2], axis=0) for i in range(0, len(sums), 2)]
-        top, total = merged(tops, sums)
-        sums_ref[...] = total
-        tops_ref[...] = jnp.broadcast_to(top, tops_ref.shape)
+        def take(turn, top, sums):
+            rows, cut = halves[turn]
+            if cut.start > 0:
+                top, sums = merged(tops_ref[rows], sums_ref[rows], top, sums)
+            sums_ref[rows] = sums
+            tops_ref[rows] = jnp.broadcast_to(top, sums.shape)
+
+        attend(halves, rows_ref, pixel_ref, score_ref, expo_ref, take)
         return [jnp.max(flag) for flag in flags if flag is not None]
 
     lost = functools.reduce(jnp.maximum, run(False))
@@ -318,26 +318,31 @@
         real = (lane % LINE < columns) & (jnp.where(lane // LINE == 1, below, 1) > 0)
         lost = fill_block(patches, real, explicit, feat, rows_ref, pixel_ref, 0)
         blocks = [(slice(at, at + half), slice(0, patches.shape[1])) for at in (0, half)]
-        tops, sums = attend(blocks, rows_ref, pixel_ref, score_ref, expo_ref)
-        tops, sums = jnp.concatenate(tops, axis=0), jnp.concatenate(sums, axis=0)
-        top, total = merged([inner_tops_ref[...], tops], [inner_sums_ref[...], sums])
-        high = total.astype(BF16)
-        low = (total - high.astype(F32)).astype(BF16)
-        high = jnp.where(iota(total.shape, 1) == ONE_TOO, low, high)
-
-        def side(values, odd):
-            heads = range(odd, HEADS, 2)
-            return jnp.concatenate([values[head * count : (head + 1) * count] for head in heads], axis=0)
-
-        placed = nn(jnp.concatenate([side(high, 0), side(high, 1)], axis=1), place)
-        lane = iota(placed.shape, 1)
-        column = lane % SLOT
-        one, two, three = thrice(jnp.where(lane < SLOT, side(top, 0), side(top, 1)))
-        placed = jnp.where(column == TOP, one.astype(F32), placed)
-        placed = jnp.where(column == TOP + 1, two.astype(F32), placed)
-        placed = jnp.where(column == TOP + 2, three.astype(F32), placed).astype(BF16)
-        for pair in range(HEADS // 2):
-            sent_ref[:, pair * LANES : (pair + 1) * LANES] = placed[pair * count : (pair + 1) * count]
+
+        def take(turn, top, sums):
+            rows = blocks[turn][0]
+            top, total = merged(inner_tops_ref[rows], inner_sums_ref[rows], top, sums)
+            high = total.astype(BF16)
+            low = (total - high.astype(F32)).astype(BF16)
+            high = jnp.where(iota(total.shape, 1) == ONE_TOO, low, high)
+
+            def side(values, odd):
+                heads = range(odd, half // count, 2)
+                return jnp.concatenate([values[head * count : (head + 1) * count] for head in heads], axis=0)
+
+            placed = nn(jnp.concatenate([side(high, 0), side(high, 1)], axis=1), place)
+            lane = iota(placed.shape, 1)
+            column = lane % SLOT
+            one, two, three = thrice(jnp.where(lane < SLOT, side(top, 0), side(top, 1)))
+            placed = jnp.where(column == TOP, one.astype(F32), placed)
+            placed = jnp.where(column == TOP + 1, two.astype(F32), placed)
+            placed = jnp.where(column == TOP + 2, three.astype(F32), placed).astype(BF16)
+            first = rows.start // count // 2
+            for pair in range(half // count // 2):
+                at = (first + pair) * LANES
+                sent_ref[:, at : at + LANES] = placed[pair * count : (pair + 1) * count]
+
+        attend(blocks, rows_ref, pixel_ref, score_ref, expo_ref, take)
         return lost
 
     def checked(starts):
@@ -470,7 +475,7 @@
     )(tiles)
     after = lax.ppermute(first, "gx", [(i + 1, i) for i in range(down - 1)])
     inner = (tile_rows - 2) * LINE
-    size = inner // 2
+    size = inner // 4
     sums, tops = kernel(
         functools.partial(inner_kernel, columns, size, feat),
         "inner",

time: 38.3 us -> 38.4 us (level)
  no operation moved by 1% of the time
where the time goes in v9:
time: 38.4 us; the launch traced here: 37.9 us
  starting transfers between devices  15.5 us (40%)
  Pallas kernels  13.2 us (34%)
  waiting for transfers between devices  6.29 us (16%)
  local copies, waits for them, and re-layouts  2.84 us (7%)
    all_to_all x1, starting transfers between devices, on_device(): lax.all_to_all(sent.reshape(down, share, -1), 'gx', 0, 0, tiled=True)  8.07 us
    all_to_all x1, starting transfers between devices, on_device(): tiles = lax.all_to_all(copies, 'gy', 0, 0, tiled=True)  6 us
    all_to_all x1, waiting for transfers between devices, on_device(): lax.all_to_all(sent.reshape(down, share, -1), 'gx', 0, 0, tiled=True)  4.73 us
    pallas_call x1, Pallas kernels, on_device(): kernel(functools.partial(inner_kernel, columns, size, feat), 'inner', [sh...  4.68 us
    pallas_call x1, Pallas kernels, on_device(): kernel(query_kernel, 'query_rows', shape((HEADS * held + table_rows(feat)...  3 us
    pallas_call x1, Pallas kernels, on_device(): kernel(functools.partial(border_kernel, columns, feat), 'border', shape((...  2.65 us
    unnamed x12, local copies, waits for them, and re-layouts  2.11 us
    all_to_all x1, waiting for transfers between devices, on_device(): tiles = lax.all_to_all(copies, 'gy', 0, 0, tiled=True)  1.56 us
  transfers between devices with their start and end apart: 3, of which 2 were waited for; matrix products, arithmetic and copies ran while one was open for 2% of the time, Pallas kernels for 23%

profile of v9, /device:TPU:32, one launch (start us, length us, event | category | flops | bytes accessed | tf_op | source)
XLA Modules:
  0.0 37.9 jit_solution(6894008904254087894)
XLA Ops:
  0.0 0.0 copy-start.5
  0.0 0.7 %copy-done.5 = bf16[14,56,6]{1,0,2:T(8,128)(2,1)S(1)} copy-done((bf16[14,56,6]{1,0,2:T(8,128)(2,1)S(1)}, bf16[14,56,6]{1,0,2:T(8,128)(2,1)}, u32[]{:S(2)}) %copy-start.5) | copy-done | bytes 9432
  0.7 0.0 copy-start.2
  0.7 0.7 %pack.1 = bf16[4,8,896]{2,1,0:T(8,128)(2,1)} custom-call(bf16[6,14,56]{2,1,0:T(8,128)(2,1)S(1)} %bitcast.3), custom_call_target="tpu_custom_call" | custom-call | flops 4096000000 | bytes 1048576 | tf_op jit(solution)/shard_map/pack/pallas_call | solution.py:438
  1.5 6.0 %all-to-all-start = ((bf16[4,8,896]{2,1,0:T(8,128)(2,1)}), bf16[4,8,896]{2,1,0:T(8,128)(2,1)S(1)}, u32[]{:S(2)}, u32[]{:S(2)}) async-start(bf16[4,8,896]{2,1,0:T(8,128)(2,1)} %pack.1), calls=%async_computation | async-start | bytes 114688 | tf_op jit(solution)/shard_map/all_to_all | solution.py:446
  7.5 0.0 copy-done.2
  7.5 0.0 copy-done.3
  7.5 0.0 copy-done.4
  7.5 3.0 %query_rows.1.rows_ref = bf16[1760,256]{1,0:T(8,128)(2,1)S(1)} custom-call(bf16[704,1024]{1,0:T(8,128)(2,1)} %key_hbm.1, bf16[54,704]{1,0:T(8,128)(2,1)S(1)} %copy-done.2, f32[704]{0:T(1024)S(1)} %copy-done.3, bf16[16,4,8,1024]{3,2,1,0:T(8,128)(2,1)} %bitcast.4, f32[1024]{0:T(1024)S(1)} %copy-done.4, bf16[1024,1024]{1,0:T(8,128)(2,1)} %query_hbm.1), custom_call_target="tpu_custom_call" | custom-call | flops 24576000 | bytes 1048576 | tf_op jit(solution)/shard_map/query_rows/pallas_call | solution.py:447
  10.5 1.6 %all-to-all-done.tiles_ref = bf16[4,8,896]{2,1,0:T(8,128)(2,1)S(1)} async-done(((bf16[4,8,896]{2,1,0:T(8,128)(2,1)}), bf16[4,8,896]{2,1,0:T(8,128)(2,1)S(1)}, u32[]{:S(2)}, u32[]{:S(2)}) %all-to-all-start) | async-done | bytes 57376 | tf_op jit(solution)/shard_map/all_to_all | solution.py:446
  12.0 0.1 join.1
  12.1 0.0 copy-start
  12.1 1.4 %collective-permute-start = (bf16[8,512]{1,0:T(8,128)(2,1)S(1)}, bf16[8,512]{1,0:T(8,128)(2,1)S(1)}, u32[]{:S(2)}, u32[]{:S(2)}) collective-permute-start(bf16[8,512]{1,0:T(8,128)(2,1)S(1)} %get-tuple-element.13), channel_id=1, source_target_pairs={{4,0},{8,4},{12,8},{16,12},{20,16},{24,20},{28,24},{32,28},{36,32}... | collective-permute-start | bytes 24584 | tf_op jit(solution)/shard_map/ppermute | solution.py:476
  13.6 4.7 %inner.1 = (f32[1024,128]{1,0:T(8,128)S(1)}, f32[1024,128]{1,0:T(8,128)S(1)}) custom-call(f32[8,3584]{1,0:T(8,128)S(1)} %get-tuple-element.12.strip_ref, bf16[1760,256]{1,0:T(8,128)(2,1)S(1)} %query_rows.1.rows_ref), custom_call_target="tpu_custom_call" | custom-call | flops 40960000 | bytes 1048576 | tf_op jit(solution)/shard_map/inner/pallas_call | solution.py:479
  18.3 0.0 collective-permute-done.after_ref
  18.3 2.6 %border.1 = bf16[128,512]{1,0:T(8,128)(2,1)} custom-call(f32[8,3584]{1,0:T(8,128)S(1)} %get-tuple-element.12.strip_ref, bf16[8,512]{1,0:T(8,128)(2,1)S(1)} %collective-permute-done.after_ref, bf16[1760,256]{1,0:T(8,128)(2,1)S(1)} %query_rows.1.rows_ref, f32[1024,128]{1,0:T(8,128)S(1)} %get-tuple-element.15.inner_sums_ref, ...), custom_call_target="tpu_custom_call" | custom-call | flops 12288000 | bytes 1048576 | tf_op jit(solution)/shard_map/border/pallas_call | solution.py:492
  20.9 8.1 %all-to-all-start.1 = ((bf16[16,8,512]{2,1,0:T(8,128)(2,1)}), bf16[16,8,512]{2,1,0:T(8,128)(2,1)S(1)}, u32[]{:S(2)}, u32[]{:S(2)}) async-start(bf16[16,8,512]{2,1,0:T(8,128)(2,1)} %bitcast.2), calls=%async_computation.1 | async-start | bytes 262144 | tf_op jit(solution)/shard_map/all_to_all | solution.py:505
  29.0 0.0 copy-done
  29.0 0.0 copy-start.1
  29.0 1.4 %copy-done.1 = bf16[704,1024]{1,0:T(8,128)(2,1)S(1)} copy-done((bf16[704,1024]{1,0:T(8,128)(2,1)S(1)}, bf16[704,1024]{1,0:T(8,128)(2,1)}, u32[]{:S(2)}) %copy-start.1) | copy-done | bytes 1441816
  30.4 1.0 %value_output.1.both_ref = bf16[512,1024]{1,0:T(8,128)(2,1)S(1)} custom-call(bf16[54,704]{1,0:T(8,128)(2,1)S(1)} %copy-done.2, f32[704]{0:T(1024)S(1)} %copy-done.3, bf16[704,1024]{1,0:T(8,128)(2,1)S(1)} %copy-done.1, bf16[1024,1024]{1,0:T(8,128)(2,1)S(1)} %copy-done), custom_call_target="tpu_custom_call" | custom-call | flops 24576000 | bytes 1048576 | tf_op jit(solution)/shard_map/value_output/pallas_call | solution.py:464
  31.4 0.7 %constant_dynamic-slice_fusion.own_ref = bf16[8,1024]{1,0:T(8,128)(2,1)S(1)} fusion(bf16[512,1024]{1,0:T(8,128)(2,1)} %param.14, s32[]{:T(128)S(6)} %select_n.3), kind=kLoop, calls=%fused_computation | loop fusion | bytes 32772 | tf_op jit(solution)/shard_map/dynamic_slice | solution.py:506
  32.1 4.7 %all-to-all-done.1.parts_ref = bf16[16,8,512]{2,1,0:T(8,128)(2,1)S(1)} async-done(((bf16[16,8,512]{2,1,0:T(8,128)(2,1)}), bf16[16,8,512]{2,1,0:T(8,128)(2,1)S(1)}, u32[]{:S(2)}, u32[]{:S(2)}) %all-to-all-start.1) | async-done | bytes 131104 | tf_op jit(solution)/shard_map/all_to_all | solution.py:505
  36.8 1.1 %combine.1 = bf16[8,1024]{1,0:T(8,128)(2,1)} custom-call(bf16[16,8,512]{2,1,0:T(8,128)(2,1)S(1)} %all-to-all-done.1.parts_ref, bf16[512,1024]{1,0:T(8,128)(2,1)S(1)} %value_output.1.both_ref, bf16[8,1024]{1,0:T(8,128)(2,1)S(1)} %constant_dynamic-slice_fusion.own_ref), custom_call_target="tpu_custom_call" | custom-call | flops 4096000 | bytes 1048576 | tf_op jit(solution)/shard_map/combine/pallas_call | solution.py:507
  (2 shorter events, 0.0 us)
Async XLA Ops:
  0.0 0.7 %copy-start.5 = (bf16[14,56,6]{1,0,2:T(8,128)(2,1)S(1)}, bf16[14,56,6]{1,0,2:T(8,128)(2,1)}, u32[]{:S(2)}) copy-start(bf16[14,56,6]{1,0,2:T(8,128)(2,1)} %param.9) | copy-start | bytes 28228
  0.7 6.7 %copy-start.2 = (bf16[54,704]{1,0:T(8,128)(2,1)S(1)}, bf16[54,704]{1,0:T(8,128)(2,1)}, u32[]{:S(2)}) copy-start(bf16[54,704]{1,0:T(8,128)(2,1)} %conv_ref.1) | copy-start | bytes 228100
  0.7 6.7 %copy-start.3 = (f32[704]{0:T(1024)S(1)}, f32[704]{0:T(1024)}, u32[]{:S(2)}) copy-start(f32[704]{0:T(1024)} %gain_ref.1) | copy-start | bytes 8452
  0.7 6.7 %copy-start.4 = (f32[1024]{0:T(1024)S(1)}, f32[1024]{0:T(1024)}, u32[]{:S(2)}) copy-start(f32[1024]{0:T(1024)} %lat_gain_hbm.1) | copy-start | bytes 12292
  1.5 10.6 %all-to-all-start = ((bf16[4,8,896]{2,1,0:T(8,128)(2,1)}), bf16[4,8,896]{2,1,0:T(8,128)(2,1)S(1)}, u32[]{:S(2)}, u32[]{:S(2)}) async-start(bf16[4,8,896]{2,1,0:T(8,128)(2,1)} %pack.1), calls=%async_computation | async-start | bytes 114688 | tf_op jit(solution)/shard_map/all_to_all | solution.py:446
  12.1 16.9 %copy-start = (bf16[1024,1024]{1,0:T(8,128)(2,1)S(1)}, bf16[1024,1024]{1,0:T(8,128)(2,1)}, u32[]{:S(2)}) copy-start(bf16[1024,1024]{1,0:T(8,128)(2,1)} %out_ref.1) | copy-start | bytes 6291460
  12.1 6.1 %collective-permute-start = (bf16[8,512]{1,0:T(8,128)(2,1)S(1)}, bf16[8,512]{1,0:T(8,128)(2,1)S(1)}, u32[]{:S(2)}, u32[]{:S(2)}) collective-permute-start(bf16[8,512]{1,0:T(8,128)(2,1)S(1)} %get-tuple-element.13), channel_id=1, source_target_pairs={{4,0},{8,4},{12,8},{16,12},{20,16},{24,20},{28,24},{32,28},{36,32}... | collective-permute-start | bytes 24584 | tf_op jit(solution)/shard_map/ppermute | solution.py:476
  20.9 15.9 %all-to-all-start.1 = ((bf16[16,8,512]{2,1,0:T(8,128)(2,1)}), bf16[16,8,512]{2,1,0:T(8,128)(2,1)S(1)}, u32[]{:S(2)}, u32[]{:S(2)}) async-start(bf16[16,8,512]{2,1,0:T(8,128)(2,1)} %bitcast.2), calls=%async_computation.1 | async-start | bytes 262144 | tf_op jit(solution)/shard_map/all_to_all | solution.py:505
  29.0 1.4 %copy-start.1 = (bf16[704,1024]{1,0:T(8,128)(2,1)S(1)}, bf16[704,1024]{1,0:T(8,128)(2,1)}, u32[]{:S(2)}) copy-start(bf16[704,1024]{1,0:T(8,128)(2,1)} %value_ref.1) | copy-start | bytes 4325380

commit v10 on v8

--- a/solution.py
+++ b/solution.py
@@ -207,8 +207,8 @@
     return lost
 
 
-def attend(blocks, rows_ref, pixel_ref, score_ref, expo_ref):
-    tops, sums = [], []
+def attend(blocks, rows_ref, pixel_ref, score_ref, expo_ref, take):
+    tops = []
     count = len(blocks)
     for turn in range(count + 2):
         if turn < count:
@@ -223,14 +223,12 @@
         if 0 <= turn - 2 < count:
             rows, cut = blocks[turn - 2]
             at = ((turn - 2) % 2, rows, slice(0, cut.stop - cut.start))
-            sums.append(nt(expo_ref[at], pixel_ref[:LANES, cut]))
-    return tops, sums
-
-
-def merged(tops, sums):
-    top = functools.reduce(jnp.maximum, tops)
-    total = sum(jnp.exp2(t - top) * s for t, s in zip(tops, sums))
-    return top, total
+            take(turn - 2, tops[turn - 2], nt(expo_ref[at], pixel_ref[:LANES, cut]))
+
+
+def merged(old_top, old_sums, top, sums):
+    new = jnp.maximum(old_top, top)
+    return new, jnp.exp2(old_top - new) * old_sums + jnp.exp2(top - new) * sums
 
 
 def inner_kernel(
@@ -257,12 +255,14 @@
 
         for turn in range(len(blocks)):
             fill(turn)
-        tops, sums = attend(halves, rows_ref, pixel_ref, score_ref, expo_ref)
-        tops = [jnp.concatenate(tops[i : i + 2], axis=0) for i in range(0, len(tops), 2)]
-        sums = [jnp.concatenate(sums[i : i + 2], axis=0) for i in range(0, len(sums), 2)]
-        top, total = merged(tops, sums)
-        sums_ref[...] = total
-        tops_ref[...] = jnp.broadcast_to(top, tops_ref.shape)
+        def take(turn, top, sums):
+            rows, cut = halves[turn]
+            if cut.start > 0:
+                top, sums = merged(tops_ref[rows], sums_ref[rows], top, sums)
+            sums_ref[rows] = sums
+            tops_ref[rows] = jnp.broadcast_to(top, sums.shape)
+
+        attend(halves, rows_ref, pixel_ref, score_ref, expo_ref, take)
         return [jnp.max(flag) for flag in flags if flag is not None]
 
     lost = functools.reduce(jnp.maximum, run(False))
@@ -318,9 +318,10 @@
         real = (lane % LINE < columns) & (jnp.where(lane // LINE == 1, below, 1) > 0)
         lost = fill_block(patches, real, explicit, feat, rows_ref, pixel_ref, 0)
         blocks = [(slice(at, at + half), slice(0, patches.shape[1])) for at in (0, half)]
-        tops, sums = attend(blocks, rows_ref, pixel_ref, score_ref, expo_ref)
-        tops, sums = jnp.concatenate(tops, axis=0), jnp.concatenate(sums, axis=0)
-        top, total = merged([inner_tops_ref[...], tops], [inner_sums_ref[...], sums])
+        results = []
+        attend(blocks, rows_ref, pixel_ref, score_ref, expo_ref, lambda turn, *result: results.append(result))
+        tops, sums = (jnp.concatenate(parts, axis=0) for parts in zip(*results))
+        top, total = merged(inner_tops_ref[...], inner_sums_ref[...], tops, sums)
         high = total.astype(BF16)
         low = (total - high.astype(F32)).astype(BF16)
         high = jnp.where(iota(total.shape, 1) == ONE_TOO, low, high)
@@ -470,7 +471,7 @@
     )(tiles)
     after = lax.ppermute(first, "gx", [(i + 1, i) for i in range(down - 1)])
     inner = (tile_rows - 2) * LINE
-    size = inner // 2
+    size = inner // 4
     sums, tops = kernel(
         functools.partial(inner_kernel, columns, size, feat),
         "inner",

time: 38.3 us -> 38.3 us (level)
  no operation moved by 1% of the time
where the time goes in v10:
time: 38.3 us; the launch traced here: 37.8 us
  starting transfers between devices  15.7 us (41%)
  Pallas kernels  12.9 us (34%)
  waiting for transfers between devices  6.29 us (16%)
  local copies, waits for them, and re-layouts  2.84 us (7%)
    all_to_all x1, starting transfers between devices, on_device(): lax.all_to_all(sent.reshape(down, share, -1), 'gx', 0, 0, tiled=True)  8.25 us
    all_to_all x1, starting transfers between devices, on_device(): tiles = lax.all_to_all(copies, 'gy', 0, 0, tiled=True)  6 us
    all_to_all x1, waiting for transfers between devices, on_device(): lax.all_to_all(sent.reshape(down, share, -1), 'gx', 0, 0, tiled=True)  4.73 us
    pallas_call x1, Pallas kernels, on_device(): kernel(functools.partial(inner_kernel, columns, size, feat), 'inner', [sh...  4.68 us
    pallas_call x1, Pallas kernels, on_device(): kernel(query_kernel, 'query_rows', shape((HEADS * held + table_rows(feat)...  3 us
    pallas_call x1, Pallas kernels, on_device(): kernel(functools.partial(border_kernel, columns, feat), 'border', shape((...  2.38 us
    unnamed x12, local copies, waits for them, and re-layouts  2.11 us
    all_to_all x1, waiting for transfers between devices, on_device(): tiles = lax.all_to_all(copies, 'gy', 0, 0, tiled=True)  1.56 us
  transfers between devices with their start and end apart: 3, of which 2 were waited for; matrix products, arithmetic and copies ran while one was open for 2% of the time, Pallas kernels for 23%

profile of v10, /device:TPU:32, one launch (start us, length us, event | category | flops | bytes accessed | tf_op | source)
XLA Modules:
  0.0 37.8 jit_solution(12307484553562683140)
XLA Ops:
  0.0 0.0 copy-start.5
  0.0 0.7 %copy-done.5 = bf16[14,56,6]{1,0,2:T(8,128)(2,1)S(1)} copy-done((bf16[14,56,6]{1,0,2:T(8,128)(2,1)S(1)}, bf16[14,56,6]{1,0,2:T(8,128)(2,1)}, u32[]{:S(2)}) %copy-start.5) | copy-done | bytes 9432
  0.7 0.0 copy-start.2
  0.7 0.7 %pack.1 = bf16[4,8,896]{2,1,0:T(8,128)(2,1)} custom-call(bf16[6,14,56]{2,1,0:T(8,128)(2,1)S(1)} %bitcast.3), custom_call_target="tpu_custom_call" | custom-call | flops 4096000000 | bytes 1048576 | tf_op jit(solution)/shard_map/pack/pallas_call | solution.py:434
  1.5 6.0 %all-to-all-start = ((bf16[4,8,896]{2,1,0:T(8,128)(2,1)}), bf16[4,8,896]{2,1,0:T(8,128)(2,1)S(1)}, u32[]{:S(2)}, u32[]{:S(2)}) async-start(bf16[4,8,896]{2,1,0:T(8,128)(2,1)} %pack.1), calls=%async_computation | async-start | bytes 114688 | tf_op jit(solution)/shard_map/all_to_all | solution.py:442
  7.5 0.0 copy-done.2
  7.5 0.0 copy-done.3
  7.5 0.0 copy-done.4
  7.5 3.0 %query_rows.1.rows_ref = bf16[1760,256]{1,0:T(8,128)(2,1)S(1)} custom-call(bf16[704,1024]{1,0:T(8,128)(2,1)} %key_hbm.1, bf16[54,704]{1,0:T(8,128)(2,1)S(1)} %copy-done.2, f32[704]{0:T(1024)S(1)} %copy-done.3, bf16[16,4,8,1024]{3,2,1,0:T(8,128)(2,1)} %bitcast.4, f32[1024]{0:T(1024)S(1)} %copy-done.4, bf16[1024,1024]{1,0:T(8,128)(2,1)} %query_hbm.1), custom_call_target="tpu_custom_call" | custom-call | flops 24576000 | bytes 1048576 | tf_op jit(solution)/shard_map/query_rows/pallas_call | solution.py:443
  10.5 1.6 %all-to-all-done.tiles_ref = bf16[4,8,896]{2,1,0:T(8,128)(2,1)S(1)} async-done(((bf16[4,8,896]{2,1,0:T(8,128)(2,1)}), bf16[4,8,896]{2,1,0:T(8,128)(2,1)S(1)}, u32[]{:S(2)}, u32[]{:S(2)}) %all-to-all-start) | async-done | bytes 57376 | tf_op jit(solution)/shard_map/all_to_all | solution.py:442
  12.0 0.1 join.1
  12.1 0.0 copy-start
  12.1 1.4 %collective-permute-start = (bf16[8,512]{1,0:T(8,128)(2,1)S(1)}, bf16[8,512]{1,0:T(8,128)(2,1)S(1)}, u32[]{:S(2)}, u32[]{:S(2)}) collective-permute-start(bf16[8,512]{1,0:T(8,128)(2,1)S(1)} %get-tuple-element.13), channel_id=1, source_target_pairs={{4,0},{8,4},{12,8},{16,12},{20,16},{24,20},{28,24},{32,28},{36,32}... | collective-permute-start | bytes 24584 | tf_op jit(solution)/shard_map/ppermute | solution.py:472
  13.6 4.7 %inner.1 = (f32[1024,128]{1,0:T(8,128)S(1)}, f32[1024,128]{1,0:T(8,128)S(1)}) custom-call(f32[8,3584]{1,0:T(8,128)S(1)} %get-tuple-element.12.strip_ref, bf16[1760,256]{1,0:T(8,128)(2,1)S(1)} %query_rows.1.rows_ref), custom_call_target="tpu_custom_call" | custom-call | flops 40960000 | bytes 1048576 | tf_op jit(solution)/shard_map/inner/pallas_call | solution.py:475
  18.3 0.0 collective-permute-done.after_ref
  18.3 2.4 %border.1 = bf16[128,512]{1,0:T(8,128)(2,1)} custom-call(f32[8,3584]{1,0:T(8,128)S(1)} %get-tuple-element.12.strip_ref, bf16[8,512]{1,0:T(8,128)(2,1)S(1)} %collective-permute-done.after_ref, bf16[1760,256]{1,0:T(8,128)(2,1)S(1)} %query_rows.1.rows_ref, f32[1024,128]{1,0:T(8,128)S(1)} %get-tuple-element.15.inner_sums_ref, ...), custom_call_target="tpu_custom_call" | custom-call | flops 12288000 | bytes 1048576 | tf_op jit(solution)/shard_map/border/pallas_call | solution.py:488
  20.7 8.2 %all-to-all-start.1 = ((bf16[16,8,512]{2,1,0:T(8,128)(2,1)}), bf16[16,8,512]{2,1,0:T(8,128)(2,1)S(1)}, u32[]{:S(2)}, u32[]{:S(2)}) async-start(bf16[16,8,512]{2,1,0:T(8,128)(2,1)} %bitcast.2), calls=%async_computation.1 | async-start | bytes 262144 | tf_op jit(solution)/shard_map/all_to_all | solution.py:501
  28.9 0.0 copy-done
  28.9 0.0 copy-start.1
  28.9 1.4 %copy-done.1 = bf16[704,1024]{1,0:T(8,128)(2,1)S(1)} copy-done((bf16[704,1024]{1,0:T(8,128)(2,1)S(1)}, bf16[704,1024]{1,0:T(8,128)(2,1)}, u32[]{:S(2)}) %copy-start.1) | copy-done | bytes 1441816
  30.3 1.0 %value_output.1.both_ref = bf16[512,1024]{1,0:T(8,128)(2,1)S(1)} custom-call(bf16[54,704]{1,0:T(8,128)(2,1)S(1)} %copy-done.2, f32[704]{0:T(1024)S(1)} %copy-done.3, bf16[704,1024]{1,0:T(8,128)(2,1)S(1)} %copy-done.1, bf16[1024,1024]{1,0:T(8,128)(2,1)S(1)} %copy-done), custom_call_target="tpu_custom_call" | custom-call | flops 24576000 | bytes 1048576 | tf_op jit(solution)/shard_map/value_output/pallas_call | solution.py:460
  31.3 0.7 %constant_dynamic-slice_fusion.own_ref = bf16[8,1024]{1,0:T(8,128)(2,1)S(1)} fusion(bf16[512,1024]{1,0:T(8,128)(2,1)} %param.14, s32[]{:T(128)S(6)} %select_n.3), kind=kLoop, calls=%fused_computation | loop fusion | bytes 32772 | tf_op jit(solution)/shard_map/dynamic_slice | solution.py:502
  32.0 4.7 %all-to-all-done.1.parts_ref = bf16[16,8,512]{2,1,0:T(8,128)(2,1)S(1)} async-done(((bf16[16,8,512]{2,1,0:T(8,128)(2,1)}), bf16[16,8,512]{2,1,0:T(8,128)(2,1)S(1)}, u32[]{:S(2)}, u32[]{:S(2)}) %all-to-all-start.1) | async-done | bytes 131104 | tf_op jit(solution)/shard_map/all_to_all | solution.py:501
  36.7 1.1 %combine.1 = bf16[8,1024]{1,0:T(8,128)(2,1)} custom-call(bf16[16,8,512]{2,1,0:T(8,128)(2,1)S(1)} %all-to-all-done.1.parts_ref, bf16[512,1024]{1,0:T(8,128)(2,1)S(1)} %value_output.1.both_ref, bf16[8,1024]{1,0:T(8,128)(2,1)S(1)} %constant_dynamic-slice_fusion.own_ref), custom_call_target="tpu_custom_call" | custom-call | flops 4096000 | bytes 1048576 | tf_op jit(solution)/shard_map/combine/pallas_call | solution.py:503
  (2 shorter events, 0.0 us)
Async XLA Ops:
  0.0 0.7 %copy-start.5 = (bf16[14,56,6]{1,0,2:T(8,128)(2,1)S(1)}, bf16[14,56,6]{1,0,2:T(8,128)(2,1)}, u32[]{:S(2)}) copy-start(bf16[14,56,6]{1,0,2:T(8,128)(2,1)} %param.9) | copy-start | bytes 28228
  0.7 6.7 %copy-start.2 = (bf16[54,704]{1,0:T(8,128)(2,1)S(1)}, bf16[54,704]{1,0:T(8,128)(2,1)}, u32[]{:S(2)}) copy-start(bf16[54,704]{1,0:T(8,128)(2,1)} %conv_ref.1) | copy-start | bytes 228100
  0.7 6.7 %copy-start.3 = (f32[704]{0:T(1024)S(1)}, f32[704]{0:T(1024)}, u32[]{:S(2)}) copy-start(f32[704]{0:T(1024)} %gain_ref.1) | copy-start | bytes 8452
  0.7 6.7 %copy-start.4 = (f32[1024]{0:T(1024)S(1)}, f32[1024]{0:T(1024)}, u32[]{:S(2)}) copy-start(f32[1024]{0:T(1024)} %lat_gain_hbm.1) | copy-start | bytes 12292
  1.5 10.6 %all-to-all-start = ((bf16[4,8,896]{2,1,0:T(8,128)(2,1)}), bf16[4,8,896]{2,1,0:T(8,128)(2,1)S(1)}, u32[]{:S(2)}, u32[]{:S(2)}) async-start(bf16[4,8,896]{2,1,0:T(8,128)(2,1)} %pack.1), calls=%async_computation | async-start | bytes 114688 | tf_op jit(solution)/shard_map/all_to_all | solution.py:442
  12.1 16.8 %copy-start = (bf16[1024,1024]{1,0:T(8,128)(2,1)S(1)}, bf16[1024,1024]{1,0:T(8,128)(2,1)}, u32[]{:S(2)}) copy-start(bf16[1024,1024]{1,0:T(8,128)(2,1)} %out_ref.1) | copy-start | bytes 6291460
  12.1 6.1 %collective-permute-start = (bf16[8,512]{1,0:T(8,128)(2,1)S(1)}, bf16[8,512]{1,0:T(8,128)(2,1)S(1)}, u32[]{:S(2)}, u32[]{:S(2)}) collective-permute-start(bf16[8,512]{1,0:T(8,128)(2,1)S(1)} %get-tuple-element.13), channel_id=1, source_target_pairs={{4,0},{8,4},{12,8},{16,12},{20,16},{24,20},{28,24},{32,28},{36,32}... | collective-permute-start | bytes 24584 | tf_op jit(solution)/shard_map/ppermute | solution.py:472
  20.7 16.1 %all-to-all-start.1 = ((bf16[16,8,512]{2,1,0:T(8,128)(2,1)}), bf16[16,8,512]{2,1,0:T(8,128)(2,1)S(1)}, u32[]{:S(2)}, u32[]{:S(2)}) async-start(bf16[16,8,512]{2,1,0:T(8,128)(2,1)} %bitcast.2), calls=%async_computation.1 | async-start | bytes 262144 | tf_op jit(solution)/shard_map/all_to_all | solution.py:501
  28.9 1.4 %copy-start.1 = (bf16[704,1024]{1,0:T(8,128)(2,1)S(1)}, bf16[704,1024]{1,0:T(8,128)(2,1)}, u32[]{:S(2)}) copy-start(bf16[704,1024]{1,0:T(8,128)(2,1)} %value_ref.1) | copy-start | bytes 4325380

commit v11 on v10

--- a/solution.py
+++ b/solution.py
@@ -188,7 +188,7 @@
         diag = jnp.where(iota(gram.shape, 0) == iota(gram.shape, 1), gram.astype(F32), 0.0)
         diag = jnp.sum(diag, axis=-1, keepdims=True)
         scale = jnp.sum(patches * patches * diag, axis=0, keepdims=True)
-        lost = jnp.where((variance + EPS) * 128.0 < scale, 1.0, 0.0)
+        lost = jnp.where(scale >= 0.0, 1.0, 0.0)
     return patches * lax.rsqrt(variance + EPS), lost
 
 

time: 38.3 us -> 46 us (1.20)
  Pallas kernels: 12.9 us -> 21.4 us
  starting transfers between devices: 15.7 us -> 14.9 us
    pallas_call x1, Pallas kernels: 4.68 us -> 11 us  [on_device(): kernel(functools.partial(inner_kernel, columns, size, feat), 'inner', [sh...]
    pallas_call x1, Pallas kernels: 2.38 us -> 4.54 us  [on_device(): kernel(functools.partial(border_kernel, columns, feat), 'border', shape((...]
    all_to_all x1, starting transfers between devices: 8.25 us -> 7.49 us  [on_device(): lax.all_to_all(sent.reshape(down, share, -1), 'gx', 0, 0, tiled=True)]
  transfers between devices with their start and end apart: 3 -> 3, of which waited for: 2 -> 2; matrix products, arithmetic and copies ran while one was open for 2% -> 2% of each run, Pallas kernels for 23% -> 33%
where the time goes in v11:
time: 46 us; the launch traced here: 45.6 us
  Pallas kernels  21.4 us (47%)
  starting transfers between devices  14.9 us (32%)
  waiting for transfers between devices  6.29 us (14%)
  local copies, waits for them, and re-layouts  2.84 us (6%)
    pallas_call x1, Pallas kernels, on_device(): kernel(functools.partial(inner_kernel, columns, size, feat), 'inner', [sh...  11 us
    all_to_all x1, starting transfers between devices, on_device(): lax.all_to_all(sent.reshape(down, share, -1), 'gx', 0, 0, tiled=True)  7.49 us
    all_to_all x1, starting transfers between devices, on_device(): tiles = lax.all_to_all(copies, 'gy', 0, 0, tiled=True)  6 us
    all_to_all x1, waiting for transfers between devices, on_device(): lax.all_to_all(sent.reshape(down, share, -1), 'gx', 0, 0, tiled=True)  4.73 us
    pallas_call x1, Pallas kernels, on_device(): kernel(functools.partial(border_kernel, columns, feat), 'border', shape((...  4.54 us
    pallas_call x1, Pallas kernels, on_device(): kernel(query_kernel, 'query_rows', shape((HEADS * held + table_rows(feat)...  3 us
    unnamed x12, local copies, waits for them, and re-layouts  2.11 us
    all_to_all x1, waiting for transfers between devices, on_device(): tiles = lax.all_to_all(copies, 'gy', 0, 0, tiled=True)  1.56 us
  transfers between devices with their start and end apart: 3, of which 2 were waited for; matrix products, arithmetic and copies ran while one was open for 2% of the time, Pallas kernels for 33%

profile of v11, /device:TPU:32, one launch (start us, length us, event | category | flops | bytes accessed | tf_op | source)
XLA Modules:
  0.0 45.6 jit_solution(7154406610643610164)
XLA Ops:
  0.0 0.0 copy-start.5
  0.0 0.7 %copy-done.5 = bf16[14,56,6]{1,0,2:T(8,128)(2,1)S(1)} copy-done((bf16[14,56,6]{1,0,2:T(8,128)(2,1)S(1)}, bf16[14,56,6]{1,0,2:T(8,128)(2,1)}, u32[]{:S(2)}) %copy-start.5) | copy-done | bytes 9432
  0.7 0.0 copy-start.2
  0.7 0.7 %pack.1 = bf16[4,8,896]{2,1,0:T(8,128)(2,1)} custom-call(bf16[6,14,56]{2,1,0:T(8,128)(2,1)S(1)} %bitcast.3), custom_call_target="tpu_custom_call" | custom-call | flops 4096000000 | bytes 1048576 | tf_op jit(solution)/shard_map/pack/pallas_call | solution.py:434
  1.5 6.0 %all-to-all-start = ((bf16[4,8,896]{2,1,0:T(8,128)(2,1)}), bf16[4,8,896]{2,1,0:T(8,128)(2,1)S(1)}, u32[]{:S(2)}, u32[]{:S(2)}) async-start(bf16[4,8,896]{2,1,0:T(8,128)(2,1)} %pack.1), calls=%async_computation | async-start | bytes 114688 | tf_op jit(solution)/shard_map/all_to_all | solution.py:442
  7.5 0.0 copy-done.2
  7.5 0.0 copy-done.3
  7.5 0.0 copy-done.4
  7.5 3.0 %query_rows.1.rows_ref = bf16[1760,256]{1,0:T(8,128)(2,1)S(1)} custom-call(bf16[704,1024]{1,0:T(8,128)(2,1)} %key_hbm.1, bf16[54,704]{1,0:T(8,128)(2,1)S(1)} %copy-done.2, f32[704]{0:T(1024)S(1)} %copy-done.3, bf16[16,4,8,1024]{3,2,1,0:T(8,128)(2,1)} %bitcast.4, f32[1024]{0:T(1024)S(1)} %copy-done.4, bf16[1024,1024]{1,0:T(8,128)(2,1)} %query_hbm.1), custom_call_target="tpu_custom_call" | custom-call | flops 24576000 | bytes 1048576 | tf_op jit(solution)/shard_map/query_rows/pallas_call | solution.py:443
  10.5 1.6 %all-to-all-done.tiles_ref = bf16[4,8,896]{2,1,0:T(8,128)(2,1)S(1)} async-done(((bf16[4,8,896]{2,1,0:T(8,128)(2,1)}), bf16[4,8,896]{2,1,0:T(8,128)(2,1)S(1)}, u32[]{:S(2)}, u32[]{:S(2)}) %all-to-all-start) | async-done | bytes 57376 | tf_op jit(solution)/shard_map/all_to_all | solution.py:442
  12.0 0.1 join.1
  12.1 0.0 copy-start
  12.1 1.4 %collective-permute-start = (bf16[8,512]{1,0:T(8,128)(2,1)S(1)}, bf16[8,512]{1,0:T(8,128)(2,1)S(1)}, u32[]{:S(2)}, u32[]{:S(2)}) collective-permute-start(bf16[8,512]{1,0:T(8,128)(2,1)S(1)} %get-tuple-element.13), channel_id=1, source_target_pairs={{4,0},{8,4},{12,8},{16,12},{20,16},{24,20},{28,24},{32,28},{36,32}... | collective-permute-start | bytes 24584 | tf_op jit(solution)/shard_map/ppermute | solution.py:472
  13.6 11.0 %inner.1 = (f32[1024,128]{1,0:T(8,128)S(1)}, f32[1024,128]{1,0:T(8,128)S(1)}) custom-call(f32[8,3584]{1,0:T(8,128)S(1)} %get-tuple-element.12.strip_ref, bf16[1760,256]{1,0:T(8,128)(2,1)S(1)} %query_rows.1.rows_ref), custom_call_target="tpu_custom_call" | custom-call | flops 40960000 | bytes 1048576 | tf_op jit(solution)/shard_map/inner/pallas_call | solution.py:475
  24.6 0.0 collective-permute-done.after_ref
  24.6 4.5 %border.1 = bf16[128,512]{1,0:T(8,128)(2,1)} custom-call(f32[8,3584]{1,0:T(8,128)S(1)} %get-tuple-element.12.strip_ref, bf16[8,512]{1,0:T(8,128)(2,1)S(1)} %collective-permute-done.after_ref, bf16[1760,256]{1,0:T(8,128)(2,1)S(1)} %query_rows.1.rows_ref, f32[1024,128]{1,0:T(8,128)S(1)} %get-tuple-element.15.inner_sums_ref, ...), custom_call_target="tpu_custom_call" | custom-call | flops 12288000 | bytes 1048576 | tf_op jit(solution)/shard_map/border/pallas_call | solution.py:488
  29.2 7.5 %all-to-all-start.1 = ((bf16[16,8,512]{2,1,0:T(8,128)(2,1)}), bf16[16,8,512]{2,1,0:T(8,128)(2,1)S(1)}, u32[]{:S(2)}, u32[]{:S(2)}) async-start(bf16[16,8,512]{2,1,0:T(8,128)(2,1)} %bitcast.2), calls=%async_computation.1 | async-start | bytes 262144 | tf_op jit(solution)/shard_map/all_to_all | solution.py:501
  36.7 0.0 copy-done
  36.7 0.0 copy-start.1
  36.7 1.4 %copy-done.1 = bf16[704,1024]{1,0:T(8,128)(2,1)S(1)} copy-done((bf16[704,1024]{1,0:T(8,128)(2,1)S(1)}, bf16[704,1024]{1,0:T(8,128)(2,1)}, u32[]{:S(2)}) %copy-start.1) | copy-done | bytes 1441816
  38.0 1.0 %value_output.1.both_ref = bf16[512,1024]{1,0:T(8,128)(2,1)S(1)} custom-call(bf16[54,704]{1,0:T(8,128)(2,1)S(1)} %copy-done.2, f32[704]{0:T(1024)S(1)} %copy-done.3, bf16[704,1024]{1,0:T(8,128)(2,1)S(1)} %copy-done.1, bf16[1024,1024]{1,0:T(8,128)(2,1)S(1)} %copy-done), custom_call_target="tpu_custom_call" | custom-call | flops 24576000 | bytes 1048576 | tf_op jit(solution)/shard_map/value_output/pallas_call | solution.py:460
  39.0 0.7 %constant_dynamic-slice_fusion.own_ref = bf16[8,1024]{1,0:T(8,128)(2,1)S(1)} fusion(bf16[512,1024]{1,0:T(8,128)(2,1)} %param.14, s32[]{:T(128)S(6)} %select_n.3), kind=kLoop, calls=%fused_computation | loop fusion | bytes 32772 | tf_op jit(solution)/shard_map/dynamic_slice | solution.py:502
  39.8 4.7 %all-to-all-done.1.parts_ref = bf16[16,8,512]{2,1,0:T(8,128)(2,1)S(1)} async-done(((bf16[16,8,512]{2,1,0:T(8,128)(2,1)}), bf16[16,8,512]{2,1,0:T(8,128)(2,1)S(1)}, u32[]{:S(2)}, u32[]{:S(2)}) %all-to-all-start.1) | async-done | bytes 131104 | tf_op jit(solution)/shard_map/all_to_all | solution.py:501
  44.5 1.1 %combine.1 = bf16[8,1024]{1,0:T(8,128)(2,1)} custom-call(bf16[16,8,512]{2,1,0:T(8,128)(2,1)S(1)} %all-to-all-done.1.parts_ref, bf16[512,1024]{1,0:T(8,128)(2,1)S(1)} %value_output.1.both_ref, bf16[8,1024]{1,0:T(8,128)(2,1)S(1)} %constant_dynamic-slice_fusion.own_ref), custom_call_target="tpu_custom_call" | custom-call | flops 4096000 | bytes 1048576 | tf_op jit(solution)/shard_map/combine/pallas_call | solution.py:503
  (2 shorter events, 0.0 us)
Async XLA Ops:
  0.0 0.7 %copy-start.5 = (bf16[14,56,6]{1,0,2:T(8,128)(2,1)S(1)}, bf16[14,56,6]{1,0,2:T(8,128)(2,1)}, u32[]{:S(2)}) copy-start(bf16[14,56,6]{1,0,2:T(8,128)(2,1)} %param.9) | copy-start | bytes 28228
  0.7 6.7 %copy-start.2 = (bf16[54,704]{1,0:T(8,128)(2,1)S(1)}, bf16[54,704]{1,0:T(8,128)(2,1)}, u32[]{:S(2)}) copy-start(bf16[54,704]{1,0:T(8,128)(2,1)} %conv_ref.1) | copy-start | bytes 228100
  0.7 6.7 %copy-start.3 = (f32[704]{0:T(1024)S(1)}, f32[704]{0:T(1024)}, u32[]{:S(2)}) copy-start(f32[704]{0:T(1024)} %gain_ref.1) | copy-start | bytes 8452
  0.7 6.7 %copy-start.4 = (f32[1024]{0:T(1024)S(1)}, f32[1024]{0:T(1024)}, u32[]{:S(2)}) copy-start(f32[1024]{0:T(1024)} %lat_gain_hbm.1) | copy-start | bytes 12292
  1.5 10.6 %all-to-all-start = ((bf16[4,8,896]{2,1,0:T(8,128)(2,1)}), bf16[4,8,896]{2,1,0:T(8,128)(2,1)S(1)}, u32[]{:S(2)}, u32[]{:S(2)}) async-start(bf16[4,8,896]{2,1,0:T(8,128)(2,1)} %pack.1), calls=%async_computation | async-start | bytes 114688 | tf_op jit(solution)/shard_map/all_to_all | solution.py:442
  12.1 24.5 %copy-start = (bf16[1024,1024]{1,0:T(8,128)(2,1)S(1)}, bf16[1024,1024]{1,0:T(8,128)(2,1)}, u32[]{:S(2)}) copy-start(bf16[1024,1024]{1,0:T(8,128)(2,1)} %out_ref.1) | copy-start | bytes 6291460
  12.1 12.5 %collective-permute-start = (bf16[8,512]{1,0:T(8,128)(2,1)S(1)}, bf16[8,512]{1,0:T(8,128)(2,1)S(1)}, u32[]{:S(2)}, u32[]{:S(2)}) collective-permute-start(bf16[8,512]{1,0:T(8,128)(2,1)S(1)} %get-tuple-element.13), channel_id=1, source_target_pairs={{4,0},{8,4},{12,8},{16,12},{20,16},{24,20},{28,24},{32,28},{36,32}... | collective-permute-start | bytes 24584 | tf_op jit(solution)/shard_map/ppermute | solution.py:472
  29.2 15.3 %all-to-all-start.1 = ((bf16[16,8,512]{2,1,0:T(8,128)(2,1)}), bf16[16,8,512]{2,1,0:T(8,128)(2,1)S(1)}, u32[]{:S(2)}, u32[]{:S(2)}) async-start(bf16[16,8,512]{2,1,0:T(8,128)(2,1)} %bitcast.2), calls=%async_computation.1 | async-start | bytes 262144 | tf_op jit(solution)/shard_map/all_to_all | solution.py:501
  36.7 1.4 %copy-start.1 = (bf16[704,1024]{1,0:T(8,128)(2,1)S(1)}, bf16[704,1024]{1,0:T(8,128)(2,1)}, u32[]{:S(2)}) copy-start(bf16[704,1024]{1,0:T(8,128)(2,1)} %value_ref.1) | copy-start | bytes 4325380
